TPU v7x, 32 devices: a whole 2x2x4 slice. The times are simulated.
32 devices in a mesh: comp: 2 (over core), tile: 16 (over z, y, x).
Axes of the slice: x: 2, y: 2, z: 4, core: 2. Of those that a mesh axis runs over, the one named last changes fastest.
Arguments:
- state: bfloat16 [2, 256, 4, 60, 128], P('comp', 'tile'), may hold values from -6 to 6
- dyn_weights: bfloat16 [2, 64, 128, 128], P('comp'), may hold values from -0.1875 to 0.1875
- vertical: float32 [2, 60, 60], P('comp'), may hold values from -0.75 to 0.75
- remap_weights: bfloat16 [2, 64, 128, 128], replicated, may hold values from -0.5 to 0.5
- neighbor_slots: int32 [2, 256, 4], P('comp', 'tile'), may hold values from 0 to 39
- neighbor_tiles: int32 [2, 256, 4], P('comp', 'tile'), may hold values from 0 to 63
- remap_source: int32 [2, 256], P('comp', 'tile'), may hold values from 0 to 15
- remap_target: int32 [2, 256], P('comp', 'tile'), may hold values from 0 to 15
- remap_tile: int32 [2, 256], P('comp', 'tile'), may hold values from 0 to 63
- remap_dest: int32 [2, 256, 1], P('comp', 'tile'), may hold values from 0 to 15, as said below
Outputs:
- new_state: bfloat16 [2, 256, 4, 60, 128], P('comp', 'tile')
Inputs may be any that keep to these rules, and one draw needn't show every extreme that they name: `remap_dest`: among the 16 entries of one device, each destination device is named at most 2 times.
All inputs are finite; a program needn't handle non-finite values.
Results may differ from a plain program's by a relative error of at most 0.0046.
Values may be sent and summed in bfloat16 or wider, within the bound.
No kernel may reach another device: no remote copies, remote signals or barrier semaphores. Data moves between devices by JAX's collectives and lax.ppermute only.
A program may use at most 64 MiB of HBM per device.

v0:
```python
import jax
import jax.numpy as jnp
from jax import lax
from jax.sharding import PartitionSpec as P

SURF = 8
HALO = 8
FOLD = 8
STEPS = 2
CAP = 2


def partner(value, axis, distance):
    mask = 2**distance
    pairs = [(source, source ^ mask) for source in range(lax.axis_size(axis))]
    return lax.ppermute(value, axis, pairs)


def padded_2(array, sides, width):
    for axis, dim in sides:
        peers, length = (lax.axis_size(axis), array.shape[dim])
        up = [(i, (i + 1) % peers) for i in range(peers)]
        down = [(j, i) for i, j in up]
        last = lax.slice_in_dim(array, length - width, length, axis=dim)
        leading = lax.slice_in_dim(array, 0, width, axis=dim)
        before = lax.ppermute(last, axis, up)
        after = lax.ppermute(leading, axis, down)
        array = jnp.concatenate([before, array, after], axis=dim)
    return array


def route_partials(payload, targets):
    moved = (
        partner(payload.astype(jnp.bfloat16), "comp", 0).astype(payload.dtype),
        partner(targets, "comp", 0),
    )
    return (
        lax.all_to_all(
            moved[0].astype(jnp.bfloat16), "tile", split_axis=0, concat_axis=0, tiled=True
        ).astype(jnp.float32),
        lax.all_to_all(moved[1], "tile", split_axis=0, concat_axis=0, tiled=True),
    )


def on_device(
    state,
    dyn_weights,
    vertical,
    remap_weights,
    neighbor_slots,
    neighbor_tiles,
    remap_source,
    remap_target,
    remap_tile,
    remap_dest,
):
    count = state.shape[1]
    fields = state.shape[2]
    levels = state.shape[3]
    width = state.shape[4]
    tile_count = lax.axis_size("tile")
    fold_bit = tile_count.bit_length() - 2
    comp = lax.axis_index("comp")
    operator_blocks = state[0].reshape(count, fields * levels, width)
    exchange_weights = dyn_weights[0]
    vertical_matrix = vertical[0]
    block_positions = neighbor_slots[0]
    which = neighbor_tiles[0]
    for step in range(STEPS):
        padded = padded_2(operator_blocks, (("tile", 0),), HALO)
        across = partner(operator_blocks[:FOLD], "tile", fold_bit)
        source_pool = jnp.concatenate([padded, across], axis=0)
        flux = jnp.zeros(operator_blocks.shape, jnp.float32)
        for k in range(block_positions.shape[1]):
            flux = flux + jnp.einsum(
                "brc,bcd->brd",
                source_pool[block_positions[:, k]],
                exchange_weights[which[:, k]],
                preferred_element_type=jnp.float32,
            )
        middle_state = (operator_blocks.astype(jnp.float32) + flux).reshape(
            count, fields, levels, width
        )
        mixed_state = jnp.einsum(
            "se,ivey->ivsy", vertical_matrix, middle_state, precision=lax.Precision.HIGHEST
        )
        operator_blocks = (
            (middle_state + jnp.tanh(mixed_state))
            .reshape(count, fields * levels, width)
            .astype(jnp.bfloat16)
        )
    shaped = operator_blocks.reshape(count, fields, levels, width)
    surface = shaped[:, :, :SURF, :].reshape(count, fields * SURF, width)
    entries = remap_source.shape[1]
    picked = surface[remap_source[0]]
    dest = remap_dest[0, :, 0]
    hits = (dest[:, None] == jnp.arange(tile_count, dtype=jnp.int32)[None, :]).astype(jnp.int32)
    rank = jnp.sum((jnp.cumsum(hits, axis=0) - 1) * hits, axis=1)
    slot_of = dest * CAP + rank
    place = jnp.arange(tile_count * CAP, dtype=jnp.int32)[:, None] == slot_of[None, :]
    target_buf = jnp.max(jnp.where(place, remap_target[0][None, :], -1), axis=1)
    outward = lax.dynamic_index_in_dim(remap_weights, 1 - comp, 0, keepdims=False)[remap_tile[0]]
    partial_value = jnp.einsum(
        "erc,ecd->erd", picked, outward, preferred_element_type=jnp.float32
    ).reshape(entries, -1)
    payload = jnp.dot(place.astype(jnp.float32), partial_value, precision=lax.Precision.HIGHEST)
    received, targets_in = route_partials(payload, target_buf)
    landing = (jnp.arange(count, dtype=jnp.int32)[:, None] == targets_in[None, :]).astype(
        jnp.float32
    )
    coupled = jnp.dot(landing, received, precision=lax.Precision.HIGHEST).reshape(
        count, fields, SURF, width
    )
    top = (shaped[:, :, :SURF, :].astype(jnp.float32) + coupled).astype(jnp.bfloat16)
    final = jnp.concatenate([top, shaped[:, :, SURF:, :]], axis=2)
    return final[None]


def solution(mesh):
    return jax.shard_map(
        on_device,
        mesh=mesh,
        in_specs=(
            P("comp", "tile", None, None, None),
            P("comp", None, None, None),
            P("comp", None, None),
            P(),
            P("comp", "tile", None),
            P("comp", "tile", None),
            P("comp", "tile"),
            P("comp", "tile"),
            P("comp", "tile"),
            P("comp", "tile", None),
        ),
        out_specs=P("comp", "tile", None, None, None),
        check_vma=False,
    )
```

profile of v0, /device:TPU:0, one launch (start us, length us, event | category | flops | bytes accessed | tf_op | source)
XLA Modules:
  0.0 170.9 jit_solution(2998300657039782721)
XLA Ops:
  0.0 1.6 copy.92
  2.7 4.1 %collective-permute-start.2 = (bf16[8,240,128]{2,1,0:T(8,128)(2,1)}, bf16[8,240,128]{2,1,0:T(8,128)(2,1)}, u32[]{:S(2)}, u32[]{:S(2)}) collective-permute-start(bf16[8,240,128]{2,1,0:T(8,128)(2,1)} %copy.97), channel_id=1, source_target_pairs={{0,8},{1,9},{2,10},{3,11},{4,12},{5,13},{6,14},{7,15},{8,0},{9,1},... | collective-permute-start | bytes 1474568 | tf_op jit(solution)/shard_map/ppermute | solution.py:16
  6.7 3.2 %collective-permute-start.1 = (bf16[8,240,128]{2,1,0:T(8,128)(2,1)}, bf16[8,240,128]{2,1,0:T(8,128)(2,1)}, u32[]{:S(2)}, u32[]{:S(2)}) collective-permute-start(bf16[8,240,128]{2,1,0:T(8,128)(2,1)} %copy.97), channel_id=1, source_target_pairs={{1,0},{2,1},{3,2},{4,3},{5,4},{6,5},{7,6},{8,7},{9,8},{10,9},{11,1... | collective-permute-start | bytes 1474568 | tf_op jit(solution)/shard_map/ppermute | solution.py:27
  17.0 14.9 %collective-permute-done = bf16[8,240,128]{2,1,0:T(8,128)(2,1)} collective-permute-done((bf16[8,240,128]{2,1,0:T(8,128)(2,1)}, bf16[8,240,128]{2,1,0:T(8,128)(2,1)}, u32[]{:S(2)}, u32[]{:S(2)}) %collective-permute-start) | collective-permute-done | bytes 491552 | tf_op jit(solution)/shard_map/ppermute | solution.py:26
  31.9 1.8 %constant_dynamic-update-slice_fusion.2 = bf16[40,240,128]{2,1,0:T(8,128)(2,1)} fusion(bf16[8,240,128]{2,1,0:T(8,128)(2,1)} %collective-permute-done), kind=kLoop, calls=%fused_computation.42 | loop fusion | bytes 983040
  35.0 1.9 %constant_dynamic-update-slice_fusion.1 = bf16[40,240,128]{2,1,0:T(8,128)(2,1)} fusion(bf16[40,240,128]{2,1,0:T(8,128)(2,1)} %copy_dynamic-update-slice_fusion.1, bf16[8,240,128]{2,1,0:T(8,128)(2,1)} %collective-permute-done.1), kind=kLoop, calls=%fused_computation.41 | loop fusion | bytes 983040
  36.8 1.8 %constant_dynamic-update-slice_fusion = bf16[40,240,128]{2,1,0:T(8,128)(2,1)} fusion(bf16[40,240,128]{2,1,0:T(8,128)(2,1)} %constant_dynamic-update-slice_fusion.1, bf16[8,240,128]{2,1,0:T(8,128)(2,1)} %collective-permute-done.2), kind=kLoop, calls=%fused_computation.40 | loop fusion | bytes 983040 | tf_op jit(solution)/shard_map/concatenate | solution.py:72
  38.7 3.3 %gather_fusion.6 = bf16[16,240,128]{2,1,0:T(8,128)(2,1)} fusion(bf16[40,240,128]{2,1,0:T(8,128)(2,1)} %constant_dynamic-update-slice_fusion, s32[1024]{0:T(1024)S(1)} %get-tuple-element.17), kind=kCustom, calls=%fused_computation.6 | custom fusion | bytes 1966144 | tf_op jit(solution)/shard_map/gather | solution.py:77
  42.0 3.3 %gather_fusion.4 = bf16[16,240,128]{2,1,0:T(8,128)(2,1)} fusion(bf16[40,240,128]{2,1,0:T(8,128)(2,1)} %constant_dynamic-update-slice_fusion, s32[1024]{0:T(1024)S(1)} %get-tuple-element.18), kind=kCustom, calls=%fused_computation.4 | custom fusion | bytes 1966144 | tf_op jit(solution)/shard_map/gather | solution.py:77
  45.3 3.3 %gather_fusion.2 = bf16[16,240,128]{2,1,0:T(8,128)(2,1)} fusion(bf16[40,240,128]{2,1,0:T(8,128)(2,1)} %constant_dynamic-update-slice_fusion, s32[1024]{0:T(1024)S(1)} %get-tuple-element.19), kind=kCustom, calls=%fused_computation.2 | custom fusion | bytes 1966144 | tf_op jit(solution)/shard_map/gather | solution.py:77
  48.6 3.3 %gather_fusion = bf16[16,240,128]{2,1,0:T(8,128)(2,1)} fusion(bf16[40,240,128]{2,1,0:T(8,128)(2,1)} %constant_dynamic-update-slice_fusion, s32[1024]{0:T(1024)S(1)} %get-tuple-element.20), kind=kCustom, calls=%fused_computation | custom fusion | bytes 1966144 | tf_op jit(solution)/shard_map/gather | solution.py:77
  52.0 2.1 %fusion.38 = f32[16,240,128]{2,1,0:T(8,128)S(1)} fusion(bf16[16,240,128]{2,1,0:T(8,128)(2,1)} %gather_fusion.4, bf16[16,128,128]{2,1,0:T(8,128)(2,1)} %gather_fusion.5), kind=kOutput, calls=%fused_computation.90 | convolution fusion | flops 125829120 | bytes 3473408 | tf_op jit(solution)/shard_map/brc,bcd->brd/dot_general | solution.py:75
  58.3 3.8 %fusion.1 = bf16[16,4,60,128]{3,2,1,0:T(8,128)(2,1)S(1)} fusion(f32[16,4,60,128]{3,0,2,1:T(8,128)S(1)} %bitcast.102, f32[1,60,60]{2,0,1:T(1,128)S(1)} %copy-done.18), kind=kOutput, calls=%fused_computation.18 | convolution fusion | flops 354877440 | bytes 2963520 | tf_op jit(solution)/shard_map/se,ivey->ivsy/dot_general | solution.py:84
  63.4 1.8 %collective-permute-start.3 = (bf16[8,240,128]{2,1,0:T(8,128)(2,1)}, bf16[8,240,128]{2,1,0:T(8,128)(2,1)}, u32[]{:S(2)}, u32[]{:S(2)}) collective-permute-start(bf16[8,240,128]{2,1,0:T(8,128)(2,1)} %copy.106), channel_id=1, source_target_pairs={{0,1},{1,2},{2,3},{3,4},{4,5},{5,6},{6,7},{7,8},{8,9},{9,10},{10,1... | collective-permute-start | bytes 1474568 | tf_op jit(solution)/shard_map/ppermute | solution.py:26
  67.8 3.9 %collective-permute-start.4 = (bf16[8,240,128]{2,1,0:T(8,128)(2,1)}, bf16[8,240,128]{2,1,0:T(8,128)(2,1)}, u32[]{:S(2)}, u32[]{:S(2)}) collective-permute-start(bf16[8,240,128]{2,1,0:T(8,128)(2,1)} %copy.108), channel_id=1, source_target_pairs={{1,0},{2,1},{3,2},{4,3},{5,4},{6,5},{7,6},{8,7},{9,8},{10,9},{11,1... | collective-permute-start | bytes 1474568 | tf_op jit(solution)/shard_map/ppermute | solution.py:27
  71.6 3.0 %gather_fusion.13 = bf16[16,128,128]{2,1,0:T(8,128)(2,1)} fusion(bf16[64,128,128]{2,1,0:T(8,128)(2,1)} %dynamic-slice_bitcast_fusion, s32[1024]{0:T(1024)S(1)} %get-tuple-element.21), kind=kCustom, calls=%fused_computation.13 | custom fusion | bytes 1048640 | tf_op jit(solution)/shard_map/gather | solution.py:102
  75.3 10.3 %collective-permute-start.5 = (bf16[8,240,128]{2,1,0:T(8,128)(2,1)}, bf16[8,240,128]{2,1,0:T(8,128)(2,1)S(1)}, u32[]{:S(2)}, u32[]{:S(2)}) collective-permute-start(bf16[8,240,128]{2,1,0:T(8,128)(2,1)} %copy.108), channel_id=1, source_target_pairs={{0,8},{1,9},{2,10},{3,11},{4,12},{5,13},{6,14},{7,15},{8,0},{9,1},... | collective-permute-start | bytes 1474568 | tf_op jit(solution)/shard_map/ppermute | solution.py:16
  86.6 1.8 %constant_dynamic-update-slice_fusion.5 = bf16[40,240,128]{2,1,0:T(8,128)(2,1)} fusion(bf16[8,240,128]{2,1,0:T(8,128)(2,1)} %collective-permute-done.3), kind=kLoop, calls=%fused_computation.45 | loop fusion | bytes 983040
  89.7 1.9 %constant_dynamic-update-slice_fusion.4 = bf16[40,240,128]{2,1,0:T(8,128)(2,1)} fusion(bf16[40,240,128]{2,1,0:T(8,128)(2,1)} %copy_dynamic-update-slice_fusion, bf16[8,240,128]{2,1,0:T(8,128)(2,1)} %collective-permute-done.4), kind=kLoop, calls=%fused_computation.44 | loop fusion | bytes 983040
  91.6 22.4 %collective-permute-done.5 = bf16[8,240,128]{2,1,0:T(8,128)(2,1)S(1)} collective-permute-done((bf16[8,240,128]{2,1,0:T(8,128)(2,1)}, bf16[8,240,128]{2,1,0:T(8,128)(2,1)S(1)}, u32[]{:S(2)}, u32[]{:S(2)}) %collective-permute-start.5) | collective-permute-done | bytes 491552 | tf_op jit(solution)/shard_map/ppermute | solution.py:16
  114.8 3.3 %gather_fusion.11 = bf16[16,240,128]{2,1,0:T(8,128)(2,1)} fusion(bf16[40,240,128]{2,1,0:T(8,128)(2,1)} %constant_dynamic-update-slice_fusion.3, s32[1024]{0:T(1024)S(1)} %get-tuple-element.17), kind=kCustom, calls=%fused_computation.11 | custom fusion | bytes 1966144 | tf_op jit(solution)/shard_map/gather | solution.py:77
  118.2 3.3 %gather_fusion.10 = bf16[16,240,128]{2,1,0:T(8,128)(2,1)} fusion(bf16[40,240,128]{2,1,0:T(8,128)(2,1)} %constant_dynamic-update-slice_fusion.3, s32[1024]{0:T(1024)S(1)} %get-tuple-element.18), kind=kCustom, calls=%fused_computation.10 | custom fusion | bytes 1966144 | tf_op jit(solution)/shard_map/gather | solution.py:77
  121.5 3.4 %gather_fusion.9 = bf16[16,240,128]{2,1,0:T(8,128)(2,1)} fusion(bf16[40,240,128]{2,1,0:T(8,128)(2,1)} %constant_dynamic-update-slice_fusion.3, s32[1024]{0:T(1024)S(1)} %get-tuple-element.19), kind=kCustom, calls=%fused_computation.9 | custom fusion | bytes 1966144 | tf_op jit(solution)/shard_map/gather | solution.py:77
  124.9 3.3 %gather_fusion.8 = bf16[16,240,128]{2,1,0:T(8,128)(2,1)} fusion(bf16[40,240,128]{2,1,0:T(8,128)(2,1)} %constant_dynamic-update-slice_fusion.3, s32[1024]{0:T(1024)S(1)} %get-tuple-element.20), kind=kCustom, calls=%fused_computation.8 | custom fusion | bytes 1966144 | tf_op jit(solution)/shard_map/gather | solution.py:77
  128.2 2.0 %fusion.41 = f32[16,240,128]{2,1,0:T(8,128)S(1)} fusion(bf16[16,240,128]{2,1,0:T(8,128)(2,1)} %gather_fusion.10, bf16[16,128,128]{2,1,0:T(8,128)(2,1)S(1)} %copy-done.7), kind=kOutput, calls=%fused_computation.93 | convolution fusion | flops 125829120 | bytes 3473408 | tf_op jit(solution)/shard_map/brc,bcd->brd/dot_general | solution.py:75
  134.6 3.8 %fusion = bf16[16,4,60,128]{3,2,1,0:T(8,128)(2,1)S(1)} fusion(f32[16,4,60,128]{3,0,2,1:T(8,128)S(1)} %bitcast.103, f32[1,60,60]{2,0,1:T(1,128)S(1)} %copy-done.18), kind=kOutput, calls=%fused_computation.16 | convolution fusion | flops 354877440 | bytes 2963520 | tf_op jit(solution)/shard_map/se,ivey->ivsy/dot_general | solution.py:84
  143.3 3.5 %all-to-all-start = ((s32[16,2,1]{1,2,0:T(1,128)}), s32[16,2,1]{1,2,0:T(1,128)S(1)}, u32[]{:S(2)}, u32[]{:S(2)}) async-start(s32[16,2,1]{1,2,0:T(1,128)} %bitcast.24), calls=%async_computation | async-start | bytes 16384 | tf_op jit(solution)/shard_map/all_to_all | solution.py:41
  146.8 1.8 %all_to_all.16 = bf16[16,2,4096]{2,1,0:T(2,128)(2,1)} reshape(bf16[32,4096]{1,0:T(8,128)(2,1)} %collective-permute-done.7) | data formatting | bytes 524288 | tf_op jit(solution)/shard_map/all_to_all | solution.py:38
  148.6 5.4 %all-to-all-done = s32[16,2,1]{1,2,0:T(1,128)S(1)} async-done(((s32[16,2,1]{1,2,0:T(1,128)}), s32[16,2,1]{1,2,0:T(1,128)S(1)}, u32[]{:S(2)}, u32[]{:S(2)}) %all-to-all-start) | async-done | bytes 160 | tf_op jit(solution)/shard_map/all_to_all | solution.py:41
  154.0 3.5 %all-to-all-start.1 = ((bf16[16,2,4096]{2,1,0:T(2,128)(2,1)}), bf16[16,2,4096]{2,1,0:T(2,128)(2,1)S(1)}, u32[]{:S(2)}, u32[]{:S(2)}) async-start(bf16[16,2,4096]{2,1,0:T(2,128)(2,1)} %all_to_all.16), calls=%async_computation.1 | async-start | bytes 524288 | tf_op jit(solution)/shard_map/all_to_all | solution.py:38
  159.8 7.0 %all-to-all-done.1 = bf16[16,2,4096]{2,1,0:T(2,128)(2,1)S(1)} async-done(((bf16[16,2,4096]{2,1,0:T(2,128)(2,1)}), bf16[16,2,4096]{2,1,0:T(2,128)(2,1)S(1)}, u32[]{:S(2)}, u32[]{:S(2)}) %all-to-all-start.1) | async-done | bytes 262176 | tf_op jit(solution)/shard_map/all_to_all | solution.py:38
  169.1 1.8 %copy.117 = bf16[1,16,4,60,128]{4,2,3,1,0:T(4,128)(2,1)} copy(bf16[1,16,4,60,128]{4,3,2,1,0:T(8,128)(2,1)S(1)} %maximum_bitcast_fusion) | data formatting | bytes 1966080 | tf_op jit(solution)/shard_map/broadcast_in_dim | solution.py:116
  (112 shorter events, 34.7 us)
Async XLA Ops:
  0.0 11.0 %copy-start = (bf16[1,64,128,128]{3,2,1,0:T(8,128)(2,1)S(1)}, bf16[1,64,128,128]{3,2,1,0:T(8,128)(2,1)}, u32[]{:S(2)}) copy-start(bf16[1,64,128,128]{3,2,1,0:T(8,128)(2,1)} %param.11) | copy-start | bytes 6291460
  1.6 9.2 %copy-start.22 = (s32[1,16]{1,0:T(1,128)S(1)}, s32[1,16]{1,0:T(1,128)}, u32[]{:S(2)}) copy-start(s32[1,16]{1,0:T(1,128)} %param.16) | copy-start | bytes 196
  1.6 9.2 %copy-start.20 = (s32[1,16,4]{1,2,0:T(4,128)S(1)}, s32[1,16,4]{1,2,0:T(4,128)}, u32[]{:S(2)}) copy-start(s32[1,16,4]{1,2,0:T(4,128)} %param.14) | copy-start | bytes 772
  1.6 9.2 %copy-start.21 = (s32[1,16,4]{1,2,0:T(4,128)S(1)}, s32[1,16,4]{1,2,0:T(4,128)}, u32[]{:S(2)}) copy-start(s32[1,16,4]{1,2,0:T(4,128)} %param.15) | copy-start | bytes 772
  1.6 9.2 %copy-start.19 = (s32[1,16,1]{1,2,0:T(1,128)S(1)}, s32[1,16,1]{1,2,0:T(1,128)}, u32[]{:S(2)}) copy-start(s32[1,16,1]{1,2,0:T(1,128)} %param.19) | copy-start | bytes 196
  2.7 34.1 %collective-permute-start.2 = (bf16[8,240,128]{2,1,0:T(8,128)(2,1)}, bf16[8,240,128]{2,1,0:T(8,128)(2,1)}, u32[]{:S(2)}, u32[]{:S(2)}) collective-permute-start(bf16[8,240,128]{2,1,0:T(8,128)(2,1)} %copy.97), channel_id=1, source_target_pairs={{0,8},{1,9},{2,10},{3,11},{4,12},{5,13},{6,14},{7,15},{8,0},{9,1},... | collective-permute-start | bytes 1474568 | tf_op jit(solution)/shard_map/ppermute | solution.py:16
  6.7 28.2 %collective-permute-start.1 = (bf16[8,240,128]{2,1,0:T(8,128)(2,1)}, bf16[8,240,128]{2,1,0:T(8,128)(2,1)}, u32[]{:S(2)}, u32[]{:S(2)}) collective-permute-start(bf16[8,240,128]{2,1,0:T(8,128)(2,1)} %copy.97), channel_id=1, source_target_pairs={{1,0},{2,1},{3,2},{4,3},{5,4},{6,5},{7,6},{8,7},{9,8},{10,9},{11,1... | collective-permute-start | bytes 1474568 | tf_op jit(solution)/shard_map/ppermute | solution.py:27
  10.8 21.0 %collective-permute-start = (bf16[8,240,128]{2,1,0:T(8,128)(2,1)}, bf16[8,240,128]{2,1,0:T(8,128)(2,1)}, u32[]{:S(2)}, u32[]{:S(2)}) collective-permute-start(bf16[8,240,128]{2,1,0:T(8,128)(2,1)} %copy.95), channel_id=1, source_target_pairs={{0,1},{1,2},{2,3},{3,4},{4,5},{5,6},{6,7},{7,8},{8,9},{9,10},{10,1... | collective-permute-start | bytes 1474568 | tf_op jit(solution)/shard_map/ppermute | solution.py:26
  11.1 5.9 %copy-start.23 = (s32[1,16]{1,0:T(1,128)S(1)}, s32[1,16]{1,0:T(1,128)}, u32[]{:S(2)}) copy-start(s32[1,16]{1,0:T(1,128)} %param.18) | copy-start | bytes 196
  52.0 2.1 %copy-start.8 = (bf16[16,128,128]{2,1,0:T(8,128)(2,1)S(1)}, bf16[16,128,128]{2,1,0:T(8,128)(2,1)}, u32[]{:S(2)}) copy-start(bf16[16,128,128]{2,1,0:T(8,128)(2,1)} %gather_fusion.1) | copy-start | bytes 1572868
  52.0 2.1 %copy-start.15 = (bf16[16,240,128]{2,1,0:T(8,128)(2,1)S(1)}, bf16[16,240,128]{2,1,0:T(8,128)(2,1)}, u32[]{:S(2)}) copy-start(bf16[16,240,128]{2,1,0:T(8,128)(2,1)} %gather_fusion) | copy-start | bytes 2949124
  54.1 1.0 copy-start.5
  54.1 1.4 copy-start.13
  55.5 1.4 copy-start.11
  58.3 6.9 %copy-start.17 = (bf16[2,64,128,128]{3,2,1,0:T(8,128)(2,1)S(1)}, bf16[2,64,128,128]{3,2,1,0:T(8,128)(2,1)}, u32[]{:S(2)}) copy-start(bf16[2,64,128,128]{3,2,1,0:T(8,128)(2,1)} %param.13) | copy-start | bytes 12582916
  63.4 23.3 %collective-permute-start.3 = (bf16[8,240,128]{2,1,0:T(8,128)(2,1)}, bf16[8,240,128]{2,1,0:T(8,128)(2,1)}, u32[]{:S(2)}, u32[]{:S(2)}) collective-permute-start(bf16[8,240,128]{2,1,0:T(8,128)(2,1)} %copy.106), channel_id=1, source_target_pairs={{0,1},{1,2},{2,3},{3,4},{4,5},{5,6},{6,7},{7,8},{8,9},{9,10},{10,1... | collective-permute-start | bytes 1474568 | tf_op jit(solution)/shard_map/ppermute | solution.py:26
  67.8 21.9 %collective-permute-start.4 = (bf16[8,240,128]{2,1,0:T(8,128)(2,1)}, bf16[8,240,128]{2,1,0:T(8,128)(2,1)}, u32[]{:S(2)}, u32[]{:S(2)}) collective-permute-start(bf16[8,240,128]{2,1,0:T(8,128)(2,1)} %copy.108), channel_id=1, source_target_pairs={{1,0},{2,1},{3,2},{4,3},{5,4},{6,5},{7,6},{8,7},{9,8},{10,9},{11,1... | collective-permute-start | bytes 1474568 | tf_op jit(solution)/shard_map/ppermute | solution.py:27
  75.3 13.1 %copy-start.1 = (bf16[16,4,60,128]{3,0,2,1:T(8,128)(2,1)}, bf16[16,4,60,128]{3,0,2,1:T(8,128)(2,1)S(1)}, u32[]{:S(2)}) copy-start(bf16[16,4,60,128]{3,0,2,1:T(8,128)(2,1)S(1)} %copy.103) | copy-start | bytes 2949124
  75.3 38.7 %collective-permute-start.5 = (bf16[8,240,128]{2,1,0:T(8,128)(2,1)}, bf16[8,240,128]{2,1,0:T(8,128)(2,1)S(1)}, u32[]{:S(2)}, u32[]{:S(2)}) collective-permute-start(bf16[8,240,128]{2,1,0:T(8,128)(2,1)} %copy.108), channel_id=1, source_target_pairs={{0,8},{1,9},{2,10},{3,11},{4,12},{5,13},{6,14},{7,15},{8,0},{9,1},... | collective-permute-start | bytes 1474568 | tf_op jit(solution)/shard_map/ppermute | solution.py:16
  121.5 6.8 %copy-start.7 = (bf16[16,128,128]{2,1,0:T(8,128)(2,1)S(1)}, bf16[16,128,128]{2,1,0:T(8,128)(2,1)}, u32[]{:S(2)}) copy-start(bf16[16,128,128]{2,1,0:T(8,128)(2,1)} %gather_fusion.5) | copy-start | bytes 1572868
  128.2 2.0 %copy-start.9 = (bf16[16,128,128]{2,1,0:T(8,128)(2,1)S(1)}, bf16[16,128,128]{2,1,0:T(8,128)(2,1)}, u32[]{:S(2)}) copy-start(bf16[16,128,128]{2,1,0:T(8,128)(2,1)} %gather_fusion.1) | copy-start | bytes 1572868
  128.2 2.0 %copy-start.14 = (bf16[16,240,128]{2,1,0:T(8,128)(2,1)S(1)}, bf16[16,240,128]{2,1,0:T(8,128)(2,1)}, u32[]{:S(2)}) copy-start(bf16[16,240,128]{2,1,0:T(8,128)(2,1)} %gather_fusion.8) | copy-start | bytes 2949124
  130.2 1.4 copy-start.12
  131.6 1.2 copy-start.2
  131.6 1.3 copy-start.4
  131.6 1.7 copy-start.10
  134.6 6.4 %copy-start.24 = (s32[1,16]{1,0:T(1,128)S(1)}, s32[1,16]{1,0:T(1,128)}, u32[]{:S(2)}) copy-start(s32[1,16]{1,0:T(1,128)} %param.17) | copy-start | bytes 196
  140.9 5.9 %collective-permute-start.7 = (bf16[32,4096]{1,0:T(8,128)(2,1)S(1)}, bf16[32,4096]{1,0:T(8,128)(2,1)}, u32[]{:S(2)}, u32[]{:S(2)}) collective-permute-start(bf16[32,4096]{1,0:T(8,128)(2,1)S(1)} %convolution_convert_fusion), channel_id=1, source_target_pairs={{0,16},{16,0},{1,17},{17,1},{2,18},{18,2},{3,19},{19,3},{4,20},{20... | collective-permute-start | bytes 786440 | tf_op jit(solution)/shard_map/ppermute | solution.py:16
  141.0 1.6 collective-permute-start.6
  143.3 10.7 %all-to-all-start = ((s32[16,2,1]{1,2,0:T(1,128)}), s32[16,2,1]{1,2,0:T(1,128)S(1)}, u32[]{:S(2)}, u32[]{:S(2)}) async-start(s32[16,2,1]{1,2,0:T(1,128)} %bitcast.24), calls=%async_computation | async-start | bytes 16384 | tf_op jit(solution)/shard_map/all_to_all | solution.py:41
  154.0 12.8 %all-to-all-start.1 = ((bf16[16,2,4096]{2,1,0:T(2,128)(2,1)}), bf16[16,2,4096]{2,1,0:T(2,128)(2,1)S(1)}, u32[]{:S(2)}, u32[]{:S(2)}) async-start(bf16[16,2,4096]{2,1,0:T(2,128)(2,1)} %all_to_all.16), calls=%async_computation.1 | async-start | bytes 524288 | tf_op jit(solution)/shard_map/all_to_all | solution.py:38
  167.5 1.4 copy-start.16
  (3 other events, 2.8 us)
where the time goes:
time: 172 us; the launch traced here: 171 us
  local copies, waits for them, and re-layouts  68.9 us (40%)
  waiting for transfers between devices  51.6 us (30%)
  starting transfers between devices  30.9 us (18%)
  matrix products  17.7 us (10%)
    gather x8, local copies, waits for them, and re-layouts, on_device(): source_pool[block_positions[:, k]]  26.7 us
    ppermute x4, waiting for transfers between devices, partner(): return lax.ppermute(value, axis, pairs)  23.5 us
    ppermute x2, waiting for transfers between devices, padded_2(): before = lax.ppermute(last, axis, up)  15.8 us
    unnamed x58, local copies, waits for them, and re-layouts  15.8 us
    ppermute x4, starting transfers between devices, partner(): return lax.ppermute(value, axis, pairs)  15 us
    dot_general x8, matrix products, on_device(): jnp.einsum('brc,bcd->brd', source_pool[block_positions[:, k]], exchange_w...  8.04 us
    dot_general x2, matrix products, on_device(): jnp.einsum('se,ivey->ivsy', vertical_matrix, middle_state, precision=lax....  7.63 us
    ppermute x2, starting transfers between devices, padded_2(): after = lax.ppermute(leading, axis, down)  7.1 us
  transfers between devices with their start and end apart: 10, of which 6 were waited for; matrix products, arithmetic and copies ran while one was open for 15% of the time, Pallas kernels for 0%

commit v1 on v0

v1 whole, which is shorter than its diff:
```python
import functools

import jax
import jax.numpy as jnp
from jax import lax
from jax.experimental import pallas as pl
from jax.experimental.pallas import tpu as pltpu
from jax.sharding import PartitionSpec as P

SURF = 8
HALO = 8
FOLD = 8
STEPS = 2
CAP = 2
STAGES = 2

VMEM = pltpu.MemorySpace.VMEM
SMEM = pltpu.MemorySpace.SMEM
HBM = pltpu.MemorySpace.HBM
BF16 = jnp.bfloat16
F32 = jnp.float32


def spec(space):
    return pl.BlockSpec(memory_space=space)


def shape_of(shape, dtype=BF16):
    return jax.ShapeDtypeStruct(shape, dtype)


def params():
    return pltpu.CompilerParams(vmem_limit_bytes=40 * 1024 * 1024)


def cost(flops, moved):
    return pl.CostEstimate(flops=flops, bytes_accessed=moved, transcendentals=0)


def select_matrix(rows, fields, group, first, inverse):
    wide = rows // group * fields
    shape = (wide, rows) if inverse else (rows, wide)
    mine = lax.broadcasted_iota(jnp.int32, shape, 1 if inverse else 0)
    other = lax.broadcasted_iota(jnp.int32, shape, 0 if inverse else 1)
    source = (mine // group) * fields + first + mine % group
    return jnp.where(source == other, 1.0, 0.0).astype(BF16)


def split_kernel(fields, group, first, x, lead, last):
    half = lead.shape[0]
    pick = select_matrix(lead.shape[1], fields, group, first, False)
    for b in range(0, x.shape[0], 2):
        pair = jnp.concatenate([x[b], x[b + 1]], axis=1)
        got = jnp.dot(pick, pair, preferred_element_type=F32).astype(BF16)
        for i in range(2):
            dst, at = (lead, b + i) if b + i < half else (last, b + i - half)
            dst[at] = got[:, i * 128 : (i + 1) * 128]


def step_kernel(slots, tiles, before, lead, last, after, across, w, k_hi, k_lo, *rest):
    outs, (pool, mid, hi, lo, sems) = rest[:-5], rest[-5:]
    final = len(outs) == 2 and outs[0].shape[0] != outs[1].shape[0] or outs[0].shape[1] != outs[1].shape[1]
    copies, at = [], 0
    for i, src in enumerate((before, lead, last, after, across)):
        n = src.shape[0]
        copies.append(pltpu.make_async_copy(src, pool.at[pl.ds(at, n)], sems.at[i]))
        at += n
    for c in copies:
        c.start()
    for c in copies:
        c.wait()
    own = before.shape[0]
    count = lead.shape[0] + last.shape[0]
    entries = slots.shape[0] // count
    width = w.shape[1]
    for b in range(count):
        total = pool[own + b].astype(F32)
        for k in range(0, entries, 2):
            e = b * entries + k
            lhs = jnp.concatenate([pool[slots[e]], pool[slots[e + 1]]], axis=1)
            rhs = jnp.concatenate([w[tiles[e]], w[tiles[e + 1]]], axis=0)
            total = total + jnp.dot(lhs, rhs, preferred_element_type=F32)
        lanes = slice(b * width, (b + 1) * width)
        mid[:, lanes] = total
        top = total.astype(BF16)
        hi[:, lanes] = top
        lo[:, lanes] = (total - top.astype(F32)).astype(BF16)
    big, small = k_hi[...], k_lo[...]
    for b in range(0, count, 2):
        lanes = slice(b * width, (b + 2) * width)
        mixed = jnp.dot(big, hi[:, lanes], preferred_element_type=F32)
        mixed = mixed + jnp.dot(big, lo[:, lanes], preferred_element_type=F32)
        mixed = mixed + jnp.dot(small, hi[:, lanes], preferred_element_type=F32)
        new = (mid[:, lanes] + jnp.tanh(mixed)).astype(BF16)
        for i in range(2):
            piece = new[:, i * width : (i + 1) * width]
            if final:
                outs[0][b + i] = piece
                outs[1][b + i] = piece[: outs[1].shape[1]]
            else:
                half = outs[0].shape[0]
                dst, at = (outs[0], b + i) if b + i < half else (outs[1], b + i - half)
                dst[at] = piece


def run_step(tables, pieces, w, k_hi, k_lo, surface_rows):
    before, lead, last, after, across = pieces
    _, rows, width = lead.shape
    count = lead.shape[0] + last.shape[0]
    total = count + before.shape[0] + after.shape[0] + across.shape[0]
    if surface_rows:
        outs = [shape_of((count, rows, width)), shape_of((count, surface_rows, width))]
    else:
        outs = [shape_of(lead.shape), shape_of(last.shape)]
    return pl.pallas_call(
        step_kernel,
        out_shape=outs,
        in_specs=[spec(SMEM)] * 2 + [spec(HBM)] * 5 + [spec(VMEM)] * 3,
        out_specs=[spec(VMEM)] * 2,
        scratch_shapes=[
            pltpu.VMEM((total, rows, width), BF16),
            pltpu.VMEM((rows, count * width), F32),
            pltpu.VMEM((rows, count * width), BF16),
            pltpu.VMEM((rows, count * width), BF16),
            pltpu.SemaphoreType.DMA((5,)),
        ],
        compiler_params=params(),
        cost_estimate=cost(4 * 2 * count * rows * width * width, 8 * 1024 * 1024),
        name="substep",
    )(*tables, *pieces, w, k_hi, k_lo)


def partial_kernel(source, tile, slot, comp, weights, *rest):
    surfaces, (payload, held, sem) = rest[:-3], rest[-3:]
    entries = source.shape[0]
    copies = [
        pltpu.make_async_copy(weights.at[comp[0], tile[e]], held.at[e], sem.at[e])
        for e in range(entries)
    ]
    for c in copies:
        c.start()
    payload[...] = jnp.zeros(payload.shape, payload.dtype)
    for c in copies:
        c.wait()
    for e in range(entries):
        rows = [s[source[e]] for s in surfaces]
        rows = rows[0] if len(rows) == 1 else jnp.concatenate(rows, axis=0)
        payload[slot[e]] = jnp.dot(rows, held[e], preferred_element_type=F32).astype(BF16)


def merge_kernel(fields, group, *refs):
    stages, out = refs[:-1], refs[-1]
    width = out.shape[2]
    picks = [
        select_matrix(s.shape[1], fields, group, i * group, True) for i, s in enumerate(stages)
    ]
    for b in range(0, out.shape[0], 2):
        got = None
        for pick, s in zip(picks, stages):
            pair = jnp.concatenate([s[b], s[b + 1]], axis=1)
            part = jnp.dot(pick, pair, preferred_element_type=F32)
            got = part if got is None else got + part
        got = got.astype(BF16)
        out[b] = got[:, :width]
        out[b + 1] = got[:, width:]


def couple_kernel(fields, group, targets, state, received, *rest):
    surfaces, (out, total, top, sem) = rest[:-4], rest[-4:]
    del state
    count, rows, _ = total.shape
    total[...] = jnp.zeros(total.shape, F32)
    for j in range(targets.shape[0]):
        t = targets[j]

        @pl.when(t >= 0)
        def _(t=t, j=j):
            total[t] = total[t] + received[j].astype(F32)

    step = rows // len(surfaces)
    picks = [select_matrix(step, fields, group, i * group, True) for i in range(len(surfaces))]
    for b in range(count):
        if len(surfaces) == 1:
            top[b] = (surfaces[0][b].astype(F32) + total[b]).astype(BF16)
        else:
            got = None
            for i, s in enumerate(surfaces):
                new = (s[b].astype(F32) + total[b, i * step : (i + 1) * step]).astype(BF16)
                part = jnp.dot(picks[i], new, preferred_element_type=F32)
                got = part if got is None else got + part
            top[b] = got.astype(BF16)
    copy = pltpu.make_async_copy(top, out.at[:, pl.ds(0, rows)], sem)
    copy.start()
    copy.wait()


def partner(value, axis, distance):
    mask = 2**distance
    pairs = [(source, source ^ mask) for source in range(lax.axis_size(axis))]
    return lax.ppermute(value, axis, pairs)


def exchange(lead, last):
    peers = lax.axis_size("tile")
    up = [(i, (i + 1) % peers) for i in range(peers)]
    down = [(j, i) for i, j in up]
    across = partner(lead, "tile", peers.bit_length() - 2)
    before = lax.ppermute(last, "tile", up)
    after = lax.ppermute(lead, "tile", down)
    return before, after, across


def on_device(
    state,
    dyn_weights,
    vertical,
    remap_weights,
    neighbor_slots,
    neighbor_tiles,
    remap_source,
    remap_target,
    remap_tile,
    remap_dest,
):
    _, count, fields, levels, width = state.shape
    group = fields // STAGES
    rows = levels * group
    tile_count = lax.axis_size("tile")
    comp = lax.axis_index("comp")
    w = dyn_weights[0]
    plain = state[0].transpose(0, 2, 1, 3).reshape(count, levels * fields, width)

    kron = (vertical[0][:, None, :, None] * jnp.eye(group, dtype=F32)[None, :, None, :]).reshape(
        rows, rows
    )
    k_hi = lax.reduce_precision(kron, 8, 7)
    k_lo = (kron - k_hi).astype(BF16)
    k_hi = k_hi.astype(BF16)

    dest = remap_dest[0, :, 0]
    hits = (dest[:, None] == jnp.arange(tile_count, dtype=jnp.int32)[None, :]).astype(jnp.int32)
    rank = jnp.sum((jnp.cumsum(hits, axis=0) - 1) * hits, axis=1)
    slot_of = dest * CAP + rank
    place = jnp.arange(tile_count * CAP, dtype=jnp.int32)[:, None] == slot_of[None, :]
    target_buf = jnp.max(jnp.where(place, remap_target[0][None, :], -1), axis=1)

    stages = []
    for s in range(STAGES):
        if STAGES == 1:
            lead, last = plain[:HALO], plain[HALO:]
        else:
            lead, last = pl.pallas_call(
                functools.partial(split_kernel, fields, group, s * group),
                out_shape=[shape_of((HALO, rows, width)), shape_of((count - HALO, rows, width))],
                in_specs=[spec(VMEM)],
                out_specs=[spec(VMEM)] * 2,
                compiler_params=params(),
                cost_estimate=cost(2 * count * rows * rows * width, 2 * 1024 * 1024),
                name="split",
            )(plain)
        before, after, across = exchange(lead, last)
        stages.append((before, lead, last, after, across))

    targets = partner(target_buf, "comp", 0)
    targets = lax.all_to_all(targets, "tile", split_axis=0, concat_axis=0, tiled=True)
    tables = (neighbor_slots[0].reshape(-1), neighbor_tiles[0].reshape(-1))
    tables, targets = lax.optimization_barrier((tables, targets))

    for step in range(STEPS - 1):
        moved = []
        for pieces in stages:
            lead, last = run_step(tables, pieces, w, k_hi, k_lo, 0)
            before, after, across = exchange(lead, last)
            moved.append((before, lead, last, after, across))
        stages = moved
    ended = [run_step(tables, pieces, w, k_hi, k_lo, SURF * group) for pieces in stages]
    bodies = [e[0] for e in ended]
    surfaces = [e[1] for e in ended]

    entries = remap_source.shape[1]
    surface = SURF * fields
    payload = pl.pallas_call(
        partial_kernel,
        out_shape=shape_of((tile_count * CAP, surface, width)),
        in_specs=[spec(SMEM)] * 4 + [spec(HBM)] + [spec(VMEM)] * STAGES,
        out_specs=spec(VMEM),
        scratch_shapes=[
            pltpu.VMEM((entries, width, width), BF16),
            pltpu.SemaphoreType.DMA((entries,)),
        ],
        compiler_params=params(),
        cost_estimate=cost(2 * entries * surface * width * width, 2 * 1024 * 1024),
        name="partials",
    )(remap_source[0], remap_tile[0], slot_of, (1 - comp).reshape(1), remap_weights, *surfaces)

    payload = partner(payload, "comp", 0).reshape(tile_count, CAP * surface, width)
    received = lax.all_to_all(payload, "tile", split_axis=0, concat_axis=0, tiled=True)
    received = received.reshape(tile_count * CAP, surface, width)

    if STAGES == 1:
        whole = bodies[0]
    else:
        whole = pl.pallas_call(
            functools.partial(merge_kernel, fields, group),
            out_shape=shape_of((count, levels * fields, width)),
            in_specs=[spec(VMEM)] * STAGES,
            out_specs=spec(VMEM),
            compiler_params=params(),
            cost_estimate=cost(2 * count * rows * rows * width, 2 * 1024 * 1024),
            name="merge",
        )(*bodies)
    final = pl.pallas_call(
        functools.partial(couple_kernel, fields, group),
        out_shape=shape_of(whole.shape),
        in_specs=[spec(SMEM), spec(HBM), spec(VMEM)] + [spec(VMEM)] * STAGES,
        out_specs=spec(HBM),
        input_output_aliases={1: 0},
        scratch_shapes=[
            pltpu.VMEM((count, surface, width), F32),
            pltpu.VMEM((count, surface, width), BF16),
            pltpu.SemaphoreType.DMA,
        ],
        compiler_params=params(),
        cost_estimate=cost(1024, 1024 * 1024),
        name="couple",
    )(targets, whole, received, *surfaces)
    return final.reshape(count, levels, fields, width).transpose(0, 2, 1, 3)[None]


def solution(mesh):
    return jax.shard_map(
        on_device,
        mesh=mesh,
        in_specs=(
            P("comp", "tile", None, None, None),
            P("comp", None, None, None),
            P("comp", None, None),
            P(),
            P("comp", "tile", None),
            P("comp", "tile", None),
            P("comp", "tile"),
            P("comp", "tile"),
            P("comp", "tile"),
            P("comp", "tile", None),
        ),
        out_specs=P("comp", "tile", None, None, None),
        check_vma=False,
    )
```

time: 172 us -> 108 us (0.63)
  local copies, waits for them, and re-layouts: 68.9 us -> 9.38 us
  Pallas kernels: 0 us -> 21 us
  matrix products: 17.7 us -> 0 us
  waiting for transfers between devices: 51.6 us -> 36.3 us
  other arithmetic: 1.39 us -> 6.21 us
  starting transfers between devices: 30.9 us -> 34.4 us
    gather x14 -> x0, local copies, waits for them, and re-layouts: 36 us -> none  [the longest x8 26.7 us: on_device(): source_pool[block_positions[:, k]]]
    pallas_call x0 -> x9, Pallas kernels: none -> 21 us  [the longest x4 15.4 us: run_step(): pl.pallas_call(step_kernel, out_shape=outs, in_specs=[spec(SMEM)] * 2 + [...]
    dot_general x13 -> x0, matrix products: 17.7 us -> none  [the longest x8 8.04 us: on_device(): jnp.einsum('brc,bcd->brd', source_pool[block_positions[:, k]], exchange_w...]
    ppermute x4 -> x8, waiting for transfers between devices: 15.8 us -> 0.02 us  [the longest x4 0.01 us: exchange(): after = lax.ppermute(lead, 'tile', down)]
    ppermute x4 -> x8, starting transfers between devices: 8.86 us -> 24.1 us  [the longest x4 22.6 us: exchange(): after = lax.ppermute(lead, 'tile', down)]
    ppermute x4 -> x6, starting transfers between devices: 15 us -> 2.38 us  [partner(): return lax.ppermute(value, axis, pairs)]
    unnamed x58 -> x23, local copies, waits for them, and re-layouts: 15.8 us -> 4.29 us
    slice x9 -> x0, local copies, waits for them, and re-layouts: 5.27 us -> none  [the longest x5 2.26 us: padded_2(): leading = lax.slice_in_dim(array, 0, width, axis=dim)]
  transfers between devices with their start and end apart: 10 -> 16, of which waited for: 6 -> 5; matrix products, arithmetic and copies ran while one was open for 15% -> 11% of each run, Pallas kernels for 0% -> 13%
where the time goes in v1:
time: 108 us
  waiting for transfers between devices  36.3 us (34%)
  starting transfers between devices  34.4 us (32%)
  Pallas kernels  21 us (19%)
  local copies, waits for them, and re-layouts  9.38 us (9%)
  other arithmetic  6.21 us (6%)
    ppermute x4, starting transfers between devices, exchange(): after = lax.ppermute(lead, 'tile', down)  22.6 us
    ppermute x6, waiting for transfers between devices, partner(): return lax.ppermute(value, axis, pairs)  18.9 us
    pallas_call x4, Pallas kernels, run_step(): pl.pallas_call(step_kernel, out_shape=outs, in_specs=[spec(SMEM)] * 2 + [...  15.4 us
    all_to_all x1, waiting for transfers between devices, on_device(): lax.all_to_all(targets, 'tile', split_axis=0, concat_axis=0, tiled=True)  8.79 us
    all_to_all x1, waiting for transfers between devices, on_device(): lax.all_to_all(payload, 'tile', split_axis=0, concat_axis=0, tiled=True)  8.57 us
    all_to_all x1, starting transfers between devices, on_device(): lax.all_to_all(payload, 'tile', split_axis=0, concat_axis=0, tiled=True)  4.47 us
    unnamed x23, local copies, waits for them, and re-layouts  4.29 us
    mul x1, local copies, waits for them, and re-layouts, on_device(): vertical[0][:, None, :, None] * jnp.eye(group, dtype=F32)[None, :, None, :]  3.64 us
  transfers between devices with their start and end apart: 16, of which 5 were waited for; matrix products, arithmetic and copies ran while one was open for 11% of the time, Pallas kernels for 13%

profile of v1, /device:TPU:0, one launch (start us, length us, event | category | flops | bytes accessed | tf_op | source)
XLA Modules:
  0.0 107.6 jit_solution(12298549262136919974)
XLA Ops:
  0.0 1.2 %copy-done.2 = bf16[1,16,4,60,128]{4,2,3,1,0:T(4,128)(2,1)S(1)} copy-done((bf16[1,16,4,60,128]{4,2,3,1,0:T(4,128)(2,1)S(1)}, bf16[1,16,4,60,128]{4,2,3,1,0:T(4,128)(2,1)}, u32[]{:S(2)}) %copy-start.2) | copy-done | bytes 983064
  1.5 7.0 %collective-permute-start.8 = (bf16[8,120,128]{2,1,0:T(8,128)(2,1)S(1)}, bf16[8,120,128]{2,1,0:T(8,128)(2,1)}, u32[]{:S(2)}, u32[]{:S(2)}) collective-permute-start(bf16[8,120,128]{2,1,0:T(8,128)(2,1)S(1)} %get-tuple-element.29.lead), channel_id=1, source_target_pairs={{1,0},{2,1},{3,2},{4,3},{5,4},{6,5},{7,6},{8,7},{9,8},{10,9},{11,1... | collective-permute-start | bytes 737288 | tf_op jit(solution)/shard_map/ppermute | solution.py:209
  8.5 0.7 fusion.1
  9.3 0.8 select_reduce_fusion.1
  10.8 0.7 select_reduce_fusion
  11.7 1.2 %copy-done.3 = bf16[1,16,4,60,128]{4,2,3,1,0:T(4,128)(2,1)S(1)} copy-done((bf16[1,16,4,60,128]{4,2,3,1,0:T(4,128)(2,1)S(1)}, bf16[1,16,4,60,128]{4,2,3,1,0:T(4,128)(2,1)}, u32[]{:S(2)}) %copy-start.3) | copy-done | bytes 983064
  13.2 5.6 %collective-permute-start.2 = (bf16[8,120,128]{2,1,0:T(8,128)(2,1)S(1)}, bf16[8,120,128]{2,1,0:T(8,128)(2,1)S(1)}, u32[]{:S(2)}, u32[]{:S(2)}) collective-permute-start(bf16[8,120,128]{2,1,0:T(8,128)(2,1)S(1)} %get-tuple-element.24.lead), channel_id=1, source_target_pairs={{1,0},{2,1},{3,2},{4,3},{5,4},{6,5},{7,6},{8,7},{9,8},{10,9},{11,1... | collective-permute-start | bytes 737288 | tf_op jit(solution)/shard_map/ppermute | solution.py:209
  18.8 0.8 copy.24
  19.6 2.5 %broadcast_multiply_fusion = f32[60,2,60,2]{3,2,1,0:T(8,128)} fusion(f32[2,2]{1,0:T(2,128)S(1)} %compare_convert_fusion, f32[60,60]{1,0:T(8,128)S(1)} %bitcast.33), kind=kLoop, calls=%fused_computation | loop fusion | flops 14400 | bytes 72016 | tf_op jit(solution)/shard_map/mul | solution.py:233
  22.1 3.6 %mul.35 = f32[120,120]{1,0:T(8,128)S(1)} reshape(f32[60,2,60,2]{3,2,1,0:T(8,128)} %broadcast_multiply_fusion) | data formatting | bytes 115200 | tf_op jit(solution)/shard_map/mul | solution.py:233
  25.9 1.1 %collective-permute-start.3 = (bf16[8,120,128]{2,1,0:T(8,128)(2,1)S(1)}, bf16[8,120,128]{2,1,0:T(8,128)(2,1)}, u32[]{:S(2)}, u32[]{:S(2)}) collective-permute-start(bf16[8,120,128]{2,1,0:T(8,128)(2,1)S(1)} %get-tuple-element.24.lead), channel_id=1, source_target_pairs={{0,8},{1,9},{2,10},{3,11},{4,12},{5,13},{6,14},{7,15},{8,0},{9,1},... | collective-permute-start | bytes 737288 | tf_op jit(solution)/shard_map/ppermute | solution.py:200
  27.0 0.7 all_to_all.11
  27.7 3.5 %all-to-all-start = ((s32[16,2,1]{1,2,0:T(1,128)}), s32[16,2,1]{1,2,0:T(1,128)S(1)}, u32[]{:S(2)}, u32[]{:S(2)}) async-start(s32[16,2,1]{1,2,0:T(1,128)} %bitcast.2), calls=%async_computation | async-start | bytes 16384 | tf_op jit(solution)/shard_map/all_to_all | solution.py:265
  31.4 8.8 %all-to-all-done = s32[16,2,1]{1,2,0:T(1,128)S(1)} async-done(((s32[16,2,1]{1,2,0:T(1,128)}), s32[16,2,1]{1,2,0:T(1,128)S(1)}, u32[]{:S(2)}, u32[]{:S(2)}) %all-to-all-start) | async-done | bytes 160 | tf_op jit(solution)/shard_map/all_to_all | solution.py:265
  40.7 0.7 reduce.3
  41.5 1.4 %collective-permute-start.1 = (bf16[8,120,128]{2,1,0:T(8,128)(2,1)S(1)}, bf16[8,120,128]{2,1,0:T(8,128)(2,1)S(1)}, u32[]{:S(2)}, u32[]{:S(2)}) collective-permute-start(bf16[8,120,128]{2,1,0:T(8,128)(2,1)S(1)} %get-tuple-element.23.last), channel_id=1, source_target_pairs={{0,1},{1,2},{2,3},{3,4},{4,5},{5,6},{6,7},{7,8},{8,9},{9,10},{10,1... | collective-permute-start | bytes 737288 | tf_op jit(solution)/shard_map/ppermute | solution.py:208
  43.0 4.2 %substep.6 = (bf16[8,120,128]{2,1,0:T(8,128)(2,1)}, bf16[8,120,128]{2,1,0:T(8,128)(2,1)}) custom-call(s32[64]{0:T(128)S(1)} %reshape_squeeze.6.slots, s32[64]{0:T(128)S(1)} %reshape_squeeze.7.tiles, bf16[8,120,128]{2,1,0:T(8,128)(2,1)} %collective-permute-done.7.before, bf16[8,120,128]{2,1,0:T(8,128)(2,1)S(1)} %get-tuple-element.29.lead, ...), custom_call_target="tpu_custom_call" | custom-call | flops 251658240 | bytes 8388608 | tf_op jit(solution)/shard_map/substep/pallas_call | solution.py:115
  47.2 4.3 %collective-permute-start.11 = (bf16[8,120,128]{2,1,0:T(8,128)(2,1)}, bf16[8,120,128]{2,1,0:T(8,128)(2,1)S(1)}, u32[]{:S(2)}, u32[]{:S(2)}) collective-permute-start(bf16[8,120,128]{2,1,0:T(8,128)(2,1)} %get-tuple-element.31.lead), channel_id=1, source_target_pairs={{1,0},{2,1},{3,2},{4,3},{5,4},{6,5},{7,6},{8,7},{9,8},{10,9},{11,1... | collective-permute-start | bytes 737288 | tf_op jit(solution)/shard_map/ppermute | solution.py:209
  51.4 0.8 collective-permute-start.12
  52.3 4.7 %substep.4 = (bf16[8,120,128]{2,1,0:T(8,128)(2,1)S(1)}, bf16[8,120,128]{2,1,0:T(8,128)(2,1)}) custom-call(s32[64]{0:T(128)S(1)} %reshape_squeeze.6.slots, s32[64]{0:T(128)S(1)} %reshape_squeeze.7.tiles, bf16[8,120,128]{2,1,0:T(8,128)(2,1)S(1)} %collective-permute-done.1.before, bf16[8,120,128]{2,1,0:T(8,128)(2,1)S(1)} %get-tuple-element.24.lead, ...), custom_call_target="tpu_custom_call" | custom-call | flops 251658240 | bytes 8388608 | tf_op jit(solution)/shard_map/substep/pallas_call | solution.py:115
  57.0 5.7 %collective-permute-start.5 = (bf16[8,120,128]{2,1,0:T(8,128)(2,1)S(1)}, bf16[8,120,128]{2,1,0:T(8,128)(2,1)S(1)}, u32[]{:S(2)}, u32[]{:S(2)}) collective-permute-start(bf16[8,120,128]{2,1,0:T(8,128)(2,1)S(1)} %get-tuple-element.26.lead), channel_id=1, source_target_pairs={{1,0},{2,1},{3,2},{4,3},{5,4},{6,5},{7,6},{8,7},{9,8},{10,9},{11,1... | collective-permute-start | bytes 737288 | tf_op jit(solution)/shard_map/ppermute | solution.py:209
  63.0 12.2 %collective-permute-done.12.across = bf16[8,120,128]{2,1,0:T(8,128)(2,1)} collective-permute-done((bf16[8,120,128]{2,1,0:T(8,128)(2,1)}, bf16[8,120,128]{2,1,0:T(8,128)(2,1)}, u32[]{:S(2)}, u32[]{:S(2)}) %collective-permute-start.12) | collective-permute-done | bytes 245792 | tf_op jit(solution)/shard_map/ppermute | solution.py:200
  75.2 3.1 %substep.7 = (bf16[16,120,128]{2,1,0:T(8,128)(2,1)S(1)}, bf16[16,16,128]{2,1,0:T(8,128)(2,1)S(1)}) custom-call(s32[64]{0:T(128)S(1)} %reshape_squeeze.6.slots, s32[64]{0:T(128)S(1)} %reshape_squeeze.7.tiles, bf16[8,120,128]{2,1,0:T(8,128)(2,1)} %collective-permute-done.10.before, bf16[8,120,128]{2,1,0:T(8,128)(2,1)} %get-tuple-element.31.lead, ...), custom_call_target="tpu_custom_call" | custom-call | flops 251658240 | bytes 8388608 | tf_op jit(solution)/shard_map/substep/pallas_call | solution.py:115
  78.3 5.1 %collective-permute-done.6.across = bf16[8,120,128]{2,1,0:T(8,128)(2,1)} collective-permute-done((bf16[8,120,128]{2,1,0:T(8,128)(2,1)S(1)}, bf16[8,120,128]{2,1,0:T(8,128)(2,1)}, u32[]{:S(2)}, u32[]{:S(2)}) %collective-permute-start.6) | collective-permute-done | bytes 245792 | tf_op jit(solution)/shard_map/ppermute | solution.py:200
  83.4 0.9 copy-done.5
  84.4 3.4 %substep.5 = (bf16[16,120,128]{2,1,0:T(8,128)(2,1)S(1)}, bf16[16,16,128]{2,1,0:T(8,128)(2,1)S(1)}) custom-call(s32[64]{0:T(128)S(1)} %reshape_squeeze.6.slots, s32[64]{0:T(128)S(1)} %reshape_squeeze.7.tiles, bf16[8,120,128]{2,1,0:T(8,128)(2,1)} %collective-permute-done.4.before, bf16[8,120,128]{2,1,0:T(8,128)(2,1)S(1)} %copy-done.5, ...), custom_call_target="tpu_custom_call" | custom-call | flops 251658240 | bytes 8388608 | tf_op jit(solution)/shard_map/substep/pallas_call | solution.py:115
  87.8 1.7 %partials.1 = bf16[32,32,128]{2,1,0:T(8,128)(2,1)S(1)} custom-call(s32[16]{0:T(128)S(1)} %bitcast.31, s32[16]{0:T(128)S(1)} %bitcast.32, s32[16]{0:T(128)S(1)} %multiply_add_fusion.slot, s32[1]{0:T(128)} %bitcast.11.comp, bf16[2,64,128,128]{3,2,1,0:T(8,128)(2,1)S(1)} %copy-done.1, bf16[16,16,128]{2,1,0:T(8,128)(2,1)S(1)} %get-tuple-element.33.rest_0_, ...), custom_call_target="tpu_custom_call" | custom-call | flops 16777216 | bytes 2097152 | tf_op jit(solution)/shard_map/partials/pallas_call | solution.py:282
  89.6 1.7 %collective-permute-done.13 = bf16[32,32,128]{2,1,0:T(8,128)(2,1)} collective-permute-done((bf16[32,32,128]{2,1,0:T(8,128)(2,1)S(1)}, bf16[32,32,128]{2,1,0:T(8,128)(2,1)}, u32[]{:S(2)}, u32[]{:S(2)}) %collective-permute-start.13) | collective-permute-done | bytes 262176 | tf_op jit(solution)/shard_map/ppermute | solution.py:200
  91.3 4.5 %all-to-all-start.1 = ((bf16[16,64,128]{2,1,0:T(8,128)(2,1)}), bf16[16,64,128]{2,1,0:T(8,128)(2,1)S(1)}, u32[]{:S(2)}, u32[]{:S(2)}) async-start(bf16[16,64,128]{2,1,0:T(8,128)(2,1)} %bitcast.12), calls=%async_computation.1 | async-start | bytes 524288 | tf_op jit(solution)/shard_map/all_to_all | solution.py:297
  95.7 1.6 %merge.1.state = bf16[16,240,128]{2,1,0:T(8,128)(2,1)} custom-call(bf16[16,120,128]{2,1,0:T(8,128)(2,1)S(1)} %get-tuple-element.27.refs_0_, bf16[16,120,128]{2,1,0:T(8,128)(2,1)S(1)} %get-tuple-element.32.refs_1_), custom_call_target="tpu_custom_call" | custom-call | flops 58982400 | bytes 2097152 | tf_op jit(solution)/shard_map/merge/pallas_call | solution.py:303
  97.3 8.6 %all-to-all-done.1 = bf16[16,64,128]{2,1,0:T(8,128)(2,1)S(1)} async-done(((bf16[16,64,128]{2,1,0:T(8,128)(2,1)}), bf16[16,64,128]{2,1,0:T(8,128)(2,1)S(1)}, u32[]{:S(2)}, u32[]{:S(2)}) %all-to-all-start.1) | async-done | bytes 262176 | tf_op jit(solution)/shard_map/all_to_all | solution.py:297
  105.9 1.7 %couple.1 = bf16[16,240,128]{2,1,0:T(8,128)(2,1)} custom-call(s32[32]{0:T(128)S(1)} %all_to_all.13.targets, bf16[16,240,128]{2,1,0:T(8,128)(2,1)} %merge.1.state, bf16[32,32,128]{2,1,0:T(8,128)(2,1)S(1)} %bitcast.30, bf16[16,16,128]{2,1,0:T(8,128)(2,1)S(1)} %get-tuple-element.33.rest_0_, ...), custom_call_target="tpu_custom_call", output_to_operand_aliasing={{}: (1, {})} | custom-call | flops 1024 | bytes 1048576 | tf_op jit(solution)/shard_map/couple/pallas_call | solution.py:312
  (47 shorter events, 2.8 us)
Async XLA Ops:
  0.0 1.2 %copy-start.2 = (bf16[1,16,4,60,128]{4,2,3,1,0:T(4,128)(2,1)S(1)}, bf16[1,16,4,60,128]{4,2,3,1,0:T(4,128)(2,1)}, u32[]{:S(2)}) copy-start(bf16[1,16,4,60,128]{4,2,3,1,0:T(4,128)(2,1)} %param.10) | copy-start | bytes 2949124
  1.5 40.0 %collective-permute-start.8 = (bf16[8,120,128]{2,1,0:T(8,128)(2,1)S(1)}, bf16[8,120,128]{2,1,0:T(8,128)(2,1)}, u32[]{:S(2)}, u32[]{:S(2)}) collective-permute-start(bf16[8,120,128]{2,1,0:T(8,128)(2,1)S(1)} %get-tuple-element.29.lead), channel_id=1, source_target_pairs={{1,0},{2,1},{3,2},{4,3},{5,4},{6,5},{7,6},{8,7},{9,8},{10,9},{11,1... | collective-permute-start | bytes 737288 | tf_op jit(solution)/shard_map/ppermute | solution.py:209
  8.5 34.4 %collective-permute-start.9 = (bf16[8,120,128]{2,1,0:T(8,128)(2,1)S(1)}, bf16[8,120,128]{2,1,0:T(8,128)(2,1)}, u32[]{:S(2)}, u32[]{:S(2)}) collective-permute-start(bf16[8,120,128]{2,1,0:T(8,128)(2,1)S(1)} %get-tuple-element.29.lead), channel_id=1, source_target_pairs={{0,8},{1,9},{2,10},{3,11},{4,12},{5,13},{6,14},{7,15},{8,0},{9,1},... | collective-permute-start | bytes 737288 | tf_op jit(solution)/shard_map/ppermute | solution.py:200
  11.5 14.4 %collective-permute-start = (s32[32]{0:T(128)S(1)}, s32[32]{0:T(128)S(1)}, u32[]{:S(2)}, u32[]{:S(2)}) collective-permute-start(s32[32]{0:T(128)S(1)} %select_reduce_fusion), channel_id=1, source_target_pairs={{0,16},{16,0},{1,17},{17,1},{2,18},{18,2},{3,19},{19,3},{4,20},{20... | collective-permute-start | bytes 392 | tf_op jit(solution)/shard_map/ppermute | solution.py:200
  11.6 31.4 %collective-permute-start.7 = (bf16[8,120,128]{2,1,0:T(8,128)(2,1)S(1)}, bf16[8,120,128]{2,1,0:T(8,128)(2,1)}, u32[]{:S(2)}, u32[]{:S(2)}) collective-permute-start(bf16[8,120,128]{2,1,0:T(8,128)(2,1)S(1)} %get-tuple-element.28.last), channel_id=1, source_target_pairs={{0,1},{1,2},{2,3},{3,4},{4,5},{5,6},{6,7},{7,8},{8,9},{9,10},{10,1... | collective-permute-start | bytes 737288 | tf_op jit(solution)/shard_map/ppermute | solution.py:208
  11.7 1.2 %copy-start.3 = (bf16[1,16,4,60,128]{4,2,3,1,0:T(4,128)(2,1)S(1)}, bf16[1,16,4,60,128]{4,2,3,1,0:T(4,128)(2,1)}, u32[]{:S(2)}) copy-start(bf16[1,16,4,60,128]{4,2,3,1,0:T(4,128)(2,1)} %param.10) | copy-start | bytes 2949124
  13.2 39.1 %collective-permute-start.2 = (bf16[8,120,128]{2,1,0:T(8,128)(2,1)S(1)}, bf16[8,120,128]{2,1,0:T(8,128)(2,1)S(1)}, u32[]{:S(2)}, u32[]{:S(2)}) collective-permute-start(bf16[8,120,128]{2,1,0:T(8,128)(2,1)S(1)} %get-tuple-element.24.lead), channel_id=1, source_target_pairs={{1,0},{2,1},{3,2},{4,3},{5,4},{6,5},{7,6},{8,7},{9,8},{10,9},{11,1... | collective-permute-start | bytes 737288 | tf_op jit(solution)/shard_map/ppermute | solution.py:209
  19.6 6.2 %copy-start.8 = (s32[1,16,4]{1,2,0:T(4,128)S(1)}, s32[1,16,4]{1,2,0:T(4,128)}, u32[]{:S(2)}) copy-start(s32[1,16,4]{1,2,0:T(4,128)} %param.14) | copy-start | bytes 772
  19.6 11.7 %copy-start.9 = (s32[1,16,4]{1,2,0:T(4,128)S(1)}, s32[1,16,4]{1,2,0:T(4,128)}, u32[]{:S(2)}) copy-start(s32[1,16,4]{1,2,0:T(4,128)} %param.15) | copy-start | bytes 772
  19.6 23.4 %copy-start = (bf16[1,64,128,128]{3,2,1,0:T(8,128)(2,1)S(1)}, bf16[1,64,128,128]{3,2,1,0:T(8,128)(2,1)}, u32[]{:S(2)}) copy-start(bf16[1,64,128,128]{3,2,1,0:T(8,128)(2,1)} %param.11) | copy-start | bytes 6291460
  25.9 26.4 %collective-permute-start.3 = (bf16[8,120,128]{2,1,0:T(8,128)(2,1)S(1)}, bf16[8,120,128]{2,1,0:T(8,128)(2,1)}, u32[]{:S(2)}, u32[]{:S(2)}) collective-permute-start(bf16[8,120,128]{2,1,0:T(8,128)(2,1)S(1)} %get-tuple-element.24.lead), channel_id=1, source_target_pairs={{0,8},{1,9},{2,10},{3,11},{4,12},{5,13},{6,14},{7,15},{8,0},{9,1},... | collective-permute-start | bytes 737288 | tf_op jit(solution)/shard_map/ppermute | solution.py:200
  27.7 12.5 %all-to-all-start = ((s32[16,2,1]{1,2,0:T(1,128)}), s32[16,2,1]{1,2,0:T(1,128)S(1)}, u32[]{:S(2)}, u32[]{:S(2)}) async-start(s32[16,2,1]{1,2,0:T(1,128)} %bitcast.2), calls=%async_computation | async-start | bytes 16384 | tf_op jit(solution)/shard_map/all_to_all | solution.py:265
  41.5 10.7 %collective-permute-start.1 = (bf16[8,120,128]{2,1,0:T(8,128)(2,1)S(1)}, bf16[8,120,128]{2,1,0:T(8,128)(2,1)S(1)}, u32[]{:S(2)}, u32[]{:S(2)}) collective-permute-start(bf16[8,120,128]{2,1,0:T(8,128)(2,1)S(1)} %get-tuple-element.23.last), channel_id=1, source_target_pairs={{0,1},{1,2},{2,3},{3,4},{4,5},{5,6},{6,7},{7,8},{8,9},{9,10},{10,1... | collective-permute-start | bytes 737288 | tf_op jit(solution)/shard_map/ppermute | solution.py:208
  47.2 15.8 %collective-permute-start.11 = (bf16[8,120,128]{2,1,0:T(8,128)(2,1)}, bf16[8,120,128]{2,1,0:T(8,128)(2,1)S(1)}, u32[]{:S(2)}, u32[]{:S(2)}) collective-permute-start(bf16[8,120,128]{2,1,0:T(8,128)(2,1)} %get-tuple-element.31.lead), channel_id=1, source_target_pairs={{1,0},{2,1},{3,2},{4,3},{5,4},{6,5},{7,6},{8,7},{9,8},{10,9},{11,1... | collective-permute-start | bytes 737288 | tf_op jit(solution)/shard_map/ppermute | solution.py:209
  51.4 23.7 %collective-permute-start.12 = (bf16[8,120,128]{2,1,0:T(8,128)(2,1)}, bf16[8,120,128]{2,1,0:T(8,128)(2,1)}, u32[]{:S(2)}, u32[]{:S(2)}) collective-permute-start(bf16[8,120,128]{2,1,0:T(8,128)(2,1)} %get-tuple-element.31.lead), channel_id=1, source_target_pairs={{0,8},{1,9},{2,10},{3,11},{4,12},{5,13},{6,14},{7,15},{8,0},{9,1},... | collective-permute-start | bytes 737288 | tf_op jit(solution)/shard_map/ppermute | solution.py:200
  52.3 22.9 %collective-permute-start.10 = (bf16[8,120,128]{2,1,0:T(8,128)(2,1)}, bf16[8,120,128]{2,1,0:T(8,128)(2,1)}, u32[]{:S(2)}, u32[]{:S(2)}) collective-permute-start(bf16[8,120,128]{2,1,0:T(8,128)(2,1)} %get-tuple-element.30.last), channel_id=1, source_target_pairs={{0,1},{1,2},{2,3},{3,4},{4,5},{5,6},{6,7},{7,8},{8,9},{9,10},{10,1... | collective-permute-start | bytes 737288 | tf_op jit(solution)/shard_map/ppermute | solution.py:208
  56.9 26.5 %copy-start.4 = (bf16[8,120,128]{2,1,0:T(8,128)(2,1)}, bf16[8,120,128]{2,1,0:T(8,128)(2,1)S(1)}, u32[]{:S(2)}) copy-start(bf16[8,120,128]{2,1,0:T(8,128)(2,1)S(1)} %get-tuple-element.26.lead) | copy-start | bytes 737284
  57.0 30.8 %copy-start.6 = (s32[1,16]{1,0:T(1,128)S(1)}, s32[1,16]{1,0:T(1,128)}, u32[]{:S(2)}) copy-start(s32[1,16]{1,0:T(1,128)} %param.16) | copy-start | bytes 196
  57.0 30.8 %copy-start.7 = (s32[1,16]{1,0:T(1,128)S(1)}, s32[1,16]{1,0:T(1,128)}, u32[]{:S(2)}) copy-start(s32[1,16]{1,0:T(1,128)} %param.18) | copy-start | bytes 196
  57.0 21.3 %collective-permute-start.5 = (bf16[8,120,128]{2,1,0:T(8,128)(2,1)S(1)}, bf16[8,120,128]{2,1,0:T(8,128)(2,1)S(1)}, u32[]{:S(2)}, u32[]{:S(2)}) collective-permute-start(bf16[8,120,128]{2,1,0:T(8,128)(2,1)S(1)} %get-tuple-element.26.lead), channel_id=1, source_target_pairs={{1,0},{2,1},{3,2},{4,3},{5,4},{6,5},{7,6},{8,7},{9,8},{10,9},{11,1... | collective-permute-start | bytes 737288 | tf_op jit(solution)/shard_map/ppermute | solution.py:209
  62.6 20.8 %collective-permute-start.6 = (bf16[8,120,128]{2,1,0:T(8,128)(2,1)S(1)}, bf16[8,120,128]{2,1,0:T(8,128)(2,1)}, u32[]{:S(2)}, u32[]{:S(2)}) collective-permute-start(bf16[8,120,128]{2,1,0:T(8,128)(2,1)S(1)} %get-tuple-element.26.lead), channel_id=1, source_target_pairs={{0,8},{1,9},{2,10},{3,11},{4,12},{5,13},{6,14},{7,15},{8,0},{9,1},... | collective-permute-start | bytes 737288 | tf_op jit(solution)/shard_map/ppermute | solution.py:200
  63.0 20.5 %collective-permute-start.4 = (bf16[8,120,128]{2,1,0:T(8,128)(2,1)}, bf16[8,120,128]{2,1,0:T(8,128)(2,1)}, u32[]{:S(2)}, u32[]{:S(2)}) collective-permute-start(bf16[8,120,128]{2,1,0:T(8,128)(2,1)} %get-tuple-element.25.last), channel_id=1, source_target_pairs={{0,1},{1,2},{2,3},{3,4},{4,5},{5,6},{6,7},{7,8},{8,9},{9,10},{10,1... | collective-permute-start | bytes 737288 | tf_op jit(solution)/shard_map/ppermute | solution.py:208
  63.0 24.8 %copy-start.1 = (bf16[2,64,128,128]{3,2,1,0:T(8,128)(2,1)S(1)}, bf16[2,64,128,128]{3,2,1,0:T(8,128)(2,1)}, u32[]{:S(2)}) copy-start(bf16[2,64,128,128]{3,2,1,0:T(8,128)(2,1)} %weights.1) | copy-start | bytes 12582916
  83.4 0.9 copy-start.5
  89.5 1.7 %collective-permute-start.13 = (bf16[32,32,128]{2,1,0:T(8,128)(2,1)S(1)}, bf16[32,32,128]{2,1,0:T(8,128)(2,1)}, u32[]{:S(2)}, u32[]{:S(2)}) collective-permute-start(bf16[32,32,128]{2,1,0:T(8,128)(2,1)S(1)} %partials.1), channel_id=1, source_target_pairs={{0,16},{16,0},{1,17},{17,1},{2,18},{18,2},{3,19},{19,3},{4,20},{20... | collective-permute-start | bytes 786440 | tf_op jit(solution)/shard_map/ppermute | solution.py:200
  91.3 14.6 %all-to-all-start.1 = ((bf16[16,64,128]{2,1,0:T(8,128)(2,1)}), bf16[16,64,128]{2,1,0:T(8,128)(2,1)S(1)}, u32[]{:S(2)}, u32[]{:S(2)}) async-start(bf16[16,64,128]{2,1,0:T(8,128)(2,1)} %bitcast.12), calls=%async_computation.1 | async-start | bytes 524288 | tf_op jit(solution)/shard_map/all_to_all | solution.py:297

commit v2 on v1

--- a/solution.py
+++ b/solution.py
@@ -12,6 +12,7 @@
 FOLD = 8
 STEPS = 2
 CAP = 2
+HEAD = 8
 STAGES = 2
 
 VMEM = pltpu.MemorySpace.VMEM
@@ -44,6 +45,39 @@
     other = lax.broadcasted_iota(jnp.int32, shape, 0 if inverse else 1)
     source = (mine // group) * fields + first + mine % group
     return jnp.where(source == other, 1.0, 0.0).astype(BF16)
+
+
+def expand_kernel(group, v, k_hi, k_lo):
+    rows, levels = k_hi.shape[0], v.shape[0]
+    shape = (rows, levels)
+    level = lax.broadcasted_iota(jnp.int32, shape, 0) // group
+    spread = jnp.where(level == lax.broadcasted_iota(jnp.int32, shape, 1), 1.0, 0.0).astype(BF16)
+    square = (rows, rows)
+    same = (
+        lax.broadcasted_iota(jnp.int32, square, 0) % group
+        == lax.broadcasted_iota(jnp.int32, square, 1) % group
+    )
+    value = v[...]
+    high = value.astype(BF16)
+    low = (value - high.astype(F32)).astype(BF16)
+    for part, out in ((high, k_hi), (low, k_lo)):
+        tall = jnp.dot(spread, part, preferred_element_type=F32).astype(BF16)
+        full = lax.dot_general(
+            tall, spread, (((1,), (1,)), ((), ())), preferred_element_type=F32
+        )
+        out[...] = jnp.where(same, full, 0.0).astype(BF16)
+
+
+def gather_kernel(tile, comp, weights, held, sem):
+    entries = held.shape[0]
+    copies = [
+        pltpu.make_async_copy(weights.at[comp[0], tile[e]], held.at[e], sem.at[e])
+        for e in range(entries)
+    ]
+    for c in copies:
+        c.start()
+    for c in copies:
+        c.wait()
 
 
 def split_kernel(fields, group, first, x, lead, last):
@@ -130,22 +164,17 @@
     )(*tables, *pieces, w, k_hi, k_lo)
 
 
-def partial_kernel(source, tile, slot, comp, weights, *rest):
-    surfaces, (payload, held, sem) = rest[:-3], rest[-3:]
-    entries = source.shape[0]
-    copies = [
-        pltpu.make_async_copy(weights.at[comp[0], tile[e]], held.at[e], sem.at[e])
-        for e in range(entries)
-    ]
-    for c in copies:
-        c.start()
+def partial_kernel(source, slot, header, held, *rest):
+    surfaces, payload = rest[:-1], rest[-1]
+    surface = sum(s.shape[1] for s in surfaces)
     payload[...] = jnp.zeros(payload.shape, payload.dtype)
-    for c in copies:
-        c.wait()
-    for e in range(entries):
+    payload[:, CAP * surface :, :] = header[...]
+    for e in range(source.shape[0]):
         rows = [s[source[e]] for s in surfaces]
         rows = rows[0] if len(rows) == 1 else jnp.concatenate(rows, axis=0)
-        payload[slot[e]] = jnp.dot(rows, held[e], preferred_element_type=F32).astype(BF16)
+        value = jnp.dot(rows, held[e], preferred_element_type=F32).astype(BF16)
+        at = pl.multiple_of((slot[e] % CAP) * surface, surface)
+        payload[slot[e] // CAP, pl.ds(at, surface), :] = value
 
 
 def merge_kernel(fields, group, *refs):
@@ -165,17 +194,23 @@
         out[b + 1] = got[:, width:]
 
 
-def couple_kernel(fields, group, targets, state, received, *rest):
-    surfaces, (out, total, top, sem) = rest[:-4], rest[-4:]
+def couple_kernel(fields, group, state, received, *rest):
+    surfaces, (out, total, top, found, targets, sem) = rest[:-6], rest[-6:]
     del state
-    count, rows, _ = total.shape
+    count, rows, width = total.shape
+    heads = received[:, CAP * rows :, :].astype(F32)
+    found[...] = jnp.sum(heads, axis=0).astype(jnp.int32)
+    copy = pltpu.make_async_copy(found, targets, sem)
+    copy.start()
     total[...] = jnp.zeros(total.shape, F32)
-    for j in range(targets.shape[0]):
-        t = targets[j]
-
-        @pl.when(t >= 0)
+    copy.wait()
+    for j in range(received.shape[0] * CAP):
+        t = targets[j // width, j % width]
+
+        @pl.when(t > 0)
         def _(t=t, j=j):
-            total[t] = total[t] + received[j].astype(F32)
+            at = (j % CAP) * rows
+            total[t - 1] = total[t - 1] + received[j // CAP, at : at + rows, :].astype(F32)
 
     step = rows // len(surfaces)
     picks = [select_matrix(step, fields, group, i * group, True) for i in range(len(surfaces))]
@@ -230,12 +265,15 @@
     w = dyn_weights[0]
     plain = state[0].transpose(0, 2, 1, 3).reshape(count, levels * fields, width)
 
-    kron = (vertical[0][:, None, :, None] * jnp.eye(group, dtype=F32)[None, :, None, :]).reshape(
-        rows, rows
-    )
-    k_hi = lax.reduce_precision(kron, 8, 7)
-    k_lo = (kron - k_hi).astype(BF16)
-    k_hi = k_hi.astype(BF16)
+    k_hi, k_lo = pl.pallas_call(
+        functools.partial(expand_kernel, group),
+        out_shape=[shape_of((rows, rows))] * 2,
+        in_specs=[spec(VMEM)],
+        out_specs=[spec(VMEM)] * 2,
+        compiler_params=params(),
+        cost_estimate=cost(8 * rows * rows * levels, 1024 * 1024),
+        name="expand",
+    )(vertical[0])
 
     dest = remap_dest[0, :, 0]
     hits = (dest[:, None] == jnp.arange(tile_count, dtype=jnp.int32)[None, :]).astype(jnp.int32)
@@ -243,6 +281,25 @@
     slot_of = dest * CAP + rank
     place = jnp.arange(tile_count * CAP, dtype=jnp.int32)[:, None] == slot_of[None, :]
     target_buf = jnp.max(jnp.where(place, remap_target[0][None, :], -1), axis=1)
+
+    entries = remap_source.shape[1]
+    mine = lax.axis_index("tile") * CAP
+    flat = jnp.arange(HEAD * width, dtype=jnp.int32).reshape(1, HEAD, width) - mine
+    header = jnp.zeros((tile_count, HEAD, width), jnp.int32)
+    for i in range(CAP):
+        mark = target_buf.reshape(tile_count, CAP)[:, i][:, None, None] + 1
+        header = jnp.where(flat == i, mark, header)
+    header = header.astype(F32).astype(BF16)
+    held = pl.pallas_call(
+        gather_kernel,
+        out_shape=shape_of((entries, width, width)),
+        in_specs=[spec(SMEM)] * 2 + [spec(HBM)],
+        out_specs=spec(VMEM),
+        scratch_shapes=[pltpu.SemaphoreType.DMA((entries,))],
+        compiler_params=params(),
+        cost_estimate=cost(1024, 1024 * 1024),
+        name="tiles",
+    )(remap_tile[0], (1 - comp).reshape(1), remap_weights)
 
     stages = []
     for s in range(STAGES):
@@ -261,10 +318,8 @@
         before, after, across = exchange(lead, last)
         stages.append((before, lead, last, after, across))
 
-    targets = partner(target_buf, "comp", 0)
-    targets = lax.all_to_all(targets, "tile", split_axis=0, concat_axis=0, tiled=True)
     tables = (neighbor_slots[0].reshape(-1), neighbor_tiles[0].reshape(-1))
-    tables, targets = lax.optimization_barrier((tables, targets))
+    tables, held, header, slot_of = lax.optimization_barrier((tables, held, header, slot_of))
 
     for step in range(STEPS - 1):
         moved = []
@@ -277,25 +332,19 @@
     bodies = [e[0] for e in ended]
     surfaces = [e[1] for e in ended]
 
-    entries = remap_source.shape[1]
     surface = SURF * fields
     payload = pl.pallas_call(
         partial_kernel,
-        out_shape=shape_of((tile_count * CAP, surface, width)),
-        in_specs=[spec(SMEM)] * 4 + [spec(HBM)] + [spec(VMEM)] * STAGES,
+        out_shape=shape_of((tile_count, CAP * surface + HEAD, width)),
+        in_specs=[spec(SMEM)] * 2 + [spec(VMEM)] * (2 + STAGES),
         out_specs=spec(VMEM),
-        scratch_shapes=[
-            pltpu.VMEM((entries, width, width), BF16),
-            pltpu.SemaphoreType.DMA((entries,)),
-        ],
         compiler_params=params(),
         cost_estimate=cost(2 * entries * surface * width * width, 2 * 1024 * 1024),
         name="partials",
-    )(remap_source[0], remap_tile[0], slot_of, (1 - comp).reshape(1), remap_weights, *surfaces)
-
-    payload = partner(payload, "comp", 0).reshape(tile_count, CAP * surface, width)
+    )(remap_source[0], slot_of, header, held, *surfaces)
+
+    payload = partner(payload, "comp", 0)
     received = lax.all_to_all(payload, "tile", split_axis=0, concat_axis=0, tiled=True)
-    received = received.reshape(tile_count * CAP, surface, width)
 
     if STAGES == 1:
         whole = bodies[0]
@@ -312,18 +361,20 @@
     final = pl.pallas_call(
         functools.partial(couple_kernel, fields, group),
         out_shape=shape_of(whole.shape),
-        in_specs=[spec(SMEM), spec(HBM), spec(VMEM)] + [spec(VMEM)] * STAGES,
+        in_specs=[spec(HBM), spec(VMEM)] + [spec(VMEM)] * STAGES,
         out_specs=spec(HBM),
-        input_output_aliases={1: 0},
+        input_output_aliases={0: 0},
         scratch_shapes=[
             pltpu.VMEM((count, surface, width), F32),
             pltpu.VMEM((count, surface, width), BF16),
+            pltpu.VMEM((HEAD, width), jnp.int32),
+            pltpu.SMEM((HEAD, width), jnp.int32),
             pltpu.SemaphoreType.DMA,
         ],
         compiler_params=params(),
         cost_estimate=cost(1024, 1024 * 1024),
         name="couple",
-    )(targets, whole, received, *surfaces)
+    )(whole, received, *surfaces)
     return final.reshape(count, levels, fields, width).transpose(0, 2, 1, 3)[None]
 
 

time: 108 us -> 101 us (0.935)
  waiting for transfers between devices: 36.3 us -> 27.7 us
  starting transfers between devices: 34.4 us -> 42.6 us
  local copies, waits for them, and re-layouts: 9.38 us -> 5.67 us
  other arithmetic: 6.21 us -> 3.3 us
    ppermute x6 -> x5, starting transfers between devices: 2.38 us -> 13.5 us  [partner(): return lax.ppermute(value, axis, pairs)]
    ppermute x4, starting transfers between devices: 22.6 us -> 13.2 us  [exchange(): after = lax.ppermute(lead, 'tile', down)]
    all_to_all x1 -> x0, waiting for transfers between devices: 8.79 us -> none  [on_device(): lax.all_to_all(targets, 'tile', split_axis=0, concat_axis=0, tiled=True)]
    all_to_all x1, starting transfers between devices: 4.47 us -> 10 us  [on_device(): lax.all_to_all(payload, 'tile', split_axis=0, concat_axis=0, tiled=True)]
    ppermute x4, starting transfers between devices: 1.5 us -> 5.9 us  [exchange(): before = lax.ppermute(last, 'tile', up)]
    mul x1 -> x0, local copies, waits for them, and re-layouts: 3.64 us -> none  [on_device(): vertical[0][:, None, :, None] * jnp.eye(group, dtype=F32)[None, :, None, :]]
    all_to_all x1 -> x0, starting transfers between devices: 3.47 us -> none  [on_device(): lax.all_to_all(targets, 'tile', split_axis=0, concat_axis=0, tiled=True)]
    mul x1 -> x0, other arithmetic: 2.52 us -> none  [on_device(): vertical[0][:, None, :, None] * jnp.eye(group, dtype=F32)[None, :, None, :]]
  transfers between devices with their start and end apart: 16 -> 14, of which waited for: 5 -> 5; matrix products, arithmetic and copies ran while one was open for 11% -> 4% of each run, Pallas kernels for 13% -> 14%
where the time goes in v2:
time: 101 us; the launch traced here: 100 us
  starting transfers between devices  42.6 us (42%)
  waiting for transfers between devices  27.7 us (27%)
  Pallas kernels  21 us (21%)
  local copies, waits for them, and re-layouts  5.67 us (6%)
  other arithmetic  3.3 us (3%)
    ppermute x5, waiting for transfers between devices, partner(): return lax.ppermute(value, axis, pairs)  19.4 us
    pallas_call x4, Pallas kernels, run_step(): pl.pallas_call(step_kernel, out_shape=outs, in_specs=[spec(SMEM)] * 2 + [...  13.8 us
    ppermute x5, starting transfers between devices, partner(): return lax.ppermute(value, axis, pairs)  13.5 us
    ppermute x4, starting transfers between devices, exchange(): after = lax.ppermute(lead, 'tile', down)  13.2 us
    all_to_all x1, starting transfers between devices, on_device(): lax.all_to_all(payload, 'tile', split_axis=0, concat_axis=0, tiled=True)  10 us
    all_to_all x1, waiting for transfers between devices, on_device(): lax.all_to_all(payload, 'tile', split_axis=0, concat_axis=0, tiled=True)  8.35 us
    ppermute x4, starting transfers between devices, exchange(): before = lax.ppermute(last, 'tile', up)  5.9 us
    unnamed x23, local copies, waits for them, and re-layouts  5.41 us
  transfers between devices with their start and end apart: 14, of which 5 were waited for; matrix products, arithmetic and copies ran while one was open for 4% of the time, Pallas kernels for 14%

profile of v2, /device:TPU:0, one launch (start us, length us, event | category | flops | bytes accessed | tf_op | source)
XLA Modules:
  0.0 100.5 jit_solution(3385873232325626061)
XLA Ops:
  0.0 1.3 %copy-done.2 = bf16[1,16,4,60,128]{4,2,3,1,0:T(4,128)(2,1)S(1)} copy-done((bf16[1,16,4,60,128]{4,2,3,1,0:T(4,128)(2,1)S(1)}, bf16[1,16,4,60,128]{4,2,3,1,0:T(4,128)(2,1)}, u32[]{:S(2)}) %copy-start.2) | copy-done | bytes 983064
  1.4 1.0 split.3
  2.4 7.0 %collective-permute-start.7 = (bf16[8,120,128]{2,1,0:T(8,128)(2,1)}, bf16[8,120,128]{2,1,0:T(8,128)(2,1)}, u32[]{:S(2)}, u32[]{:S(2)}) collective-permute-start(bf16[8,120,128]{2,1,0:T(8,128)(2,1)} %get-tuple-element.34.lead), channel_id=1, source_target_pairs={{1,0},{2,1},{3,2},{4,3},{5,4},{6,5},{7,6},{8,7},{9,8},{10,9},{11,1... | collective-permute-start | bytes 737288 | tf_op jit(solution)/shard_map/ppermute | solution.py:244
  9.6 0.9 collective-permute-start.1
  10.5 2.1 %collective-permute-start.2 = (bf16[8,120,128]{2,1,0:T(8,128)(2,1)S(1)}, bf16[8,120,128]{2,1,0:T(8,128)(2,1)}, u32[]{:S(2)}, u32[]{:S(2)}) collective-permute-start(bf16[8,120,128]{2,1,0:T(8,128)(2,1)S(1)} %get-tuple-element.27.lead), channel_id=1, source_target_pairs={{0,8},{1,9},{2,10},{3,11},{4,12},{5,13},{6,14},{7,15},{8,0},{9,1},... | collective-permute-start | bytes 737288 | tf_op jit(solution)/shard_map/ppermute | solution.py:235
  12.7 1.9 %collective-permute-start.6 = (bf16[8,120,128]{2,1,0:T(8,128)(2,1)}, bf16[8,120,128]{2,1,0:T(8,128)(2,1)}, u32[]{:S(2)}, u32[]{:S(2)}) collective-permute-start(bf16[8,120,128]{2,1,0:T(8,128)(2,1)} %get-tuple-element.33.last), channel_id=1, source_target_pairs={{0,1},{1,2},{2,3},{3,4},{4,5},{5,6},{6,7},{7,8},{8,9},{9,10},{10,1... | collective-permute-start | bytes 737288 | tf_op jit(solution)/shard_map/ppermute | solution.py:243
  14.6 0.7 fusion.2
  15.4 0.8 select_reduce_fusion.1
  16.2 0.7 multiply_add_fusion.slot
  16.9 0.7 select_reduce_fusion
  17.9 2.2 %copy-done.1 = bf16[2,64,128,128]{3,2,1,0:T(8,128)(2,1)S(1)} copy-done((bf16[2,64,128,128]{3,2,1,0:T(8,128)(2,1)S(1)}, bf16[2,64,128,128]{3,2,1,0:T(8,128)(2,1)}, u32[]{:S(2)}) %copy-start.1) | copy-done | bytes 4194328
  20.8 1.4 %tiles.1.held = bf16[16,128,128]{2,1,0:T(8,128)(2,1)S(1)} custom-call(s32[16]{0:T(128)S(1)} %bitcast.27, s32[1]{0:T(128)} %bitcast.1.comp, bf16[2,64,128,128]{3,2,1,0:T(8,128)(2,1)S(1)} %copy-done.1), custom_call_target="tpu_custom_call" | custom-call | flops 1024 | bytes 1048576 | tf_op jit(solution)/shard_map/tiles/pallas_call | solution.py:293
  23.0 4.5 %collective-permute-done.8.across = bf16[8,120,128]{2,1,0:T(8,128)(2,1)} collective-permute-done((bf16[8,120,128]{2,1,0:T(8,128)(2,1)}, bf16[8,120,128]{2,1,0:T(8,128)(2,1)}, u32[]{:S(2)}, u32[]{:S(2)}) %collective-permute-start.8) | collective-permute-done | bytes 245792 | tf_op jit(solution)/shard_map/ppermute | solution.py:235
  27.6 3.1 %substep.6 = (bf16[8,120,128]{2,1,0:T(8,128)(2,1)S(1)}, bf16[8,120,128]{2,1,0:T(8,128)(2,1)S(1)}) custom-call(s32[64]{0:T(128)S(1)} %reshape_squeeze.6.slots, s32[64]{0:T(128)S(1)} %reshape_squeeze.7.tiles, bf16[8,120,128]{2,1,0:T(8,128)(2,1)} %collective-permute-done.6.before, bf16[8,120,128]{2,1,0:T(8,128)(2,1)} %get-tuple-element.34.lead, ...), custom_call_target="tpu_custom_call" | custom-call | flops 251658240 | bytes 8388608 | tf_op jit(solution)/shard_map/substep/pallas_call | solution.py:149
  30.7 1.6 %collective-permute-start.10 = (bf16[8,120,128]{2,1,0:T(8,128)(2,1)S(1)}, bf16[8,120,128]{2,1,0:T(8,128)(2,1)S(1)}, u32[]{:S(2)}, u32[]{:S(2)}) collective-permute-start(bf16[8,120,128]{2,1,0:T(8,128)(2,1)S(1)} %get-tuple-element.36.lead), channel_id=1, source_target_pairs={{1,0},{2,1},{3,2},{4,3},{5,4},{6,5},{7,6},{8,7},{9,8},{10,9},{11,1... | collective-permute-start | bytes 737288 | tf_op jit(solution)/shard_map/ppermute | solution.py:244
  32.3 9.6 %collective-permute-start.11 = (bf16[8,120,128]{2,1,0:T(8,128)(2,1)S(1)}, bf16[8,120,128]{2,1,0:T(8,128)(2,1)S(1)}, u32[]{:S(2)}, u32[]{:S(2)}) collective-permute-start(bf16[8,120,128]{2,1,0:T(8,128)(2,1)S(1)} %get-tuple-element.36.lead), channel_id=1, source_target_pairs={{0,8},{1,9},{2,10},{3,11},{4,12},{5,13},{6,14},{7,15},{8,0},{9,1},... | collective-permute-start | bytes 737288 | tf_op jit(solution)/shard_map/ppermute | solution.py:235
  42.0 1.9 %collective-permute-start.9 = (bf16[8,120,128]{2,1,0:T(8,128)(2,1)S(1)}, bf16[8,120,128]{2,1,0:T(8,128)(2,1)S(1)}, u32[]{:S(2)}, u32[]{:S(2)}) collective-permute-start(bf16[8,120,128]{2,1,0:T(8,128)(2,1)S(1)} %get-tuple-element.35.last), channel_id=1, source_target_pairs={{0,1},{1,2},{2,3},{3,4},{4,5},{5,6},{6,7},{7,8},{8,9},{9,10},{10,1... | collective-permute-start | bytes 737288 | tf_op jit(solution)/shard_map/ppermute | solution.py:243
  43.9 4.0 %substep.4 = (bf16[8,120,128]{2,1,0:T(8,128)(2,1)S(1)}, bf16[8,120,128]{2,1,0:T(8,128)(2,1)S(1)}) custom-call(s32[64]{0:T(128)S(1)} %reshape_squeeze.6.slots, s32[64]{0:T(128)S(1)} %reshape_squeeze.7.tiles, bf16[8,120,128]{2,1,0:T(8,128)(2,1)S(1)} %collective-permute-done.before, bf16[8,120,128]{2,1,0:T(8,128)(2,1)S(1)} %get-tuple-element.27.lead, ...), custom_call_target="tpu_custom_call" | custom-call | flops 251658240 | bytes 8388608 | tf_op jit(solution)/shard_map/substep/pallas_call | solution.py:149
  47.9 3.7 %collective-permute-start.4 = (bf16[8,120,128]{2,1,0:T(8,128)(2,1)S(1)}, bf16[8,120,128]{2,1,0:T(8,128)(2,1)S(1)}, u32[]{:S(2)}, u32[]{:S(2)}) collective-permute-start(bf16[8,120,128]{2,1,0:T(8,128)(2,1)S(1)} %get-tuple-element.31.lead), channel_id=1, source_target_pairs={{1,0},{2,1},{3,2},{4,3},{5,4},{6,5},{7,6},{8,7},{9,8},{10,9},{11,1... | collective-permute-start | bytes 737288 | tf_op jit(solution)/shard_map/ppermute | solution.py:244
  51.6 1.6 %collective-permute-start.5 = (bf16[8,120,128]{2,1,0:T(8,128)(2,1)S(1)}, bf16[8,120,128]{2,1,0:T(8,128)(2,1)S(1)}, u32[]{:S(2)}, u32[]{:S(2)}) collective-permute-start(bf16[8,120,128]{2,1,0:T(8,128)(2,1)S(1)} %get-tuple-element.31.lead), channel_id=1, source_target_pairs={{0,8},{1,9},{2,10},{3,11},{4,12},{5,13},{6,14},{7,15},{8,0},{9,1},... | collective-permute-start | bytes 737288 | tf_op jit(solution)/shard_map/ppermute | solution.py:235
  53.3 1.9 %collective-permute-start.3 = (bf16[8,120,128]{2,1,0:T(8,128)(2,1)S(1)}, bf16[8,120,128]{2,1,0:T(8,128)(2,1)S(1)}, u32[]{:S(2)}, u32[]{:S(2)}) collective-permute-start(bf16[8,120,128]{2,1,0:T(8,128)(2,1)S(1)} %get-tuple-element.30.last), channel_id=1, source_target_pairs={{0,1},{1,2},{2,3},{3,4},{4,5},{5,6},{6,7},{7,8},{8,9},{9,10},{10,1... | collective-permute-start | bytes 737288 | tf_op jit(solution)/shard_map/ppermute | solution.py:243
  55.2 3.9 %collective-permute-done.11.across = bf16[8,120,128]{2,1,0:T(8,128)(2,1)S(1)} collective-permute-done((bf16[8,120,128]{2,1,0:T(8,128)(2,1)S(1)}, bf16[8,120,128]{2,1,0:T(8,128)(2,1)S(1)}, u32[]{:S(2)}, u32[]{:S(2)}) %collective-permute-start.11) | collective-permute-done | bytes 245792 | tf_op jit(solution)/shard_map/ppermute | solution.py:235
  59.2 3.3 %substep.7 = (bf16[16,120,128]{2,1,0:T(8,128)(2,1)S(1)}, bf16[16,16,128]{2,1,0:T(8,128)(2,1)S(1)}) custom-call(s32[64]{0:T(128)S(1)} %reshape_squeeze.6.slots, s32[64]{0:T(128)S(1)} %reshape_squeeze.7.tiles, bf16[8,120,128]{2,1,0:T(8,128)(2,1)S(1)} %collective-permute-done.9.before, bf16[8,120,128]{2,1,0:T(8,128)(2,1)S(1)} %get-tuple-element.36.lead, ...), custom_call_target="tpu_custom_call" | custom-call | flops 251658240 | bytes 8388608 | tf_op jit(solution)/shard_map/substep/pallas_call | solution.py:149
  62.5 9.2 %collective-permute-done.5.across = bf16[8,120,128]{2,1,0:T(8,128)(2,1)S(1)} collective-permute-done((bf16[8,120,128]{2,1,0:T(8,128)(2,1)S(1)}, bf16[8,120,128]{2,1,0:T(8,128)(2,1)S(1)}, u32[]{:S(2)}, u32[]{:S(2)}) %collective-permute-start.5) | collective-permute-done | bytes 245792 | tf_op jit(solution)/shard_map/ppermute | solution.py:235
  71.8 3.4 %substep.5 = (bf16[16,120,128]{2,1,0:T(8,128)(2,1)S(1)}, bf16[16,16,128]{2,1,0:T(8,128)(2,1)S(1)}) custom-call(s32[64]{0:T(128)S(1)} %reshape_squeeze.6.slots, s32[64]{0:T(128)S(1)} %reshape_squeeze.7.tiles, bf16[8,120,128]{2,1,0:T(8,128)(2,1)S(1)} %collective-permute-done.3.before, bf16[8,120,128]{2,1,0:T(8,128)(2,1)S(1)} %get-tuple-element.31.lead, ...), custom_call_target="tpu_custom_call" | custom-call | flops 251658240 | bytes 8388608 | tf_op jit(solution)/shard_map/substep/pallas_call | solution.py:149
  75.1 0.8 partials.1
  76.0 1.7 %collective-permute-done.12 = bf16[16,72,128]{2,1,0:T(8,128)(2,1)} collective-permute-done((bf16[16,72,128]{2,1,0:T(8,128)(2,1)S(1)}, bf16[16,72,128]{2,1,0:T(8,128)(2,1)}, u32[]{:S(2)}, u32[]{:S(2)}) %collective-permute-start.12) | collective-permute-done | bytes 294944 | tf_op jit(solution)/shard_map/ppermute | solution.py:235
  77.7 10.0 %all-to-all-start = ((bf16[16,72,128]{2,1,0:T(8,128)(2,1)}), bf16[16,72,128]{2,1,0:T(8,128)(2,1)S(1)}, u32[]{:S(2)}, u32[]{:S(2)}) async-start(bf16[16,72,128]{2,1,0:T(8,128)(2,1)} %collective-permute-done.12), calls=%async_computation | async-start | bytes 589824 | tf_op jit(solution)/shard_map/all_to_all | solution.py:347
  87.8 1.0 %copy-done.4 = bf16[16,120,128]{2,1,0:T(8,128)(2,1)S(1)} copy-done((bf16[16,120,128]{2,1,0:T(8,128)(2,1)S(1)}, bf16[16,120,128]{2,1,0:T(8,128)(2,1)}, u32[]{:S(2)}) %copy-start.4) | copy-done | bytes 491544
  88.8 1.6 %merge.1.state = bf16[16,240,128]{2,1,0:T(8,128)(2,1)} custom-call(bf16[16,120,128]{2,1,0:T(8,128)(2,1)S(1)} %copy-done.4, bf16[16,120,128]{2,1,0:T(8,128)(2,1)S(1)} %get-tuple-element.37.refs_1_), custom_call_target="tpu_custom_call" | custom-call | flops 58982400 | bytes 2097152 | tf_op jit(solution)/shard_map/merge/pallas_call | solution.py:352
  90.4 8.3 %all-to-all-done.received = bf16[16,72,128]{2,1,0:T(8,128)(2,1)S(1)} async-done(((bf16[16,72,128]{2,1,0:T(8,128)(2,1)}), bf16[16,72,128]{2,1,0:T(8,128)(2,1)S(1)}, u32[]{:S(2)}, u32[]{:S(2)}) %all-to-all-start) | async-done | bytes 294944 | tf_op jit(solution)/shard_map/all_to_all | solution.py:347
  98.7 1.8 %couple.1 = bf16[16,240,128]{2,1,0:T(8,128)(2,1)} custom-call(bf16[16,240,128]{2,1,0:T(8,128)(2,1)} %merge.1.state, bf16[16,72,128]{2,1,0:T(8,128)(2,1)S(1)} %all-to-all-done.received, bf16[16,16,128]{2,1,0:T(8,128)(2,1)S(1)} %get-tuple-element.41.rest_0_, bf16[16,16,128]{2,1,0:T(8,128)(2,1)S(1)} %get-tuple-element.42.rest_1_), custom_call_target="tpu_custom_call", output_to_operand_aliasing={{}: (0, {})} | custom-call | flops 1024 | bytes 1048576 | tf_op jit(solution)/shard_map/couple/pallas_call | solution.py:361
  (41 shorter events, 2.2 us)
Async XLA Ops:
  0.0 27.6 %copy-start = (bf16[1,64,128,128]{3,2,1,0:T(8,128)(2,1)S(1)}, bf16[1,64,128,128]{3,2,1,0:T(8,128)(2,1)}, u32[]{:S(2)}) copy-start(bf16[1,64,128,128]{3,2,1,0:T(8,128)(2,1)} %param.11) | copy-start | bytes 6291460
  0.0 1.4 %copy-start.2 = (bf16[1,16,4,60,128]{4,2,3,1,0:T(4,128)(2,1)S(1)}, bf16[1,16,4,60,128]{4,2,3,1,0:T(4,128)(2,1)}, u32[]{:S(2)}) copy-start(bf16[1,16,4,60,128]{4,2,3,1,0:T(4,128)(2,1)} %param.10) | copy-start | bytes 2949124
  2.4 20.6 %collective-permute-start.7 = (bf16[8,120,128]{2,1,0:T(8,128)(2,1)}, bf16[8,120,128]{2,1,0:T(8,128)(2,1)}, u32[]{:S(2)}, u32[]{:S(2)}) collective-permute-start(bf16[8,120,128]{2,1,0:T(8,128)(2,1)} %get-tuple-element.34.lead), channel_id=1, source_target_pairs={{1,0},{2,1},{3,2},{4,3},{5,4},{6,5},{7,6},{8,7},{9,8},{10,9},{11,1... | collective-permute-start | bytes 737288 | tf_op jit(solution)/shard_map/ppermute | solution.py:244
  9.3 18.2 %collective-permute-start.8 = (bf16[8,120,128]{2,1,0:T(8,128)(2,1)}, bf16[8,120,128]{2,1,0:T(8,128)(2,1)}, u32[]{:S(2)}, u32[]{:S(2)}) collective-permute-start(bf16[8,120,128]{2,1,0:T(8,128)(2,1)} %get-tuple-element.34.lead), channel_id=1, source_target_pairs={{0,8},{1,9},{2,10},{3,11},{4,12},{5,13},{6,14},{7,15},{8,0},{9,1},... | collective-permute-start | bytes 737288 | tf_op jit(solution)/shard_map/ppermute | solution.py:235
  9.6 32.3 %collective-permute-start.1 = (bf16[8,120,128]{2,1,0:T(8,128)(2,1)S(1)}, bf16[8,120,128]{2,1,0:T(8,128)(2,1)S(1)}, u32[]{:S(2)}, u32[]{:S(2)}) collective-permute-start(bf16[8,120,128]{2,1,0:T(8,128)(2,1)S(1)} %get-tuple-element.27.lead), channel_id=1, source_target_pairs={{1,0},{2,1},{3,2},{4,3},{5,4},{6,5},{7,6},{8,7},{9,8},{10,9},{11,1... | collective-permute-start | bytes 737288 | tf_op jit(solution)/shard_map/ppermute | solution.py:244
  10.5 33.4 %collective-permute-start.2 = (bf16[8,120,128]{2,1,0:T(8,128)(2,1)S(1)}, bf16[8,120,128]{2,1,0:T(8,128)(2,1)}, u32[]{:S(2)}, u32[]{:S(2)}) collective-permute-start(bf16[8,120,128]{2,1,0:T(8,128)(2,1)S(1)} %get-tuple-element.27.lead), channel_id=1, source_target_pairs={{0,8},{1,9},{2,10},{3,11},{4,12},{5,13},{6,14},{7,15},{8,0},{9,1},... | collective-permute-start | bytes 737288 | tf_op jit(solution)/shard_map/ppermute | solution.py:235
  12.7 14.9 %collective-permute-start.6 = (bf16[8,120,128]{2,1,0:T(8,128)(2,1)}, bf16[8,120,128]{2,1,0:T(8,128)(2,1)}, u32[]{:S(2)}, u32[]{:S(2)}) collective-permute-start(bf16[8,120,128]{2,1,0:T(8,128)(2,1)} %get-tuple-element.33.last), channel_id=1, source_target_pairs={{0,1},{1,2},{2,3},{3,4},{4,5},{5,6},{6,7},{7,8},{8,9},{9,10},{10,1... | collective-permute-start | bytes 737288 | tf_op jit(solution)/shard_map/ppermute | solution.py:243
  17.9 2.2 %copy-start.1 = (bf16[2,64,128,128]{3,2,1,0:T(8,128)(2,1)S(1)}, bf16[2,64,128,128]{3,2,1,0:T(8,128)(2,1)}, u32[]{:S(2)}) copy-start(bf16[2,64,128,128]{3,2,1,0:T(8,128)(2,1)} %weights.1) | copy-start | bytes 12582916
  20.1 0.7 copy-start.5
  20.8 1.4 %copy-start.8 = (s32[1,16,4]{1,2,0:T(4,128)S(1)}, s32[1,16,4]{1,2,0:T(4,128)}, u32[]{:S(2)}) copy-start(s32[1,16,4]{1,2,0:T(4,128)} %param.14) | copy-start | bytes 772
  20.8 1.6 %copy-start.9 = (s32[1,16,4]{1,2,0:T(4,128)S(1)}, s32[1,16,4]{1,2,0:T(4,128)}, u32[]{:S(2)}) copy-start(s32[1,16,4]{1,2,0:T(4,128)} %param.15) | copy-start | bytes 772
  20.8 1.9 %copy-start.7 = (f32[1,60,60]{2,0,1:T(1,128)S(1)}, f32[1,60,60]{2,0,1:T(1,128)}, u32[]{:S(2)}) copy-start(f32[1,60,60]{2,0,1:T(1,128)} %param.12) | copy-start | bytes 43204
  23.0 20.9 %collective-permute-start = (bf16[8,120,128]{2,1,0:T(8,128)(2,1)S(1)}, bf16[8,120,128]{2,1,0:T(8,128)(2,1)S(1)}, u32[]{:S(2)}, u32[]{:S(2)}) collective-permute-start(bf16[8,120,128]{2,1,0:T(8,128)(2,1)S(1)} %get-tuple-element.26.last), channel_id=1, source_target_pairs={{0,1},{1,2},{2,3},{3,4},{4,5},{5,6},{6,7},{7,8},{8,9},{9,10},{10,1... | collective-permute-start | bytes 737288 | tf_op jit(solution)/shard_map/ppermute | solution.py:243
  30.7 22.6 %collective-permute-start.10 = (bf16[8,120,128]{2,1,0:T(8,128)(2,1)S(1)}, bf16[8,120,128]{2,1,0:T(8,128)(2,1)S(1)}, u32[]{:S(2)}, u32[]{:S(2)}) collective-permute-start(bf16[8,120,128]{2,1,0:T(8,128)(2,1)S(1)} %get-tuple-element.36.lead), channel_id=1, source_target_pairs={{1,0},{2,1},{3,2},{4,3},{5,4},{6,5},{7,6},{8,7},{9,8},{10,9},{11,1... | collective-permute-start | bytes 737288 | tf_op jit(solution)/shard_map/ppermute | solution.py:244
  32.3 26.8 %collective-permute-start.11 = (bf16[8,120,128]{2,1,0:T(8,128)(2,1)S(1)}, bf16[8,120,128]{2,1,0:T(8,128)(2,1)S(1)}, u32[]{:S(2)}, u32[]{:S(2)}) collective-permute-start(bf16[8,120,128]{2,1,0:T(8,128)(2,1)S(1)} %get-tuple-element.36.lead), channel_id=1, source_target_pairs={{0,8},{1,9},{2,10},{3,11},{4,12},{5,13},{6,14},{7,15},{8,0},{9,1},... | collective-permute-start | bytes 737288 | tf_op jit(solution)/shard_map/ppermute | solution.py:235
  42.0 17.2 %collective-permute-start.9 = (bf16[8,120,128]{2,1,0:T(8,128)(2,1)S(1)}, bf16[8,120,128]{2,1,0:T(8,128)(2,1)S(1)}, u32[]{:S(2)}, u32[]{:S(2)}) collective-permute-start(bf16[8,120,128]{2,1,0:T(8,128)(2,1)S(1)} %get-tuple-element.35.last), channel_id=1, source_target_pairs={{0,1},{1,2},{2,3},{3,4},{4,5},{5,6},{6,7},{7,8},{8,9},{9,10},{10,1... | collective-permute-start | bytes 737288 | tf_op jit(solution)/shard_map/ppermute | solution.py:243
  47.9 27.2 %copy-start.6 = (s32[1,16]{1,0:T(1,128)S(1)}, s32[1,16]{1,0:T(1,128)}, u32[]{:S(2)}) copy-start(s32[1,16]{1,0:T(1,128)} %param.16) | copy-start | bytes 196
  47.9 14.6 %collective-permute-start.4 = (bf16[8,120,128]{2,1,0:T(8,128)(2,1)S(1)}, bf16[8,120,128]{2,1,0:T(8,128)(2,1)S(1)}, u32[]{:S(2)}, u32[]{:S(2)}) collective-permute-start(bf16[8,120,128]{2,1,0:T(8,128)(2,1)S(1)} %get-tuple-element.31.lead), channel_id=1, source_target_pairs={{1,0},{2,1},{3,2},{4,3},{5,4},{6,5},{7,6},{8,7},{9,8},{10,9},{11,1... | collective-permute-start | bytes 737288 | tf_op jit(solution)/shard_map/ppermute | solution.py:244
  51.6 20.1 %collective-permute-start.5 = (bf16[8,120,128]{2,1,0:T(8,128)(2,1)S(1)}, bf16[8,120,128]{2,1,0:T(8,128)(2,1)S(1)}, u32[]{:S(2)}, u32[]{:S(2)}) collective-permute-start(bf16[8,120,128]{2,1,0:T(8,128)(2,1)S(1)} %get-tuple-element.31.lead), channel_id=1, source_target_pairs={{0,8},{1,9},{2,10},{3,11},{4,12},{5,13},{6,14},{7,15},{8,0},{9,1},... | collective-permute-start | bytes 737288 | tf_op jit(solution)/shard_map/ppermute | solution.py:235
  53.3 18.5 %collective-permute-start.3 = (bf16[8,120,128]{2,1,0:T(8,128)(2,1)S(1)}, bf16[8,120,128]{2,1,0:T(8,128)(2,1)S(1)}, u32[]{:S(2)}, u32[]{:S(2)}) collective-permute-start(bf16[8,120,128]{2,1,0:T(8,128)(2,1)S(1)} %get-tuple-element.30.last), channel_id=1, source_target_pairs={{0,1},{1,2},{2,3},{3,4},{4,5},{5,6},{6,7},{7,8},{8,9},{9,10},{10,1... | collective-permute-start | bytes 737288 | tf_op jit(solution)/shard_map/ppermute | solution.py:243
  75.1 0.8 copy-start.3
  75.9 1.8 %collective-permute-start.12 = (bf16[16,72,128]{2,1,0:T(8,128)(2,1)S(1)}, bf16[16,72,128]{2,1,0:T(8,128)(2,1)}, u32[]{:S(2)}, u32[]{:S(2)}) collective-permute-start(bf16[16,72,128]{2,1,0:T(8,128)(2,1)S(1)} %partials.1), channel_id=1, source_target_pairs={{0,16},{16,0},{1,17},{17,1},{2,18},{18,2},{3,19},{19,3},{4,20},{20... | collective-permute-start | bytes 884744 | tf_op jit(solution)/shard_map/ppermute | solution.py:235
  77.7 21.0 %all-to-all-start = ((bf16[16,72,128]{2,1,0:T(8,128)(2,1)}), bf16[16,72,128]{2,1,0:T(8,128)(2,1)S(1)}, u32[]{:S(2)}, u32[]{:S(2)}) async-start(bf16[16,72,128]{2,1,0:T(8,128)(2,1)} %collective-permute-done.12), calls=%async_computation | async-start | bytes 589824 | tf_op jit(solution)/shard_map/all_to_all | solution.py:347
  87.7 1.0 %copy-start.4 = (bf16[16,120,128]{2,1,0:T(8,128)(2,1)S(1)}, bf16[16,120,128]{2,1,0:T(8,128)(2,1)}, u32[]{:S(2)}) copy-start(bf16[16,120,128]{2,1,0:T(8,128)(2,1)} %copy-done.3) | copy-start | bytes 1474564

commit v3 on v0

v3 whole, which is shorter than its diff:
```python
import functools

import jax
import jax.numpy as jnp
from jax import lax
from jax.experimental import pallas as pl
from jax.experimental.pallas import tpu as pltpu
from jax.sharding import PartitionSpec as P


SURF = 8
HALO = 8
STEPS = 2
CAP = 2
HEAD = 8

VMEM = pltpu.MemorySpace.VMEM
SMEM = pltpu.MemorySpace.SMEM
HBM = pltpu.MemorySpace.HBM
BF16 = jnp.bfloat16
F32 = jnp.float32
I32 = jnp.int32


def spec(space):
    return pl.BlockSpec(memory_space=space)


def shape_of(shape, dtype=BF16):
    return jax.ShapeDtypeStruct(shape, dtype)


def params():
    return pltpu.CompilerParams(vmem_limit_bytes=16 * 1024 * 1024)


def cost(flops, moved):
    return pl.CostEstimate(flops=flops, bytes_accessed=moved, transcendentals=0)


def select_matrix(rows, wide, fields, group, first, inverse):
    shape = (wide, rows) if inverse else (rows, wide)
    mine = lax.broadcasted_iota(I32, shape, 1 if inverse else 0)
    other = lax.broadcasted_iota(I32, shape, 0 if inverse else 1)
    source = (mine // group) * fields + first + mine % group
    return jnp.where(source == other, 1.0, 0.0).astype(BF16)


def expand_kernel(group, v, k_hi, k_lo):
    rows, levels = k_hi.shape[0], v.shape[0]
    shape = (rows, levels)
    level = lax.broadcasted_iota(I32, shape, 0) // group
    spread = jnp.where(level == lax.broadcasted_iota(I32, shape, 1), 1.0, 0.0).astype(BF16)
    square = (rows, rows)
    same = (
        lax.broadcasted_iota(I32, square, 0) % group == lax.broadcasted_iota(I32, square, 1) % group
    )
    value = v[...]
    high = value.astype(BF16)
    low = (value - high.astype(F32)).astype(BF16)
    for part, out in ((high, k_hi), (low, k_lo)):
        tall = jnp.dot(spread, part, preferred_element_type=F32).astype(BF16)
        full = lax.dot_general(tall, spread, (((1,), (1,)), ((), ())), preferred_element_type=F32)
        out[...] = jnp.where(same, full, 0.0).astype(BF16)


def table_kernel(slots, tiles, *rest):
    singles, table = rest[:-1], rest[-1]
    at = 0
    for src in (slots, tiles, *singles):
        for i in range(src.shape[0]):
            for j in range(src.shape[1]):
                table[at] = src[i, j]
                at += 1


def route_kernel(size, entries, ids, own, far, weights, held, slot, header, marks, taken, sem):
    peers = header.shape[0]
    copies = []
    for x, table in enumerate((own, far)):
        for e in range(entries):
            src = weights.at[1 - ids[1], table[2 * size + entries + e]]
            copies.append(pltpu.make_async_copy(src, held.at[x * entries + e], sem.at[x * entries + e]))
    for c in copies:
        c.start()
    for x, table in enumerate((own, far)):
        for p in range(peers):
            taken[p] = 0
            for i in range(CAP):
                marks[p * 2 * CAP + x * CAP + i] = 0
        for e in range(entries):
            dest = table[2 * size + 2 * entries + e]
            rank = taken[dest]
            taken[dest] = rank + 1
            slot[x * entries + e] = dest * CAP + rank
            marks[dest * 2 * CAP + x * CAP + rank] = table[2 * size + 3 * entries + e] + 1
    shape = header.shape[1:]
    flat = lax.broadcasted_iota(I32, shape, 0) * shape[1] + lax.broadcasted_iota(I32, shape, 1)
    flat = flat - ids[0] * 2 * CAP
    for p in range(peers):
        value = jnp.zeros(shape, I32)
        for i in range(2 * CAP):
            value = jnp.where(flat == i, marks[p * 2 * CAP + i], value)
        header[p] = value.astype(F32).astype(BF16)
    for c in copies:
        c.wait()


def far_fields(near_group, far_group, ring, ids):
    is_low = jnp.where(ids[0] < ring, 1, 0)
    return near_group + is_low * far_group, near_group + (1 - is_low) * far_group


def split_kernel(fields, near_group, far_group, ring, ids, x, lead, last, sent, kept):
    half, rows, width = lead.shape
    wide = x.shape[1]
    near = select_matrix(rows, wide, fields, near_group, 0, False)
    first = far_fields(near_group, far_group, ring, ids)
    far = [select_matrix(sent.shape[1], wide, fields, far_group, f, False) for f in first]
    for b in range(0, x.shape[0], 2):
        pair = jnp.concatenate([x[b], x[b + 1]], axis=1)
        for pick, outs in zip((near, *far), ((lead, last), (sent,), (kept,))):
            got = jnp.dot(pick, pair, preferred_element_type=F32).astype(BF16)
            for i in range(2):
                dst, at = (outs[0], b + i) if b + i < outs[0].shape[0] else (outs[1], b + i - half)
                dst[at] = got[:, i * width : (i + 1) * width]


def pack_kernel(mine, other, leads, lasts):
    half = leads.shape[0] // 2
    for i, src in enumerate((mine, other)):
        leads[pl.ds(i * half, half)] = src[pl.ds(0, half)]
        lasts[pl.ds(i * half, half)] = src[pl.ds(half, half)]


def far_index(slot, x, at, ring, count):
    side_before = jnp.where(at == 0, 1 - x, x)
    side_after = jnp.where(at == ring - 1, 1 - x, x)
    inner = slot - HALO
    later = inner - count
    home = jnp.where(inner < HALO, x * HALO + inner, HALO + x * HALO + inner)
    beyond = jnp.where(
        later < HALO, 3 * count + side_after * HALO + later, (1 - x) * HALO + later - HALO
    )
    inside = jnp.where(inner < count, home, beyond)
    return jnp.where(inner < 0, 2 * count + side_before * HALO + slot, inside)


def step_kernel(pieces, size, ring, own_at, writes, ids, own, far, *refs):
    sources, (w, k_hi, k_lo) = refs[:pieces], refs[pieces : pieces + 3]
    outs, (pool, mid, hi, lo) = refs[pieces + 3 : -4], refs[-4:]
    at = 0
    for src in sources:
        n = src.shape[0]
        pool[pl.ds(at, n)] = src[...]
        at += n
    count = len(own_at)
    stride = count // 2 if ring else count
    width = w.shape[1]
    for b in range(count):
        total = pool[own_at[b]].astype(F32)
        x, table = b // stride, far if b >= stride else own
        entries = range(b % stride, size, stride)
        where = [table[e] for e in entries]
        if ring:
            where = [far_index(slot, x, ids[0] % ring, ring, stride) for slot in where]
        what = [table[size + e] for e in entries]
        for k in range(0, len(what), 2):
            lhs = jnp.concatenate([pool[where[k]], pool[where[k + 1]]], axis=1)
            rhs = jnp.concatenate([w[what[k]], w[what[k + 1]]], axis=0)
            total = total + jnp.dot(lhs, rhs, preferred_element_type=F32)
        lanes = slice(b * width, (b + 1) * width)
        mid[:, lanes] = total
        top = total.astype(BF16)
        hi[:, lanes] = top
        lo[:, lanes] = (total - top.astype(F32)).astype(BF16)
    big, small = k_hi[...], k_lo[...]
    for b in range(0, count, 2):
        lanes = slice(b * width, (b + 2) * width)
        mixed = jnp.dot(big, hi[:, lanes], preferred_element_type=F32)
        mixed = mixed + jnp.dot(big, lo[:, lanes], preferred_element_type=F32)
        mixed = mixed + jnp.dot(small, hi[:, lanes], preferred_element_type=F32)
        new = (mid[:, lanes] + jnp.tanh(mixed)).astype(BF16)
        for i in range(2):
            for out, place, rows in writes[b + i]:
                outs[out][place] = new[:rows, i * width : (i + 1) * width]


def run_step(size, ring, tables, pieces, w, k, own_at, outs, writes):
    _, rows, width = pieces[0].shape
    count = len(own_at)
    total = sum(p.shape[0] for p in pieces)
    return pl.pallas_call(
        functools.partial(step_kernel, len(pieces), size, ring, own_at, writes),
        out_shape=[shape_of(o) for o in outs],
        in_specs=[spec(SMEM)] * 3 + [spec(VMEM)] * len(pieces) + [spec(VMEM)] * 3,
        out_specs=[spec(VMEM)] * len(outs),
        scratch_shapes=[
            pltpu.VMEM((total, rows, width), BF16),
            pltpu.VMEM((rows, count * width), F32),
            pltpu.VMEM((rows, count * width), BF16),
            pltpu.VMEM((rows, count * width), BF16),
        ],
        compiler_params=params(),
        cost_estimate=cost(4 * 2 * count * rows * width * width, 8 * 1024 * 1024),
    )(*tables, *pieces, w, *k)


def partial_kernel(size, own, far, slot, header, held, near, mine, other, payload):
    entries = slot.shape[0] // 2
    wide = (near.shape[1] + mine.shape[1]) // 8
    thin = other.shape[1] // 8
    payload[...] = jnp.zeros(payload.shape, payload.dtype)
    payload[:, payload.shape[1] - HEAD // 8] = header[...]
    for e in range(2 * entries):
        src = (own if e < entries else far)[2 * size + e % entries]
        groups, base = thin, CAP * wide
        if e < entries:
            rows, groups, base = jnp.concatenate([near[src], mine[src]], axis=0), wide, 0
        else:
            rows = other[src]
        value = jnp.dot(rows, held[e], preferred_element_type=F32)
        value = value.reshape(groups, 8, value.shape[1]).astype(BF16)
        payload[slot[e] // CAP, pl.ds(base + (slot[e] % CAP) * groups, groups)] = value


def merge_kernel(fields, near_group, far_group, ring, ids, near, mine, other, out):
    _, wide, width = out.shape
    first = far_fields(near_group, far_group, ring, ids)
    picks = [
        select_matrix(near.shape[1], wide, fields, near_group, 0, True),
        select_matrix(mine.shape[1], wide, fields, far_group, first[1], True),
        select_matrix(mine.shape[1], wide, fields, far_group, first[0], True),
    ]
    for b in range(0, out.shape[0], 2):
        got = None
        for pick, s in zip(picks, (near, mine, other)):
            pair = jnp.concatenate([s[b], s[b + 1]], axis=1)
            part = jnp.dot(pick, pair, preferred_element_type=F32)
            got = part if got is None else got + part
        got = got.astype(BF16)
        out[b] = got[:, :width]
        out[b + 1] = got[:, width:]


def couple_kernel(
    fields, near_group, far_group, ids, state, received, near, mine, other, out, *scratch
):
    total, top, found, targets, sem = scratch
    del state
    count, rows, width = top.shape
    peers = received.shape[0]
    close, far = near.shape[1], mine.shape[1]
    wide, thin = (close + far) // 8, far // 8
    heads = received[:, received.shape[1] - HEAD // 8].astype(F32)
    found[...] = jnp.sum(heads, axis=0).astype(I32)
    copy = pltpu.make_async_copy(found, targets, sem)
    copy.start()
    total[...] = jnp.zeros(total.shape, F32)
    copy.wait()
    for p in range(peers):
        side = close if p < peers // 2 else close + far
        for i in range(2 * CAP):
            q = p * 2 * CAP + i
            t = targets[q // width, q % width]
            if i < CAP:
                got = received[p, i * wide : (i + 1) * wide].astype(F32)
                got = got.reshape(close + far, width)
                total[t, :close] = total[t, :close] + got[:close]
                total[t, side : side + far] = total[t, side : side + far] + got[close:]
            else:
                at = CAP * wide + (i - CAP) * thin
                got = received[p, at : at + thin].astype(F32).reshape(far, width)
                total[t, side : side + far] = total[t, side : side + far] + got
    shape = (rows, rows)
    have = lax.broadcasted_iota(I32, shape, 1)
    a, b = have - close, have - close - far
    want = jnp.where(
        have < close,
        (have // near_group) * fields + have % near_group,
        jnp.where(
            have < close + far,
            (a // far_group) * fields + near_group + a % far_group,
            (b // far_group) * fields + near_group + far_group + b % far_group,
        ),
    )
    pick = jnp.where(want == lax.broadcasted_iota(I32, shape, 0), 1.0, 0.0).astype(BF16)
    is_low = ids[0] < peers // 2
    for g in range(count):
        here = mine[g].astype(F32)
        there = other[g, :far].astype(F32)
        base = jnp.concatenate(
            [near[g].astype(F32), jnp.where(is_low, here, there), jnp.where(is_low, there, here)],
            axis=0,
        )
        new = (base + total[g + 1]).astype(BF16)
        top[g] = jnp.dot(pick, new, preferred_element_type=F32).astype(BF16)
    copy = pltpu.make_async_copy(top, out.at[:, pl.ds(0, rows)], sem)
    copy.start()
    copy.wait()


def partner(value, axis, distance):
    mask = 2**distance
    pairs = [(source, source ^ mask) for source in range(lax.axis_size(axis))]
    return lax.ppermute(value, axis, pairs)


def shift(last, lead, ring):
    peers = lax.axis_size("tile")
    up = [(i, i // ring * ring + (i + 1) % ring) for i in range(peers)]
    down = [(j, i) for i, j in up]
    before = lax.ppermute(last, "tile", up)
    return before, lax.ppermute(lead, "tile", down)


def on_device(
    state,
    dyn_weights,
    vertical,
    remap_weights,
    neighbor_slots,
    neighbor_tiles,
    remap_source,
    remap_target,
    remap_tile,
    remap_dest,
):
    _, count, fields, levels, width = state.shape
    near_group = fields // 2
    far_group = (fields - near_group) // 2
    near_rows = levels * near_group
    far_rows = -(-levels * far_group // 16) * 16
    peers = lax.axis_size("tile")
    ring = peers // 2
    fold_bit = peers.bit_length() - 2
    ids = jnp.stack([lax.axis_index("tile"), lax.axis_index("comp")])
    w = dyn_weights[0]
    plain = state[0].transpose(0, 2, 1, 3).reshape(count, levels * fields, width)

    lead, last, sent, mine = pl.pallas_call(
        functools.partial(split_kernel, fields, near_group, far_group, ring),
        out_shape=[
            shape_of((HALO, near_rows, width)),
            shape_of((count - HALO, near_rows, width)),
            shape_of((count, far_rows, width)),
            shape_of((count, far_rows, width)),
        ],
        in_specs=[spec(SMEM), spec(VMEM)],
        out_specs=[spec(VMEM)] * 4,
        compiler_params=params(),
        cost_estimate=cost(4 * count * near_rows * levels * fields * width, 2 * 1024 * 1024),
        name="split",
    )(ids, plain)
    other = partner(sent, "tile", fold_bit)
    across = partner(lead, "tile", fold_bit)
    before, after = shift(last, lead, peers)

    lists = (neighbor_slots[0].T, neighbor_tiles[0].T, remap_source, remap_tile, remap_dest[:, :, 0], remap_target)
    size, entries = lists[0].size, remap_source.shape[1]
    own_table = pl.pallas_call(
        table_kernel,
        out_shape=shape_of((2 * size + 4 * entries,), I32),
        in_specs=[spec(SMEM)] * len(lists),
        out_specs=spec(SMEM),
        name="table",
    )(*lists)
    far_table = partner(own_table, "tile", fold_bit)

    leads, lasts = pl.pallas_call(
        pack_kernel,
        out_shape=[shape_of((count, far_rows, width))] * 2,
        in_specs=[spec(VMEM)] * 2,
        out_specs=[spec(VMEM)] * 2,
        compiler_params=params(),
        cost_estimate=cost(1024, 1024 * 1024),
        name="pack",
    )(mine, other)

    k_near, k_far = (
        pl.pallas_call(
            functools.partial(expand_kernel, group),
            out_shape=[shape_of((rows, rows))] * 2,
            in_specs=[spec(VMEM)],
            out_specs=[spec(VMEM)] * 2,
            compiler_params=params(),
            cost_estimate=cost(8 * rows * rows * levels, 1024 * 1024),
            name="expand",
        )(vertical[0])
        for group, rows in ((near_group, near_rows), (far_group, far_rows))
    )
    tables = (ids, own_table, far_table)
    tail = 2 * HALO
    tables, k_near, k_far = lax.optimization_barrier((tables, k_near, k_far))
    near_at = tuple(HALO + b for b in range(count))
    far_at = tuple(
        x * HALO + i if i < HALO else tail + x * (count - HALO) + i - HALO
        for x in range(2)
        for i in range(count)
    )
    for step in range(STEPS):
        prior, following = shift(lasts, leads, ring)
        if step < STEPS - 1:
            near_pieces = (before, lead, last, after, across)
            far_pieces = (leads, lasts, prior, following)
            leads, lasts = run_step(
                size, ring, tables, far_pieces, w, k_far, far_at, [leads.shape, lasts.shape],
                [((i % count >= HALO, p if i % count < HALO else p - tail, far_rows),) for i, p in enumerate(far_at)],
            )
            lead, last = run_step(
                size, 0, tables, near_pieces, w, k_near, near_at, [lead.shape, last.shape],
                [((i >= HALO, i % HALO, near_rows),) for i in range(count)],
            )
            across = partner(lead, "tile", fold_bit)
            before, after = shift(last, lead, peers)
    tables, lead, leads = lax.optimization_barrier((tables, lead, leads))
    route = pl.pallas_call(
        functools.partial(route_kernel, size, entries),
        out_shape=[
            shape_of((2 * entries, width, width)),
            shape_of((2 * entries,), I32),
            shape_of((peers, HEAD, width)),
        ],
        in_specs=[spec(SMEM)] * 3 + [spec(HBM)],
        out_specs=[spec(VMEM), spec(SMEM), spec(VMEM)],
        scratch_shapes=[
            pltpu.SMEM((2 * CAP * peers,), I32),
            pltpu.SMEM((peers,), I32),
            pltpu.SemaphoreType.DMA((2 * entries,)),
        ],
        compiler_params=params(),
        cost_estimate=cost(1024, 1024 * 1024),
        name="routes",
    )
    held, slot_of, header = route(*tables, remap_weights)
    tables, held, header, slot_of = lax.optimization_barrier((tables, held, header, slot_of))
    near_pieces = (before, lead, last, after, across)
    far_pieces = (leads, lasts, prior, following)
    far = SURF * far_group
    close = SURF * near_group
    body = (count, far_rows, width)
    mine, back, mine_top, back_top = run_step(
        size, ring, tables, far_pieces, w, k_far, far_at,
        [body, body, (count, far, width), (count, far, width)],
        [((i // count, i % count, far_rows), (2 + i // count, i % count, far)) for i in range(2 * count)],
    )
    other = partner(back, "tile", fold_bit)
    near, near_top = run_step(
        size, 0, tables, near_pieces, w, k_near, near_at,
        [(count, near_rows, width), (count, close, width)],
        [((0, i, near_rows), (1, i, close)) for i in range(count)],
    )

    surface = SURF * fields
    groups = CAP * (close + 2 * far) // 8 + HEAD // 8
    payload_call = pl.pallas_call(
        functools.partial(partial_kernel, size),
        out_shape=shape_of((peers, groups, 8, width)),
        in_specs=[spec(SMEM)] * 3 + [spec(VMEM)] * 5,
        out_specs=spec(VMEM),
        compiler_params=params(),
        cost_estimate=cost(2 * entries * surface * width * width, 2 * 1024 * 1024),
        name="partials",
    )
    payload = payload_call(*tables[1:], slot_of, header, held, near_top, mine_top, back_top)
    payload = partner(payload, "comp", 0)
    received = lax.all_to_all(payload, "tile", split_axis=0, concat_axis=0, tiled=True)

    whole = pl.pallas_call(
        functools.partial(merge_kernel, fields, near_group, far_group, ring),
        out_shape=shape_of(plain.shape),
        in_specs=[spec(SMEM)] + [spec(VMEM)] * 3,
        out_specs=spec(VMEM),
        compiler_params=params(),
        cost_estimate=cost(2 * count * near_rows * levels * fields * width, 2 * 1024 * 1024),
        name="merge",
    )(ids, near, mine, other)
    final = pl.pallas_call(
        functools.partial(couple_kernel, fields, near_group, far_group),
        out_shape=shape_of(whole.shape),
        in_specs=[spec(SMEM), spec(HBM)] + [spec(VMEM)] * 4,
        out_specs=spec(HBM),
        input_output_aliases={1: 0},
        scratch_shapes=[
            pltpu.VMEM((count + 1, surface, width), F32),
            pltpu.VMEM((count, surface, width), BF16),
            pltpu.VMEM((HEAD, width), I32),
            pltpu.SMEM((HEAD, width), I32),
            pltpu.SemaphoreType.DMA,
        ],
        compiler_params=params(),
        cost_estimate=cost(1024, 1024 * 1024),
        name="couple",
    )(ids, whole, received, near_top, mine_top, other)
    return final.reshape(count, levels, fields, width).transpose(0, 2, 1, 3)[None]


def solution(mesh):
    return jax.shard_map(
        on_device,
        mesh=mesh,
        in_specs=(
            P("comp", "tile", None, None, None),
            P("comp", None, None, None),
            P("comp", None, None),
            P(),
            P("comp", "tile", None),
            P("comp", "tile", None),
            P("comp", "tile"),
            P("comp", "tile"),
            P("comp", "tile"),
            P("comp", "tile", None),
        ),
        out_specs=P("comp", "tile", None, None, None),
        check_vma=False,
    )
```

time: 172 us -> 109 us (0.63)
  local copies, waits for them, and re-layouts: 68.9 us -> 4.23 us
  Pallas kernels: 0 us -> 20.2 us
  matrix products: 17.7 us -> 0 us
  starting transfers between devices: 30.9 us -> 40.8 us
  waiting for transfers between devices: 51.6 us -> 43.3 us
    gather x14 -> x0, local copies, waits for them, and re-layouts: 36 us -> none  [the longest x8 26.7 us: on_device(): source_pool[block_positions[:, k]]]
    pallas_call x0 -> x13, Pallas kernels: none -> 20.2 us  [the longest x4 8.15 us: run_step(): pl.pallas_call(functools.partial(step_kernel, len(pieces), size, ring, ow...]
    dot_general x13 -> x0, matrix products: 17.7 us -> none  [the longest x8 8.04 us: on_device(): jnp.einsum('brc,bcd->brd', source_pool[block_positions[:, k]], exchange_w...]
    ppermute x4 -> x6, waiting for transfers between devices: 23.5 us -> 38.3 us  [partner(): return lax.ppermute(value, axis, pairs)]
    all_to_all x2 -> x1, waiting for transfers between devices: 12.3 us -> 0.01 us  [on_device(): lax.all_to_all(payload, 'tile', split_axis=0, concat_axis=0, tiled=True)]
    ppermute x4 -> x8, starting transfers between devices: 8.86 us -> 20.5 us  [the longest x4 15.2 us: shift(): return (before, lax.ppermute(lead, 'tile', down))]
    unnamed x58 -> x11, local copies, waits for them, and re-layouts: 15.8 us -> 4.23 us
    ppermute x4 -> x8, waiting for transfers between devices: 15.8 us -> 5 us  [the longest x4 2.63 us: shift(): before = lax.ppermute(last, 'tile', up)]
  transfers between devices with their start and end apart: 10 -> 15, of which waited for: 6 -> 8; matrix products, arithmetic and copies ran while one was open for 15% -> 1% of each run, Pallas kernels for 0% -> 12%
where the time goes in v3:
time: 109 us
  waiting for transfers between devices  43.3 us (40%)
  starting transfers between devices  40.8 us (37%)
  Pallas kernels  20.2 us (19%)
  local copies, waits for them, and re-layouts  4.23 us (4%)
    ppermute x6, waiting for transfers between devices, partner(): return lax.ppermute(value, axis, pairs)  38.3 us
    ppermute x4, starting transfers between devices, shift(): return (before, lax.ppermute(lead, 'tile', down))  15.2 us
    ppermute x6, starting transfers between devices, partner(): return lax.ppermute(value, axis, pairs)  10.6 us
    all_to_all x1, starting transfers between devices, on_device(): lax.all_to_all(payload, 'tile', split_axis=0, concat_axis=0, tiled=True)  9.67 us
    pallas_call x4, Pallas kernels, run_step(): pl.pallas_call(functools.partial(step_kernel, len(pieces), size, ring, ow...  8.15 us
    ppermute x4, starting transfers between devices, shift(): before = lax.ppermute(last, 'tile', up)  5.31 us
    unnamed x11, local copies, waits for them, and re-layouts  4.23 us
    pallas_call x1, Pallas kernels, on_device(): held, slot_of, header = route(*tables, remap_weights)  3.2 us
  transfers between devices with their start and end apart: 15, of which 8 were waited for; matrix products, arithmetic and copies ran while one was open for 1% of the time, Pallas kernels for 12%

profile of v3, /device:TPU:0, one launch (start us, length us, event | category | flops | bytes accessed | tf_op | source)
XLA Modules:
  0.0 108.7 jit_solution(3914524779312358078)
XLA Ops:
  0.1 1.2 %copy-done.3 = bf16[1,16,4,60,128]{4,2,3,1,0:T(4,128)(2,1)S(1)} copy-done((bf16[1,16,4,60,128]{4,2,3,1,0:T(4,128)(2,1)S(1)}, bf16[1,16,4,60,128]{4,2,3,1,0:T(4,128)(2,1)}, u32[]{:S(2)}) %copy-start.3) | copy-done | bytes 983064
  1.3 1.1 %split.1 = (bf16[8,120,128]{2,1,0:T(8,128)(2,1)S(1)}, bf16[8,120,128]{2,1,0:T(8,128)(2,1)S(1)}, bf16[16,64,128]{2,1,0:T(8,128)(2,1)S(1)}, bf16[16,64,128]{2,1,0:T(8,128)(2,1)S(1)}) custom-call(s32[2]{0:T(128)S(1)} %pad_add_fusion.ids, bf16[16,240,128]{2,1,0:T(8,128)(2,1)S(1)} %bitcast.27), custom_call_target="tpu_custom_call" | custom-call | flops 235929600 | bytes 2097152 | tf_op jit(solution)/shard_map/split/pallas_call | solution.py:341
  2.4 4.1 %collective-permute-start.4 = (bf16[16,64,128]{2,1,0:T(8,128)(2,1)S(1)}, bf16[16,64,128]{2,1,0:T(8,128)(2,1)S(1)}, u32[]{:S(2)}, u32[]{:S(2)}) collective-permute-start(bf16[16,64,128]{2,1,0:T(8,128)(2,1)S(1)} %get-tuple-element.59), channel_id=1, source_target_pairs={{0,8},{1,9},{2,10},{3,11},{4,12},{5,13},{6,14},{7,15},{8,0},{9,1},... | collective-permute-start | bytes 786440 | tf_op jit(solution)/shard_map/ppermute | solution.py:306
  6.5 1.5 %collective-permute-start.1 = (bf16[8,120,128]{2,1,0:T(8,128)(2,1)S(1)}, bf16[8,120,128]{2,1,0:T(8,128)(2,1)S(1)}, u32[]{:S(2)}, u32[]{:S(2)}) collective-permute-start(bf16[8,120,128]{2,1,0:T(8,128)(2,1)S(1)} %get-tuple-element.53.refs_2_), channel_id=1, source_target_pairs={{0,1},{1,2},{2,3},{3,4},{4,5},{5,6},{6,7},{7,8},{8,9},{9,10},{10,1... | collective-permute-start | bytes 737288 | tf_op jit(solution)/shard_map/ppermute | solution.py:313
  8.0 4.1 %collective-permute-start.2 = (bf16[8,120,128]{2,1,0:T(8,128)(2,1)S(1)}, bf16[8,120,128]{2,1,0:T(8,128)(2,1)S(1)}, u32[]{:S(2)}, u32[]{:S(2)}) collective-permute-start(bf16[8,120,128]{2,1,0:T(8,128)(2,1)S(1)} %get-tuple-element.54.refs_1_), channel_id=1, source_target_pairs={{1,0},{2,1},{3,2},{4,3},{5,4},{6,5},{7,6},{8,7},{9,8},{10,9},{11,1... | collective-permute-start | bytes 737288 | tf_op jit(solution)/shard_map/ppermute | solution.py:314
  12.2 1.4 %table.1.own = s32[192]{0:T(256)} custom-call(s32[4,16]{1,0:T(4,128)} %bitcast.30, s32[4,16]{1,0:T(4,128)} %bitcast.31, s32[1,16]{1,0:T(1,128)} %rest_0_.1, s32[1,16]{1,0:T(1,128)} %rest_1_.1, s32[1,16]{1,0:T(1,128)} %bitcast.32, s32[1,16]{1,0:T(1,128)} %rest_3_.1), custom_call_target="tpu_custom_call" | custom-call | tf_op jit(solution)/shard_map/table/pallas_call | solution.py:361
  13.6 3.0 %collective-permute-start = (s32[192]{0:T(256)}, s32[192]{0:T(256)S(1)}, u32[]{:S(2)}, u32[]{:S(2)}) collective-permute-start(s32[192]{0:T(256)} %table.1.own), channel_id=1, source_target_pairs={{0,8},{1,9},{2,10},{3,11},{4,12},{5,13},{6,14},{7,15},{8,0},{9,1},... | collective-permute-start | bytes 2312 | tf_op jit(solution)/shard_map/ppermute | solution.py:306
  16.6 8.1 %collective-permute-done.4.other = bf16[16,64,128]{2,1,0:T(8,128)(2,1)S(1)} collective-permute-done((bf16[16,64,128]{2,1,0:T(8,128)(2,1)S(1)}, bf16[16,64,128]{2,1,0:T(8,128)(2,1)S(1)}, u32[]{:S(2)}, u32[]{:S(2)}) %collective-permute-start.4) | collective-permute-done | bytes 262176 | tf_op jit(solution)/shard_map/ppermute | solution.py:306
  24.7 1.8 %collective-permute-start.5 = (bf16[16,64,128]{2,1,0:T(8,128)(2,1)S(1)}, bf16[16,64,128]{2,1,0:T(8,128)(2,1)S(1)}, u32[]{:S(2)}, u32[]{:S(2)}) collective-permute-start(bf16[16,64,128]{2,1,0:T(8,128)(2,1)S(1)} %get-tuple-element.61.refs_1_), channel_id=1, source_target_pairs={{0,1},{1,2},{2,3},{3,4},{4,5},{5,6},{6,7},{7,0},{8,9},{9,10},{10,1... | collective-permute-start | bytes 786440 | tf_op jit(solution)/shard_map/ppermute | solution.py:313
  26.5 7.9 %collective-permute-done.far = s32[192]{0:T(256)S(1)} collective-permute-done((s32[192]{0:T(256)}, s32[192]{0:T(256)S(1)}, u32[]{:S(2)}, u32[]{:S(2)}) %collective-permute-start) | collective-permute-done | bytes 800 | tf_op jit(solution)/shard_map/ppermute | solution.py:306
  34.4 4.3 %collective-permute-start.6 = (bf16[16,64,128]{2,1,0:T(8,128)(2,1)S(1)}, bf16[16,64,128]{2,1,0:T(8,128)(2,1)S(1)}, u32[]{:S(2)}, u32[]{:S(2)}) collective-permute-start(bf16[16,64,128]{2,1,0:T(8,128)(2,1)S(1)} %get-tuple-element.60.refs_0_), channel_id=1, source_target_pairs={{1,0},{2,1},{3,2},{4,3},{5,4},{6,5},{7,6},{0,7},{9,8},{10,9},{11,1... | collective-permute-start | bytes 786440 | tf_op jit(solution)/shard_map/ppermute | solution.py:314
  38.7 0.8 copy.14
  40.0 1.6 %copy-done = bf16[1,64,128,128]{3,2,1,0:T(8,128)(2,1)S(1)} copy-done((bf16[1,64,128,128]{3,2,1,0:T(8,128)(2,1)S(1)}, bf16[1,64,128,128]{3,2,1,0:T(8,128)(2,1)}, u32[]{:S(2)}) %copy-start) | copy-done | bytes 2097176
  41.6 0.7 copy-done.4
  42.3 1.8 %shard_map.100 = (bf16[8,120,128]{2,1,0:T(8,128)(2,1)S(1)}, bf16[8,120,128]{2,1,0:T(8,128)(2,1)S(1)}) custom-call(s32[2]{0:T(128)S(1)} %pad_add_fusion.ids, s32[192]{0:T(256)S(1)} %copy-done.4, s32[192]{0:T(256)S(1)} %collective-permute-done.far, bf16[8,120,128]{2,1,0:T(8,128)(2,1)S(1)} %collective-permute-done.1.refs_0_, ...), custom_call_target="tpu_custom_call" | custom-call | flops 251658240 | bytes 8388608 | tf_op jit(solution)/shard_map/pallas_call | solution.py:193
  44.1 2.9 %collective-permute-start.8 = (bf16[8,120,128]{2,1,0:T(8,128)(2,1)S(1)}, bf16[8,120,128]{2,1,0:T(8,128)(2,1)S(1)}, u32[]{:S(2)}, u32[]{:S(2)}) collective-permute-start(bf16[8,120,128]{2,1,0:T(8,128)(2,1)S(1)} %get-tuple-element.75.refs_1_), channel_id=1, source_target_pairs={{1,0},{2,1},{3,2},{4,3},{5,4},{6,5},{7,6},{8,7},{9,8},{10,9},{11,1... | collective-permute-start | bytes 737288 | tf_op jit(solution)/shard_map/ppermute | solution.py:314
  47.7 1.9 %collective-permute-start.7 = (bf16[8,120,128]{2,1,0:T(8,128)(2,1)S(1)}, bf16[8,120,128]{2,1,0:T(8,128)(2,1)S(1)}, u32[]{:S(2)}, u32[]{:S(2)}) collective-permute-start(bf16[8,120,128]{2,1,0:T(8,128)(2,1)S(1)} %get-tuple-element.74.refs_2_), channel_id=1, source_target_pairs={{0,1},{1,2},{2,3},{3,4},{4,5},{5,6},{6,7},{7,8},{8,9},{9,10},{10,1... | collective-permute-start | bytes 737288 | tf_op jit(solution)/shard_map/ppermute | solution.py:313
  49.7 2.3 %shard_map.101 = (bf16[16,64,128]{2,1,0:T(8,128)(2,1)S(1)}, bf16[16,64,128]{2,1,0:T(8,128)(2,1)S(1)}) custom-call(s32[2]{0:T(128)S(1)} %pad_add_fusion.ids, s32[192]{0:T(256)S(1)} %copy-done.4, s32[192]{0:T(256)S(1)} %collective-permute-done.far, bf16[16,64,128]{2,1,0:T(8,128)(2,1)S(1)} %get-tuple-element.60.refs_0_, ...), custom_call_target="tpu_custom_call" | custom-call | flops 268435456 | bytes 8388608 | tf_op jit(solution)/shard_map/pallas_call | solution.py:193
  52.0 3.8 %collective-permute-start.11 = (bf16[16,64,128]{2,1,0:T(8,128)(2,1)S(1)}, bf16[16,64,128]{2,1,0:T(8,128)(2,1)S(1)}, u32[]{:S(2)}, u32[]{:S(2)}) collective-permute-start(bf16[16,64,128]{2,1,0:T(8,128)(2,1)S(1)} %get-tuple-element.77.refs_0_), channel_id=1, source_target_pairs={{1,0},{2,1},{3,2},{4,3},{5,4},{6,5},{7,6},{0,7},{9,8},{10,9},{11,1... | collective-permute-start | bytes 786440 | tf_op jit(solution)/shard_map/ppermute | solution.py:314
  55.8 3.2 %routes.1 = (bf16[32,128,128]{2,1,0:T(8,128)(2,1)S(1)}, s32[32]{0:T(128)S(1)}, bf16[16,8,128]{2,1,0:T(8,128)(2,1)S(1)}) custom-call(s32[2]{0:T(128)S(1)} %pad_add_fusion.ids, s32[192]{0:T(256)S(1)} %copy-done.4, s32[192]{0:T(256)S(1)} %collective-permute-done.far, bf16[2,64,128,128]{3,2,1,0:T(8,128)(2,1)S(1)} %copy-done.2), custom_call_target="tpu_custom_call" | custom-call | flops 1024 | bytes 1048576 | tf_op jit(solution)/shard_map/routes/pallas_call | solution.py:435
  59.0 2.5 %collective-permute-done.7.refs_0_ = bf16[8,120,128]{2,1,0:T(8,128)(2,1)S(1)} collective-permute-done((bf16[8,120,128]{2,1,0:T(8,128)(2,1)S(1)}, bf16[8,120,128]{2,1,0:T(8,128)(2,1)S(1)}, u32[]{:S(2)}, u32[]{:S(2)}) %collective-permute-start.7) | collective-permute-done | bytes 245792 | tf_op jit(solution)/shard_map/ppermute | solution.py:313
  61.6 2.4 %collective-permute-done.9.refs_4_ = bf16[8,120,128]{2,1,0:T(8,128)(2,1)S(1)} collective-permute-done((bf16[8,120,128]{2,1,0:T(8,128)(2,1)S(1)}, bf16[8,120,128]{2,1,0:T(8,128)(2,1)S(1)}, u32[]{:S(2)}, u32[]{:S(2)}) %collective-permute-start.9) | collective-permute-done | bytes 245792 | tf_op jit(solution)/shard_map/ppermute | solution.py:306
  64.0 1.8 %shard_map.102 = (bf16[16,120,128]{2,1,0:T(8,128)(2,1)S(1)}, bf16[16,16,128]{2,1,0:T(8,128)(2,1)S(1)}) custom-call(s32[2]{0:T(128)S(1)} %pad_add_fusion.ids, s32[192]{0:T(256)S(1)} %copy-done.4, s32[192]{0:T(256)S(1)} %collective-permute-done.far, bf16[8,120,128]{2,1,0:T(8,128)(2,1)S(1)} %collective-permute-done.7.refs_0_, ...), custom_call_target="tpu_custom_call" | custom-call | flops 251658240 | bytes 8388608 | tf_op jit(solution)/shard_map/pallas_call | solution.py:193
  65.9 2.4 %collective-permute-done.11.refs_3_ = bf16[16,64,128]{2,1,0:T(8,128)(2,1)S(1)} collective-permute-done((bf16[16,64,128]{2,1,0:T(8,128)(2,1)S(1)}, bf16[16,64,128]{2,1,0:T(8,128)(2,1)S(1)}, u32[]{:S(2)}, u32[]{:S(2)}) %collective-permute-start.11) | collective-permute-done | bytes 262176 | tf_op jit(solution)/shard_map/ppermute | solution.py:314
  68.3 2.3 %shard_map.103 = (bf16[16,64,128]{2,1,0:T(8,128)(2,1)S(1)}, bf16[16,64,128]{2,1,0:T(8,128)(2,1)S(1)}, bf16[16,8,128]{2,1,0:T(8,128)(2,1)S(1)}, bf16[16,8,128]{2,1,0:T(8,128)(2,1)S(1)}) custom-call(s32[2]{0:T(128)S(1)} %pad_add_fusion.ids, s32[192]{0:T(256)S(1)} %copy-done.4, s32[192]{0:T(256)S(1)} %collective-permute-done.far, ...), custom_call_target="tpu_custom_call" | custom-call | flops 268435456 | bytes 8388608 | tf_op jit(solution)/shard_map/pallas_call | solution.py:193
  70.5 1.0 partials.1
  71.6 1.7 %collective-permute-done.13 = bf16[16,9,8,128]{3,2,1,0:T(8,128)(2,1)} collective-permute-done((bf16[16,9,8,128]{3,2,1,0:T(8,128)(2,1)S(1)}, bf16[16,9,8,128]{3,2,1,0:T(8,128)(2,1)}, u32[]{:S(2)}, u32[]{:S(2)}) %collective-permute-start.13) | collective-permute-done | bytes 294944 | tf_op jit(solution)/shard_map/ppermute | solution.py:306
  73.3 9.7 %all-to-all-start = ((bf16[16,9,8,128]{3,2,1,0:T(8,128)(2,1)}), bf16[16,9,8,128]{3,2,1,0:T(8,128)(2,1)S(1)}, u32[]{:S(2)}, u32[]{:S(2)}) async-start(bf16[16,9,8,128]{3,2,1,0:T(8,128)(2,1)} %collective-permute-done.13), calls=%async_computation | async-start | bytes 589824 | tf_op jit(solution)/shard_map/all_to_all | solution.py:467
  83.0 2.8 %collective-permute-start.12 = (bf16[16,64,128]{2,1,0:T(8,128)(2,1)S(1)}, bf16[16,64,128]{2,1,0:T(8,128)(2,1)S(1)}, u32[]{:S(2)}, u32[]{:S(2)}) collective-permute-start(bf16[16,64,128]{2,1,0:T(8,128)(2,1)S(1)} %get-tuple-element.80), channel_id=1, source_target_pairs={{0,8},{1,9},{2,10},{3,11},{4,12},{5,13},{6,14},{7,15},{8,0},{9,1},... | collective-permute-start | bytes 786440 | tf_op jit(solution)/shard_map/ppermute | solution.py:306
  85.8 18.2 %collective-permute-done.12.other = bf16[16,64,128]{2,1,0:T(8,128)(2,1)S(1)} collective-permute-done((bf16[16,64,128]{2,1,0:T(8,128)(2,1)S(1)}, bf16[16,64,128]{2,1,0:T(8,128)(2,1)S(1)}, u32[]{:S(2)}, u32[]{:S(2)}) %collective-permute-start.12) | collective-permute-done | bytes 262176 | tf_op jit(solution)/shard_map/ppermute | solution.py:306
  104.0 2.4 %merge.1.state = bf16[16,240,128]{2,1,0:T(8,128)(2,1)} custom-call(s32[2]{0:T(128)S(1)} %pad_add_fusion.ids, bf16[16,120,128]{2,1,0:T(8,128)(2,1)S(1)} %get-tuple-element.76.near, bf16[16,64,128]{2,1,0:T(8,128)(2,1)S(1)} %get-tuple-element.79.mine, bf16[16,64,128]{2,1,0:T(8,128)(2,1)S(1)} %collective-permute-done.12.other), custom_call_target="tpu_custom_call" | custom-call | flops 117964800 | bytes 2097152 | tf_op jit(solution)/shard_map/merge/pallas_call | solution.py:469
  106.4 2.3 %couple.1 = bf16[16,240,128]{2,1,0:T(8,128)(2,1)} custom-call(s32[2]{0:T(128)S(1)} %pad_add_fusion.ids, bf16[16,240,128]{2,1,0:T(8,128)(2,1)} %merge.1.state, bf16[16,9,8,128]{3,2,1,0:T(8,128)(2,1)S(1)} %all-to-all-done.received, bf16[16,16,128]{2,1,0:T(8,128)(2,1)S(1)} %get-tuple-element.84.near, ...), custom_call_target="tpu_custom_call", output_to_operand_aliasing={{}: (1, {})} | custom-call | flops 1024 | bytes 1048576 | tf_op jit(solution)/shard_map/couple/pallas_call | solution.py:478
  (23 shorter events, 1.5 us)
Async XLA Ops:
  0.1 1.2 %copy-start.3 = (bf16[1,16,4,60,128]{4,2,3,1,0:T(4,128)(2,1)S(1)}, bf16[1,16,4,60,128]{4,2,3,1,0:T(4,128)(2,1)}, u32[]{:S(2)}) copy-start(bf16[1,16,4,60,128]{4,2,3,1,0:T(4,128)(2,1)} %param.10) | copy-start | bytes 2949124
  2.4 22.2 %collective-permute-start.4 = (bf16[16,64,128]{2,1,0:T(8,128)(2,1)S(1)}, bf16[16,64,128]{2,1,0:T(8,128)(2,1)S(1)}, u32[]{:S(2)}, u32[]{:S(2)}) collective-permute-start(bf16[16,64,128]{2,1,0:T(8,128)(2,1)S(1)} %get-tuple-element.59), channel_id=1, source_target_pairs={{0,8},{1,9},{2,10},{3,11},{4,12},{5,13},{6,14},{7,15},{8,0},{9,1},... | collective-permute-start | bytes 786440 | tf_op jit(solution)/shard_map/ppermute | solution.py:306
  6.5 33.5 %collective-permute-start.1 = (bf16[8,120,128]{2,1,0:T(8,128)(2,1)S(1)}, bf16[8,120,128]{2,1,0:T(8,128)(2,1)S(1)}, u32[]{:S(2)}, u32[]{:S(2)}) collective-permute-start(bf16[8,120,128]{2,1,0:T(8,128)(2,1)S(1)} %get-tuple-element.53.refs_2_), channel_id=1, source_target_pairs={{0,1},{1,2},{2,3},{3,4},{4,5},{5,6},{6,7},{7,8},{8,9},{9,10},{10,1... | collective-permute-start | bytes 737288 | tf_op jit(solution)/shard_map/ppermute | solution.py:313
  8.0 32.0 %collective-permute-start.2 = (bf16[8,120,128]{2,1,0:T(8,128)(2,1)S(1)}, bf16[8,120,128]{2,1,0:T(8,128)(2,1)S(1)}, u32[]{:S(2)}, u32[]{:S(2)}) collective-permute-start(bf16[8,120,128]{2,1,0:T(8,128)(2,1)S(1)} %get-tuple-element.54.refs_1_), channel_id=1, source_target_pairs={{1,0},{2,1},{3,2},{4,3},{5,4},{6,5},{7,6},{8,7},{9,8},{10,9},{11,1... | collective-permute-start | bytes 737288 | tf_op jit(solution)/shard_map/ppermute | solution.py:314
  12.2 27.9 %collective-permute-start.3 = (bf16[8,120,128]{2,1,0:T(8,128)(2,1)S(1)}, bf16[8,120,128]{2,1,0:T(8,128)(2,1)S(1)}, u32[]{:S(2)}, u32[]{:S(2)}) collective-permute-start(bf16[8,120,128]{2,1,0:T(8,128)(2,1)S(1)} %get-tuple-element.54.refs_1_), channel_id=1, source_target_pairs={{0,8},{1,9},{2,10},{3,11},{4,12},{5,13},{6,14},{7,15},{8,0},{9,1},... | collective-permute-start | bytes 737288 | tf_op jit(solution)/shard_map/ppermute | solution.py:306
  13.6 20.8 %collective-permute-start = (s32[192]{0:T(256)}, s32[192]{0:T(256)S(1)}, u32[]{:S(2)}, u32[]{:S(2)}) collective-permute-start(s32[192]{0:T(256)} %table.1.own), channel_id=1, source_target_pairs={{0,8},{1,9},{2,10},{3,11},{4,12},{5,13},{6,14},{7,15},{8,0},{9,1},... | collective-permute-start | bytes 2312 | tf_op jit(solution)/shard_map/ppermute | solution.py:306
  24.7 25.0 %collective-permute-start.5 = (bf16[16,64,128]{2,1,0:T(8,128)(2,1)S(1)}, bf16[16,64,128]{2,1,0:T(8,128)(2,1)S(1)}, u32[]{:S(2)}, u32[]{:S(2)}) collective-permute-start(bf16[16,64,128]{2,1,0:T(8,128)(2,1)S(1)} %get-tuple-element.61.refs_1_), channel_id=1, source_target_pairs={{0,1},{1,2},{2,3},{3,4},{4,5},{5,6},{6,7},{7,0},{8,9},{9,10},{10,1... | collective-permute-start | bytes 786440 | tf_op jit(solution)/shard_map/ppermute | solution.py:313
  34.4 15.3 %collective-permute-start.6 = (bf16[16,64,128]{2,1,0:T(8,128)(2,1)S(1)}, bf16[16,64,128]{2,1,0:T(8,128)(2,1)S(1)}, u32[]{:S(2)}, u32[]{:S(2)}) collective-permute-start(bf16[16,64,128]{2,1,0:T(8,128)(2,1)S(1)} %get-tuple-element.60.refs_0_), channel_id=1, source_target_pairs={{1,0},{2,1},{3,2},{4,3},{5,4},{6,5},{7,6},{0,7},{9,8},{10,9},{11,1... | collective-permute-start | bytes 786440 | tf_op jit(solution)/shard_map/ppermute | solution.py:314
  40.0 1.6 %copy-start = (bf16[1,64,128,128]{3,2,1,0:T(8,128)(2,1)S(1)}, bf16[1,64,128,128]{3,2,1,0:T(8,128)(2,1)}, u32[]{:S(2)}) copy-start(bf16[1,64,128,128]{3,2,1,0:T(8,128)(2,1)} %param.11) | copy-start | bytes 6291460
  41.6 0.7 copy-start.4
  42.3 7.4 %copy-start.1 = (bf16[1,64,128,128]{3,2,1,0:T(8,128)(2,1)S(1)}, bf16[1,64,128,128]{3,2,1,0:T(8,128)(2,1)}, u32[]{:S(2)}) copy-start(bf16[1,64,128,128]{3,2,1,0:T(8,128)(2,1)} %param.11) | copy-start | bytes 6291460
  42.3 13.5 %copy-start.2 = (bf16[2,64,128,128]{3,2,1,0:T(8,128)(2,1)S(1)}, bf16[2,64,128,128]{3,2,1,0:T(8,128)(2,1)}, u32[]{:S(2)}) copy-start(bf16[2,64,128,128]{3,2,1,0:T(8,128)(2,1)} %weights.1) | copy-start | bytes 12582916
  44.1 17.4 %collective-permute-start.8 = (bf16[8,120,128]{2,1,0:T(8,128)(2,1)S(1)}, bf16[8,120,128]{2,1,0:T(8,128)(2,1)S(1)}, u32[]{:S(2)}, u32[]{:S(2)}) collective-permute-start(bf16[8,120,128]{2,1,0:T(8,128)(2,1)S(1)} %get-tuple-element.75.refs_1_), channel_id=1, source_target_pairs={{1,0},{2,1},{3,2},{4,3},{5,4},{6,5},{7,6},{8,7},{9,8},{10,9},{11,1... | collective-permute-start | bytes 737288 | tf_op jit(solution)/shard_map/ppermute | solution.py:314
  47.1 16.9 %collective-permute-start.9 = (bf16[8,120,128]{2,1,0:T(8,128)(2,1)S(1)}, bf16[8,120,128]{2,1,0:T(8,128)(2,1)S(1)}, u32[]{:S(2)}, u32[]{:S(2)}) collective-permute-start(bf16[8,120,128]{2,1,0:T(8,128)(2,1)S(1)} %get-tuple-element.75.refs_1_), channel_id=1, source_target_pairs={{0,8},{1,9},{2,10},{3,11},{4,12},{5,13},{6,14},{7,15},{8,0},{9,1},... | collective-permute-start | bytes 737288 | tf_op jit(solution)/shard_map/ppermute | solution.py:306
  47.7 13.8 %collective-permute-start.7 = (bf16[8,120,128]{2,1,0:T(8,128)(2,1)S(1)}, bf16[8,120,128]{2,1,0:T(8,128)(2,1)S(1)}, u32[]{:S(2)}, u32[]{:S(2)}) collective-permute-start(bf16[8,120,128]{2,1,0:T(8,128)(2,1)S(1)} %get-tuple-element.74.refs_2_), channel_id=1, source_target_pairs={{0,1},{1,2},{2,3},{3,4},{4,5},{5,6},{6,7},{7,8},{8,9},{9,10},{10,1... | collective-permute-start | bytes 737288 | tf_op jit(solution)/shard_map/ppermute | solution.py:313
  52.0 14.0 %collective-permute-start.10 = (bf16[16,64,128]{2,1,0:T(8,128)(2,1)S(1)}, bf16[16,64,128]{2,1,0:T(8,128)(2,1)S(1)}, u32[]{:S(2)}, u32[]{:S(2)}) collective-permute-start(bf16[16,64,128]{2,1,0:T(8,128)(2,1)S(1)} %get-tuple-element.78.refs_1_), channel_id=1, source_target_pairs={{0,1},{1,2},{2,3},{3,4},{4,5},{5,6},{6,7},{7,0},{8,9},{9,10},{10,1... | collective-permute-start | bytes 786440 | tf_op jit(solution)/shard_map/ppermute | solution.py:313
  52.0 16.2 %collective-permute-start.11 = (bf16[16,64,128]{2,1,0:T(8,128)(2,1)S(1)}, bf16[16,64,128]{2,1,0:T(8,128)(2,1)S(1)}, u32[]{:S(2)}, u32[]{:S(2)}) collective-permute-start(bf16[16,64,128]{2,1,0:T(8,128)(2,1)S(1)} %get-tuple-element.77.refs_0_), channel_id=1, source_target_pairs={{1,0},{2,1},{3,2},{4,3},{5,4},{6,5},{7,6},{0,7},{9,8},{10,9},{11,1... | collective-permute-start | bytes 786440 | tf_op jit(solution)/shard_map/ppermute | solution.py:314
  71.5 1.7 %collective-permute-start.13 = (bf16[16,9,8,128]{3,2,1,0:T(8,128)(2,1)S(1)}, bf16[16,9,8,128]{3,2,1,0:T(8,128)(2,1)}, u32[]{:S(2)}, u32[]{:S(2)}) collective-permute-start(bf16[16,9,8,128]{3,2,1,0:T(8,128)(2,1)S(1)} %partials.1), channel_id=1, source_target_pairs={{0,16},{16,0},{1,17},{17,1},{2,18},{18,2},{3,19},{19,3},{4,20},{20... | collective-permute-start | bytes 884744 | tf_op jit(solution)/shard_map/ppermute | solution.py:306
  73.3 33.1 %all-to-all-start = ((bf16[16,9,8,128]{3,2,1,0:T(8,128)(2,1)}), bf16[16,9,8,128]{3,2,1,0:T(8,128)(2,1)S(1)}, u32[]{:S(2)}, u32[]{:S(2)}) async-start(bf16[16,9,8,128]{3,2,1,0:T(8,128)(2,1)} %collective-permute-done.13), calls=%async_computation | async-start | bytes 589824 | tf_op jit(solution)/shard_map/all_to_all | solution.py:467
  83.0 21.0 %collective-permute-start.12 = (bf16[16,64,128]{2,1,0:T(8,128)(2,1)S(1)}, bf16[16,64,128]{2,1,0:T(8,128)(2,1)S(1)}, u32[]{:S(2)}, u32[]{:S(2)}) collective-permute-start(bf16[16,64,128]{2,1,0:T(8,128)(2,1)S(1)} %get-tuple-element.80), channel_id=1, source_target_pairs={{0,8},{1,9},{2,10},{3,11},{4,12},{5,13},{6,14},{7,15},{8,0},{9,1},... | collective-permute-start | bytes 786440 | tf_op jit(solution)/shard_map/ppermute | solution.py:306

commit v4 on v3

v4 whole, which is shorter than its diff:
```python
import functools

import jax
import jax.numpy as jnp
from jax import lax
from jax.experimental import pallas as pl
from jax.experimental.pallas import tpu as pltpu
from jax.sharding import PartitionSpec as P


SURF = 8
HALO = 8
STEPS = 2
CAP = 2
HEAD = 8

VMEM = pltpu.MemorySpace.VMEM
SMEM = pltpu.MemorySpace.SMEM
HBM = pltpu.MemorySpace.HBM
BF16 = jnp.bfloat16
F32 = jnp.float32
I32 = jnp.int32


def spec(space):
    return pl.BlockSpec(memory_space=space)


def shape_of(shape, dtype=BF16):
    return jax.ShapeDtypeStruct(shape, dtype)


def params():
    return pltpu.CompilerParams(vmem_limit_bytes=16 * 1024 * 1024)


def cost(flops, moved):
    return pl.CostEstimate(flops=flops, bytes_accessed=moved, transcendentals=0)


def select_matrix(rows, wide, fields, group, first, inverse):
    shape = (wide, rows) if inverse else (rows, wide)
    mine = lax.broadcasted_iota(I32, shape, 1 if inverse else 0)
    other = lax.broadcasted_iota(I32, shape, 0 if inverse else 1)
    source = (mine // group) * fields + first + mine % group
    return jnp.where(source == other, 1.0, 0.0).astype(BF16)


def expand_kernel(group, v, k_hi, k_lo):
    rows, levels = k_hi.shape[0], v.shape[0]
    shape = (rows, levels)
    level = lax.broadcasted_iota(I32, shape, 0) // group
    spread = jnp.where(level == lax.broadcasted_iota(I32, shape, 1), 1.0, 0.0).astype(BF16)
    square = (rows, rows)
    same = (
        lax.broadcasted_iota(I32, square, 0) % group == lax.broadcasted_iota(I32, square, 1) % group
    )
    value = v[...]
    high = value.astype(BF16)
    low = (value - high.astype(F32)).astype(BF16)
    for part, out in ((high, k_hi), (low, k_lo)):
        tall = jnp.dot(spread, part, preferred_element_type=F32).astype(BF16)
        full = lax.dot_general(tall, spread, (((1,), (1,)), ((), ())), preferred_element_type=F32)
        out[...] = jnp.where(same, full, 0.0).astype(BF16)


def load_kernel(ids, w, remap, w_out, remap_out, sems):
    copies = [
        pltpu.make_async_copy(w, w_out, sems.at[0]),
        pltpu.make_async_copy(remap.at[1 - ids[1]], remap_out, sems.at[1]),
    ]
    for c in copies:
        c.start()
    for c in copies:
        c.wait()


def table_kernel(*refs):
    lists, (table, sent, taken) = refs[:6], refs[6:]
    for p in range(taken.shape[0]):
        taken[p] = 0
    at = 0
    for n, src in enumerate(lists):
        for i in range(src.shape[0]):
            for j in range(src.shape[1]):
                value = src[i, j]
                if n == 4:
                    rank = taken[value]
                    taken[value] = rank + 1
                    value = value * CAP + rank
                table[at] = value
                sent[at] = value
                at += 1


def groups_of(group, near, ring, ids):
    odd = ids[0] % 2
    low = jnp.where(ids[0] < ring, 1, 0)
    return (1 - odd) * group, odd * group, near + low * group, near + (1 - low) * group


def split_kernel(fields, group, ring, ids, x, *outs):
    rows, width = outs[0].shape[1:]
    firsts = groups_of(group, 2 * group, ring, ids)
    picks = [select_matrix(rows, x.shape[1], fields, group, f, False) for f in firsts]
    pick = jnp.concatenate(picks, axis=0)
    for b in range(0, x.shape[0], 2):
        pair = jnp.concatenate([x[b], x[b + 1]], axis=1)
        got = jnp.dot(pick, pair, preferred_element_type=F32).astype(BF16)
        for j, dst in enumerate(outs):
            for i in range(2):
                dst[b + i] = got[j * rows : (j + 1) * rows, i * width : (i + 1) * width]


def edges(ids, leads, lasts, up, down):
    odd = ids[0] % 2
    up[...] = lasts[pl.ds((1 - odd) * HALO, HALO)]
    down[...] = leads[pl.ds(odd * HALO, HALO)]


def pack_kernel(ids, mine, other, leads, lasts, *ends):
    half = leads.shape[0] // 2
    for i, src in enumerate((mine, other)):
        leads[pl.ds(i * half, half)] = src[pl.ds(0, half)]
        lasts[pl.ds(i * half, half)] = src[pl.ds(half, half)]
    if ends:
        edges(ids, leads, lasts, *ends)


def pair_index(slot, x, odd, count):
    second = x + odd - 2 * x * odd
    inner = slot - HALO
    later = inner - count
    home = jnp.where(inner < HALO, x * HALO + inner, HALO + x * HALO + inner)
    after = jnp.where(second == 1, 3 * count + HALO + later, (1 - x) * HALO + later)
    beyond = jnp.where(later < HALO, after, 2 * count + x * HALO + later - HALO)
    inside = jnp.where(inner < count, home, beyond)
    before = jnp.where(second == 1, count + (1 - x) * HALO + slot, 3 * count + slot)
    return jnp.where(inner < 0, before, inside)


def far_index(slot, x, at, ring, count):
    side_before = jnp.where(at == 0, 1 - x, x)
    side_after = jnp.where(at == ring - 1, 1 - x, x)
    inner = slot - HALO
    later = inner - count
    home = jnp.where(inner < HALO, x * HALO + inner, HALO + x * HALO + inner)
    beyond = jnp.where(
        later < HALO, 3 * count + side_after * HALO + later, (1 - x) * HALO + later - HALO
    )
    inside = jnp.where(inner < count, home, beyond)
    return jnp.where(inner < 0, 2 * count + side_before * HALO + slot, inside)


def step_kernel(pieces, size, ring, own_at, writes, ids, own, mate, *refs):
    sources, (w, k_hi, k_lo) = refs[:pieces], refs[pieces : pieces + 3]
    outs, (pool, mid, hi, lo) = refs[pieces + 3 : -4], refs[-4:]
    at = 0
    for src in sources:
        n = src.shape[0]
        pool[pl.ds(at, n)] = src[...]
        at += n
    count = len(own_at)
    stride = count // 2
    width = w.shape[1]
    for b in range(count):
        total = pool[own_at[b]].astype(F32)
        x, table = b // stride, mate if b >= stride else own
        entries = range(b % stride, size, stride)
        where = [table[e] for e in entries]
        if ring:
            where = [far_index(slot, x, ids[0] % ring, ring, stride) for slot in where]
        else:
            where = [pair_index(slot, x, ids[0] % 2, stride) for slot in where]
        what = [table[size + e] for e in entries]
        for k in range(0, len(what), 2):
            lhs = jnp.concatenate([pool[where[k]], pool[where[k + 1]]], axis=1)
            rhs = jnp.concatenate([w[what[k]], w[what[k + 1]]], axis=0)
            total = total + jnp.dot(lhs, rhs, preferred_element_type=F32)
        lanes = slice(b * width, (b + 1) * width)
        mid[:, lanes] = total
        top = total.astype(BF16)
        hi[:, lanes] = top
        lo[:, lanes] = (total - top.astype(F32)).astype(BF16)
    big, small = k_hi[...], k_lo[...]
    for b in range(0, count, 2):
        lanes = slice(b * width, (b + 2) * width)
        mixed = jnp.dot(big, hi[:, lanes], preferred_element_type=F32)
        mixed = mixed + jnp.dot(big, lo[:, lanes], preferred_element_type=F32)
        mixed = mixed + jnp.dot(small, hi[:, lanes], preferred_element_type=F32)
        new = (mid[:, lanes] + jnp.tanh(mixed)).astype(BF16)
        for i in range(2):
            for out, place, rows in writes[b + i]:
                outs[out][place] = new[:rows, i * width : (i + 1) * width]
    if not ring and outs[2].shape[0] == HALO:
        edges(ids, *outs)


def run_step(size, ring, tables, pieces, w, k, own_at, outs, writes):
    _, rows, width = pieces[0].shape
    count = len(own_at)
    total = sum(p.shape[0] for p in pieces)
    return pl.pallas_call(
        functools.partial(step_kernel, len(pieces), size, ring, own_at, writes),
        out_shape=[shape_of(o) for o in outs],
        in_specs=[spec(SMEM)] * 3 + [spec(VMEM)] * len(pieces) + [spec(VMEM)] * 3,
        out_specs=[spec(VMEM)] * len(outs),
        scratch_shapes=[
            pltpu.VMEM((total, rows, width), BF16),
            pltpu.VMEM((rows, count * width), F32),
            pltpu.VMEM((rows, count * width), BF16),
            pltpu.VMEM((rows, count * width), BF16),
        ],
        compiler_params=params(),
        cost_estimate=cost(4 * 2 * count * rows * width * width, 8 * 1024 * 1024),
    )(*tables, *pieces, w, *k)


def partial_kernel(size, entries, ids, own, pair, far, weights, *rest):
    pair_mine, pair_back, far_mine, far_back, payload = rest
    thin = pair_mine.shape[1] // 8
    head = payload.shape[1] - HEAD // 8
    payload[...] = jnp.zeros(payload.shape, payload.dtype)
    shape = payload.shape[2:]
    flat = lax.broadcasted_iota(I32, shape, 0) * shape[1] + lax.broadcasted_iota(I32, shape, 1)
    flat = flat - ids[0] * 3 * CAP
    for e in range(3 * entries):
        kind = e // entries
        table, at = (own, pair, far)[kind], 2 * size + e % entries
        src, slot = table[at], table[at + 2 * entries]
        place, rank = slot // CAP, slot % CAP
        if kind == 0:
            rows, groups, base = jnp.concatenate([pair_mine[src], far_mine[src]], axis=0), 2 * thin, 0
        else:
            rows = (pair_back if kind == 1 else far_back)[src]
            groups, base = thin, CAP * thin * (1 + kind)
        value = jnp.dot(rows, weights[table[at + entries]], preferred_element_type=F32)
        value = value.reshape(groups, 8, value.shape[1]).astype(BF16)
        payload[place, pl.ds(base + rank * groups, groups)] = value
        mark = (table[at + 3 * entries] + 1).astype(F32)
        old = payload[place, head].astype(F32)
        payload[place, head] = jnp.where(flat == kind * CAP + rank, mark, old).astype(BF16)


def merge_kernel(fields, group, ring, ids, pair_mine, pair_other, far_mine, far_other, out):
    _, wide, width = out.shape
    rows = pair_mine.shape[1]
    firsts = groups_of(group, 2 * group, ring, ids)
    picks = [select_matrix(rows, wide, fields, group, f, True) for f in firsts]
    for b in range(0, out.shape[0], 2):
        got = None
        for pick, s in zip(picks, (pair_other, pair_mine, far_other, far_mine)):
            part = jnp.concatenate([s[b], s[b + 1]], axis=1)
            part = jnp.dot(pick, part, preferred_element_type=F32)
            got = part if got is None else got + part
        got = got.astype(BF16)
        out[b] = got[:, :width]
        out[b + 1] = got[:, width:]


def couple_kernel(fields, group, ids, state, received, *rest):
    pair_mine, pair_other, far_mine, far_other, out, total, top, found, targets, sem = rest
    del state
    count, rows, width = top.shape
    peers = received.shape[0]
    part = pair_mine.shape[1]
    thin = part // 8
    heads = received[:, received.shape[1] - HEAD // 8].astype(F32)
    found[...] = jnp.sum(heads, axis=0).astype(I32)
    copy = pltpu.make_async_copy(found, targets, sem)
    copy.start()
    total[...] = jnp.zeros(total.shape, F32)
    copy.wait()
    for p in range(peers):
        close = part * (p % 2)
        side = 2 * part if p < peers // 2 else 3 * part
        for i in range(3 * CAP):
            q = p * 3 * CAP + i
            t = targets[q // width, q % width]
            kind, at = i // CAP, i % CAP
            if kind == 0:
                got = received[p, 2 * thin * at : 2 * thin * (at + 1)].astype(F32)
                got = got.reshape(2 * part, width)
                total[t, close : close + part] = total[t, close : close + part] + got[:part]
                total[t, side : side + part] = total[t, side : side + part] + got[part:]
            else:
                base = CAP * thin * (1 + kind) + at * thin
                got = received[p, base : base + thin].astype(F32).reshape(part, width)
                here = close if kind == 1 else side
                total[t, here : here + part] = total[t, here : here + part] + got
    shape = (rows, rows)
    have = lax.broadcasted_iota(I32, shape, 1)
    field = have // part * group + have % part % group
    want = have % part // group * fields + field
    pick = jnp.where(want == lax.broadcasted_iota(I32, shape, 0), 1.0, 0.0).astype(BF16)
    even = ids[0] % 2 == 0
    is_low = ids[0] < peers // 2
    for g in range(count):
        base = []
        for first, mine, other in ((even, pair_mine, pair_other), (is_low, far_mine, far_other)):
            here, there = mine[g].astype(F32), other[g, :part].astype(F32)
            base += [jnp.where(first, here, there), jnp.where(first, there, here)]
        new = (jnp.concatenate(base, axis=0) + total[g + 1]).astype(BF16)
        top[g] = jnp.dot(pick, new, preferred_element_type=F32).astype(BF16)
    copy = pltpu.make_async_copy(top, out.at[:, pl.ds(0, rows)], sem)
    copy.start()
    copy.wait()


def partner(value, axis, distance):
    mask = 2**distance
    pairs = [(source, source ^ mask) for source in range(lax.axis_size(axis))]
    return lax.ppermute(value, axis, pairs)


def shift(last, lead, ring, stride):
    peers = lax.axis_size("tile")
    up = [(i, i // ring * ring + (i + stride) % ring) for i in range(peers)]
    down = [(j, i) for i, j in up]
    before = lax.ppermute(last, "tile", up)
    return before, lax.ppermute(lead, "tile", down)


def on_device(
    state,
    dyn_weights,
    vertical,
    remap_weights,
    neighbor_slots,
    neighbor_tiles,
    remap_source,
    remap_target,
    remap_tile,
    remap_dest,
):
    _, count, fields, levels, width = state.shape
    group = fields // 4
    rows = -(-levels * group // 16) * 16
    peers = lax.axis_size("tile")
    ring = peers // 2
    fold_bit = peers.bit_length() - 2
    ids = jnp.stack([lax.axis_index("tile"), lax.axis_index("comp")])
    w = dyn_weights[0]
    plain = state[0].transpose(0, 2, 1, 3).reshape(count, levels * fields, width)
    body = (count, rows, width)

    pair_sent, pair_mine, far_sent, far_mine = pl.pallas_call(
        functools.partial(split_kernel, fields, group, ring),
        out_shape=[shape_of(body)] * 4,
        in_specs=[spec(SMEM), spec(VMEM)],
        out_specs=[spec(VMEM)] * 4,
        compiler_params=params(),
        cost_estimate=cost(8 * count * rows * levels * fields * width, 2 * 1024 * 1024),
        name="split",
    )(ids, plain)
    far_other = partner(far_sent, "tile", fold_bit)
    pair_other = partner(pair_sent, "tile", 0)

    lists = (neighbor_slots[0].T, neighbor_tiles[0].T, remap_source, remap_tile, remap_dest[:, :, 0], remap_target)
    size, entries = lists[0].size, remap_source.shape[1]
    own_table, sent_table = pl.pallas_call(
        table_kernel,
        out_shape=[shape_of((2 * size + 4 * entries,), I32)] * 2,
        in_specs=[spec(SMEM)] * len(lists),
        out_specs=[spec(SMEM)] * 2,
        scratch_shapes=[pltpu.SMEM((peers,), I32)],
        name="table",
    )(*lists)
    far_table = partner(sent_table, "tile", fold_bit)
    pair_table = partner(sent_table, "tile", 0)

    def pack(mine, other, ends):
        return pl.pallas_call(
            pack_kernel,
            out_shape=[shape_of(body)] * 2 + [shape_of((HALO, rows, width))] * ends,
            in_specs=[spec(SMEM)] + [spec(VMEM)] * 2,
            out_specs=[spec(VMEM)] * (2 + ends),
            compiler_params=params(),
            cost_estimate=cost(1024, 1024 * 1024),
            name="pack",
        )(ids, mine, other)

    pair_leads, pair_lasts, up, down = pack(pair_mine, pair_other, 2)
    expand = pl.pallas_call(
        functools.partial(expand_kernel, group),
        out_shape=[shape_of((rows, rows))] * 2,
        in_specs=[spec(VMEM)],
        out_specs=[spec(VMEM)] * 2,
        compiler_params=params(),
        cost_estimate=cost(8 * rows * rows * levels, 1024 * 1024),
        name="expand",
    )
    load = pl.pallas_call(
        load_kernel,
        out_shape=[shape_of(w.shape), shape_of(remap_weights.shape[1:])],
        in_specs=[spec(SMEM)] + [spec(HBM)] * 2,
        out_specs=[spec(VMEM)] * 2,
        scratch_shapes=[pltpu.SemaphoreType.DMA((2,))],
        compiler_params=params(),
        cost_estimate=cost(1024, 8 * 1024 * 1024),
        name="load",
    )
    k = expand(vertical[0])
    w, remap = load(ids, w, remap_weights)
    far_other, k, w, remap = lax.optimization_barrier((far_other, k, w, remap))
    tables = (own_table, pair_table, far_table)
    leads, lasts = pack(far_mine, far_other, 0)

    tail = 2 * HALO
    places = tuple(
        x * HALO + i if i < HALO else tail + x * (count - HALO) + i - HALO
        for x in range(2)
        for i in range(count)
    )
    onward = [((i % count >= HALO, p if i % count < HALO else p - tail, rows),) for i, p in enumerate(places)]
    part = SURF * group
    finish = [((i // count, i % count, rows), (2 + i // count, i % count, part)) for i in range(2 * count)]
    ended = [body, body, (count, part, width), (count, part, width)]
    edge = (HALO, rows, width)
    for step in range(STEPS):
        across = partner(pair_leads, "tile", fold_bit)
        before, after = shift(up, down, peers, 2)
        prior, following = shift(lasts, leads, ring, 1)
        pair_pieces = (pair_leads, pair_lasts, across, before, after)
        far_pieces = (leads, lasts, prior, following)
        pair_ids, far_ids = (ids, tables[0], tables[1]), (ids, tables[0], tables[2])
        if step < STEPS - 1:
            pair_leads, pair_lasts, up, down = run_step(
                size, 0, pair_ids, pair_pieces, w, k, places, [body, body, edge, edge], onward
            )
            leads, lasts = run_step(size, ring, far_ids, far_pieces, w, k, places, [body, body], onward)
    pair_mine, pair_back, pair_top, pair_back_top = run_step(
        size, 0, (ids, tables[0], tables[1]), pair_pieces, w, k, places, ended, finish
    )
    far_mine, far_back, far_top, far_back_top = run_step(
        size, ring, (ids, tables[0], tables[2]), far_pieces, w, k, places, ended, finish
    )
    pair_other = partner(pair_back, "tile", 0)
    far_other = partner(far_back, "tile", fold_bit)

    surface = SURF * fields
    payload_call = pl.pallas_call(
        functools.partial(partial_kernel, size, entries),
        out_shape=shape_of((peers, CAP * surface // 8 + HEAD // 8, 8, width)),
        in_specs=[spec(SMEM)] * 4 + [spec(VMEM)] * 5,
        out_specs=spec(VMEM),
        compiler_params=params(),
        cost_estimate=cost(2 * entries * surface * width * width, 2 * 1024 * 1024),
        name="partials",
    )
    payload = payload_call(ids, *tables, remap, pair_top, pair_back_top, far_top, far_back_top)
    payload = partner(payload, "comp", 0)
    received = lax.all_to_all(payload, "tile", split_axis=0, concat_axis=0, tiled=True)

    whole = pl.pallas_call(
        functools.partial(merge_kernel, fields, group, ring),
        out_shape=shape_of(plain.shape),
        in_specs=[spec(SMEM)] + [spec(VMEM)] * 4,
        out_specs=spec(VMEM),
        compiler_params=params(),
        cost_estimate=cost(8 * count * rows * levels * fields * width, 2 * 1024 * 1024),
        name="merge",
    )(ids, pair_mine, pair_other, far_mine, far_other)
    final = pl.pallas_call(
        functools.partial(couple_kernel, fields, group),
        out_shape=shape_of(whole.shape),
        in_specs=[spec(SMEM), spec(HBM)] + [spec(VMEM)] * 5,
        out_specs=spec(HBM),
        input_output_aliases={1: 0},
        scratch_shapes=[
            pltpu.VMEM((count + 1, surface, width), F32),
            pltpu.VMEM((count, surface, width), BF16),
            pltpu.VMEM((HEAD, width), I32),
            pltpu.SMEM((HEAD, width), I32),
            pltpu.SemaphoreType.DMA,
        ],
        compiler_params=params(),
        cost_estimate=cost(1024, 1024 * 1024),
        name="couple",
    )(ids, whole, received, pair_top, pair_other, far_top, far_other)
    return final.reshape(count, levels, fields, width).transpose(0, 2, 1, 3)[None]


def solution(mesh):
    return jax.shard_map(
        on_device,
        mesh=mesh,
        in_specs=(
            P("comp", "tile", None, None, None),
            P("comp", None, None, None),
            P("comp", None, None),
            P(),
            P("comp", "tile", None),
            P("comp", "tile", None),
            P("comp", "tile"),
            P("comp", "tile"),
            P("comp", "tile"),
            P("comp", "tile", None),
        ),
        out_specs=P("comp", "tile", None, None, None),
        check_vma=False,
    )
```

time: 109 us -> 103 us (0.945)
  waiting for transfers between devices: 43.3 us -> 37.6 us
  starting transfers between devices: 40.8 us -> 35.6 us
  local copies, waits for them, and re-layouts: 4.23 us -> 8.29 us
    ppermute x6 -> x9, starting transfers between devices: 10.6 us -> 17.2 us  [partner(): return lax.ppermute(value, axis, pairs)]
    all_to_all x1, starting transfers between devices: 9.67 us -> 4.8 us  [on_device(): lax.all_to_all(payload, 'tile', split_axis=0, concat_axis=0, tiled=True)]
    unnamed x11 -> x19, local copies, waits for them, and re-layouts: 4.23 us -> 8.29 us
    ppermute x4, starting transfers between devices: 15.2 us -> 11.1 us  [shift(): return (before, lax.ppermute(lead, 'tile', down))]
    ppermute x6 -> x9, waiting for transfers between devices: 38.3 us -> 34.7 us  [partner(): return lax.ppermute(value, axis, pairs)]
    ppermute x4, starting transfers between devices: 5.31 us -> 2.38 us  [shift(): before = lax.ppermute(last, 'tile', up)]
    ppermute x4, waiting for transfers between devices: 2.63 us -> 1.13 us  [shift(): before = lax.ppermute(last, 'tile', up)]
    pallas_call x4, Pallas kernels: 8.15 us -> 9.63 us  [run_step(): pl.pallas_call(functools.partial(step_kernel, len(pieces), size, ring, ow...]
  transfers between devices with their start and end apart: 15 -> 18, of which waited for: 8 -> 8; matrix products, arithmetic and copies ran while one was open for 1% -> 0% of each run, Pallas kernels for 12% -> 14%
where the time goes in v4:
time: 103 us
  waiting for transfers between devices  37.6 us (37%)
  starting transfers between devices  35.6 us (35%)
  Pallas kernels  20.8 us (20%)
  local copies, waits for them, and re-layouts  8.29 us (8%)
    ppermute x9, waiting for transfers between devices, partner(): return lax.ppermute(value, axis, pairs)  34.7 us
    ppermute x9, starting transfers between devices, partner(): return lax.ppermute(value, axis, pairs)  17.2 us
    ppermute x4, starting transfers between devices, shift(): return (before, lax.ppermute(lead, 'tile', down))  11.1 us
    pallas_call x4, Pallas kernels, run_step(): pl.pallas_call(functools.partial(step_kernel, len(pieces), size, ring, ow...  9.63 us
    unnamed x19, local copies, waits for them, and re-layouts  8.29 us
    all_to_all x1, starting transfers between devices, on_device(): lax.all_to_all(payload, 'tile', split_axis=0, concat_axis=0, tiled=True)  4.8 us
    pallas_call x1, Pallas kernels, on_device(): pl.pallas_call(functools.partial(merge_kernel, fields, group, ring), out_...  2.64 us
    pallas_call x1, Pallas kernels, on_device(): pl.pallas_call(functools.partial(couple_kernel, fields, group), out_shape...  2.46 us
  transfers between devices with their start and end apart: 18, of which 8 were waited for; matrix products, arithmetic and copies ran while one was open for 0% of the time, Pallas kernels for 14%

profile of v4, /device:TPU:0, one launch (start us, length us, event | category | flops | bytes accessed | tf_op | source)
XLA Modules:
  0.0 102.5 jit_solution(13101220932980849721)
XLA Ops:
  0.1 1.2 %copy-done.4 = bf16[1,16,4,60,128]{4,2,3,1,0:T(4,128)(2,1)S(1)} copy-done((bf16[1,16,4,60,128]{4,2,3,1,0:T(4,128)(2,1)S(1)}, bf16[1,16,4,60,128]{4,2,3,1,0:T(4,128)(2,1)}, u32[]{:S(2)}) %copy-start.4) | copy-done | bytes 983064
  1.3 1.0 split.1
  2.3 4.1 %collective-permute-start.5 = (bf16[16,64,128]{2,1,0:T(8,128)(2,1)S(1)}, bf16[16,64,128]{2,1,0:T(8,128)(2,1)S(1)}, u32[]{:S(2)}, u32[]{:S(2)}) collective-permute-start(bf16[16,64,128]{2,1,0:T(8,128)(2,1)S(1)} %get-tuple-element.48), channel_id=1, source_target_pairs={{0,8},{1,9},{2,10},{3,11},{4,12},{5,13},{6,14},{7,15},{8,0},{9,1},... | collective-permute-start | bytes 786440 | tf_op jit(solution)/shard_map/ppermute | solution.py:313
  6.4 1.5 %collective-permute-start.1 = (bf16[16,64,128]{2,1,0:T(8,128)(2,1)S(1)}, bf16[16,64,128]{2,1,0:T(8,128)(2,1)S(1)}, u32[]{:S(2)}, u32[]{:S(2)}) collective-permute-start(bf16[16,64,128]{2,1,0:T(8,128)(2,1)S(1)} %get-tuple-element.43), channel_id=1, source_target_pairs={{0,1},{1,0},{2,3},{3,2},{4,5},{5,4},{6,7},{7,6},{8,9},{9,8},{10,11... | collective-permute-start | bytes 786440 | tf_op jit(solution)/shard_map/ppermute | solution.py:313
  7.9 2.2 %copy-done = bf16[2,64,128,128]{3,2,1,0:T(8,128)(2,1)S(1)} copy-done((bf16[2,64,128,128]{3,2,1,0:T(8,128)(2,1)S(1)}, bf16[2,64,128,128]{3,2,1,0:T(8,128)(2,1)}, u32[]{:S(2)}) %copy-start) | copy-done | bytes 4194328
  10.1 1.6 %copy-done.1 = bf16[1,64,128,128]{3,2,1,0:T(8,128)(2,1)S(1)} copy-done((bf16[1,64,128,128]{3,2,1,0:T(8,128)(2,1)S(1)}, bf16[1,64,128,128]{3,2,1,0:T(8,128)(2,1)}, u32[]{:S(2)}) %copy-start.1) | copy-done | bytes 2097176
  12.5 1.3 %copy-done.2 = bf16[64,128,128]{2,1,0:T(8,128)(2,1)} copy-done((bf16[64,128,128]{2,1,0:T(8,128)(2,1)}, bf16[64,128,128]{2,1,0:T(8,128)(2,1)S(1)}, u32[]{:S(2)}) %copy-start.2) | copy-done | bytes 2097176
  14.1 4.2 %collective-permute-done.5.other = bf16[16,64,128]{2,1,0:T(8,128)(2,1)S(1)} collective-permute-done((bf16[16,64,128]{2,1,0:T(8,128)(2,1)S(1)}, bf16[16,64,128]{2,1,0:T(8,128)(2,1)S(1)}, u32[]{:S(2)}, u32[]{:S(2)}) %collective-permute-start.5) | collective-permute-done | bytes 262176 | tf_op jit(solution)/shard_map/ppermute | solution.py:313
  18.9 1.6 %collective-permute-start.11 = (bf16[16,64,128]{2,1,0:T(8,128)(2,1)S(1)}, bf16[16,64,128]{2,1,0:T(8,128)(2,1)}, u32[]{:S(2)}, u32[]{:S(2)}) collective-permute-start(bf16[16,64,128]{2,1,0:T(8,128)(2,1)S(1)} %get-tuple-element.65.refs_1_), channel_id=1, source_target_pairs={{0,1},{1,2},{2,3},{3,4},{4,5},{5,6},{6,7},{7,0},{8,9},{9,10},{10,1... | collective-permute-start | bytes 786440 | tf_op jit(solution)/shard_map/ppermute | solution.py:320
  20.5 2.3 %collective-permute-start.12 = (bf16[16,64,128]{2,1,0:T(8,128)(2,1)S(1)}, bf16[16,64,128]{2,1,0:T(8,128)(2,1)}, u32[]{:S(2)}, u32[]{:S(2)}) collective-permute-start(bf16[16,64,128]{2,1,0:T(8,128)(2,1)S(1)} %get-tuple-element.64.refs_0_), channel_id=1, source_target_pairs={{1,0},{2,1},{3,2},{4,3},{5,4},{6,5},{7,6},{0,7},{9,8},{10,9},{11,1... | collective-permute-start | bytes 786440 | tf_op jit(solution)/shard_map/ppermute | solution.py:321
  24.7 2.2 %collective-permute-start.2 = (bf16[16,64,128]{2,1,0:T(8,128)(2,1)S(1)}, bf16[16,64,128]{2,1,0:T(8,128)(2,1)S(1)}, u32[]{:S(2)}, u32[]{:S(2)}) collective-permute-start(bf16[16,64,128]{2,1,0:T(8,128)(2,1)S(1)} %get-tuple-element.44.refs_0_), channel_id=1, source_target_pairs={{0,8},{1,9},{2,10},{3,11},{4,12},{5,13},{6,14},{7,15},{8,0},{9,1},... | collective-permute-start | bytes 786440 | tf_op jit(solution)/shard_map/ppermute | solution.py:313
  26.9 1.7 %table.1 = (s32[192]{0:T(256)}, s32[192]{0:T(256)}) custom-call(s32[4,16]{1,0:T(4,128)} %bitcast.26, s32[4,16]{1,0:T(4,128)} %bitcast.27, s32[1,16]{1,0:T(1,128)} %refs_2_.1, s32[1,16]{1,0:T(1,128)} %refs_3_.1, s32[1,16]{1,0:T(1,128)} %bitcast.28, s32[1,16]{1,0:T(1,128)} %refs_5_.1), custom_call_target="tpu_custom_call" | custom-call | tf_op jit(solution)/shard_map/table/pallas_call | solution.py:361
  30.0 9.0 %collective-permute-done.10.mate.far = s32[192]{0:T(256)S(1)} collective-permute-done((s32[192]{0:T(256)}, s32[192]{0:T(256)S(1)}, u32[]{:S(2)}, u32[]{:S(2)}) %collective-permute-start.10) | collective-permute-done | bytes 800 | tf_op jit(solution)/shard_map/ppermute | solution.py:313
  39.4 4.2 %collective-permute-start = (s32[192]{0:T(256)}, s32[192]{0:T(256)S(1)}, u32[]{:S(2)}, u32[]{:S(2)}) collective-permute-start(s32[192]{0:T(256)} %get-tuple-element.41), channel_id=1, source_target_pairs={{0,1},{1,0},{2,3},{3,2},{4,5},{5,4},{6,7},{7,6},{8,9},{9,8},{10,11... | collective-permute-start | bytes 2312 | tf_op jit(solution)/shard_map/ppermute | solution.py:313
  44.2 2.7 %shard_map.102 = (bf16[16,64,128]{2,1,0:T(8,128)(2,1)S(1)}, bf16[16,64,128]{2,1,0:T(8,128)(2,1)S(1)}) custom-call(s32[2]{0:T(128)S(1)} %pad_add_fusion.ids, s32[192]{0:T(256)S(1)} %copy-done.5, s32[192]{0:T(256)S(1)} %collective-permute-done.10.mate.far, bf16[16,64,128]{2,1,0:T(8,128)(2,1)S(1)} %get-tuple-element.64.refs_0_, ...), custom_call_target="tpu_custom_call" | custom-call | flops 268435456 | bytes 8388608 | tf_op jit(solution)/shard_map/pallas_call | solution.py:203
  47.0 3.8 %collective-permute-start.14 = (bf16[16,64,128]{2,1,0:T(8,128)(2,1)S(1)}, bf16[16,64,128]{2,1,0:T(8,128)(2,1)S(1)}, u32[]{:S(2)}, u32[]{:S(2)}) collective-permute-start(bf16[16,64,128]{2,1,0:T(8,128)(2,1)S(1)} %get-tuple-element.66.refs_0_), channel_id=1, source_target_pairs={{1,0},{2,1},{3,2},{4,3},{5,4},{6,5},{7,6},{0,7},{9,8},{10,9},{11,1... | collective-permute-start | bytes 786440 | tf_op jit(solution)/shard_map/ppermute | solution.py:321
  50.8 2.3 %shard_map.100 = (bf16[16,64,128]{2,1,0:T(8,128)(2,1)S(1)}, bf16[16,64,128]{2,1,0:T(8,128)(2,1)S(1)}, bf16[8,64,128]{2,1,0:T(8,128)(2,1)S(1)}, bf16[8,64,128]{2,1,0:T(8,128)(2,1)S(1)}) custom-call(s32[2]{0:T(128)S(1)} %pad_add_fusion.ids, s32[192]{0:T(256)S(1)} %copy-done.5, s32[192]{0:T(256)S(1)} %collective-permute-done.mate.pair, ...), custom_call_target="tpu_custom_call" | custom-call | flops 268435456 | bytes 8388608 | tf_op jit(solution)/shard_map/pallas_call | solution.py:203
  53.3 4.7 %collective-permute-start.8 = (bf16[8,64,128]{2,1,0:T(8,128)(2,1)S(1)}, bf16[8,64,128]{2,1,0:T(8,128)(2,1)S(1)}, u32[]{:S(2)}, u32[]{:S(2)}) collective-permute-start(bf16[8,64,128]{2,1,0:T(8,128)(2,1)S(1)} %get-tuple-element.59), channel_id=1, source_target_pairs={{2,0},{3,1},{4,2},{5,3},{6,4},{7,5},{8,6},{9,7},{10,8},{11,9},{12,... | collective-permute-start | bytes 393224 | tf_op jit(solution)/shard_map/ppermute | solution.py:321
  58.0 2.3 %shard_map.103 = (bf16[16,64,128]{2,1,0:T(8,128)(2,1)S(1)}, bf16[16,64,128]{2,1,0:T(8,128)(2,1)S(1)}, bf16[16,8,128]{2,1,0:T(8,128)(2,1)S(1)}, bf16[16,8,128]{2,1,0:T(8,128)(2,1)S(1)}) custom-call(s32[2]{0:T(128)S(1)} %pad_add_fusion.ids, s32[192]{0:T(256)S(1)} %copy-done.5, s32[192]{0:T(256)S(1)} %collective-permute-done.10.mate.far, ...), custom_call_target="tpu_custom_call" | custom-call | flops 268435456 | bytes 8388608 | tf_op jit(solution)/shard_map/pallas_call | solution.py:203
  60.3 1.1 %collective-permute-done.7.refs_3_ = bf16[8,64,128]{2,1,0:T(8,128)(2,1)S(1)} collective-permute-done((bf16[8,64,128]{2,1,0:T(8,128)(2,1)S(1)}, bf16[8,64,128]{2,1,0:T(8,128)(2,1)S(1)}, u32[]{:S(2)}, u32[]{:S(2)}) %collective-permute-start.7) | collective-permute-done | bytes 131104 | tf_op jit(solution)/shard_map/ppermute | solution.py:320
  61.4 1.7 %collective-permute-done.8.refs_4_ = bf16[8,64,128]{2,1,0:T(8,128)(2,1)S(1)} collective-permute-done((bf16[8,64,128]{2,1,0:T(8,128)(2,1)S(1)}, bf16[8,64,128]{2,1,0:T(8,128)(2,1)S(1)}, u32[]{:S(2)}, u32[]{:S(2)}) %collective-permute-start.8) | collective-permute-done | bytes 131104 | tf_op jit(solution)/shard_map/ppermute | solution.py:321
  63.2 3.1 %collective-permute-done.6.refs_2_ = bf16[16,64,128]{2,1,0:T(8,128)(2,1)S(1)} collective-permute-done((bf16[16,64,128]{2,1,0:T(8,128)(2,1)S(1)}, bf16[16,64,128]{2,1,0:T(8,128)(2,1)S(1)}, u32[]{:S(2)}, u32[]{:S(2)}) %collective-permute-start.6) | collective-permute-done | bytes 262176 | tf_op jit(solution)/shard_map/ppermute | solution.py:313
  66.3 2.3 %shard_map.101 = (bf16[16,64,128]{2,1,0:T(8,128)(2,1)S(1)}, bf16[16,64,128]{2,1,0:T(8,128)(2,1)S(1)}, bf16[16,8,128]{2,1,0:T(8,128)(2,1)S(1)}, bf16[16,8,128]{2,1,0:T(8,128)(2,1)S(1)}) custom-call(s32[2]{0:T(128)S(1)} %pad_add_fusion.ids, s32[192]{0:T(256)S(1)} %copy-done.5, s32[192]{0:T(256)S(1)} %collective-permute-done.mate.pair, ...), custom_call_target="tpu_custom_call" | custom-call | flops 268435456 | bytes 8388608 | tf_op jit(solution)/shard_map/pallas_call | solution.py:203
  68.6 1.2 %partials.1 = bf16[16,9,8,128]{3,2,1,0:T(8,128)(2,1)S(1)} custom-call(s32[2]{0:T(128)S(1)} %pad_add_fusion.ids, s32[192]{0:T(256)S(1)} %copy-done.5, s32[192]{0:T(256)S(1)} %collective-permute-done.mate.pair, s32[192]{0:T(256)S(1)} %collective-permute-done.10.mate.far, bf16[64,128,128]{2,1,0:T(8,128)(2,1)S(1)} %copy-done.3, ...), custom_call_target="tpu_custom_call" | custom-call | flops 16777216 | bytes 2097152 | tf_op jit(solution)/shard_map/partials/pallas_call | solution.py:451
  69.9 1.7 %collective-permute-done.16 = bf16[16,9,8,128]{3,2,1,0:T(8,128)(2,1)} collective-permute-done((bf16[16,9,8,128]{3,2,1,0:T(8,128)(2,1)S(1)}, bf16[16,9,8,128]{3,2,1,0:T(8,128)(2,1)}, u32[]{:S(2)}, u32[]{:S(2)}) %collective-permute-start.16) | collective-permute-done | bytes 294944 | tf_op jit(solution)/shard_map/ppermute | solution.py:313
  71.6 4.8 %all-to-all-start = ((bf16[16,9,8,128]{3,2,1,0:T(8,128)(2,1)}), bf16[16,9,8,128]{3,2,1,0:T(8,128)(2,1)S(1)}, u32[]{:S(2)}, u32[]{:S(2)}) async-start(bf16[16,9,8,128]{3,2,1,0:T(8,128)(2,1)} %collective-permute-done.16), calls=%async_computation | async-start | bytes 589824 | tf_op jit(solution)/shard_map/all_to_all | solution.py:453
  76.4 1.9 %collective-permute-start.9 = (bf16[16,64,128]{2,1,0:T(8,128)(2,1)S(1)}, bf16[16,64,128]{2,1,0:T(8,128)(2,1)S(1)}, u32[]{:S(2)}, u32[]{:S(2)}) collective-permute-start(bf16[16,64,128]{2,1,0:T(8,128)(2,1)S(1)} %get-tuple-element.61), channel_id=1, source_target_pairs={{0,1},{1,0},{2,3},{3,2},{4,5},{5,4},{6,7},{7,6},{8,9},{9,8},{10,11... | collective-permute-start | bytes 786440 | tf_op jit(solution)/shard_map/ppermute | solution.py:313
  78.3 2.4 %collective-permute-start.15 = (bf16[16,64,128]{2,1,0:T(8,128)(2,1)S(1)}, bf16[16,64,128]{2,1,0:T(8,128)(2,1)S(1)}, u32[]{:S(2)}, u32[]{:S(2)}) collective-permute-start(bf16[16,64,128]{2,1,0:T(8,128)(2,1)S(1)} %get-tuple-element.69), channel_id=1, source_target_pairs={{0,8},{1,9},{2,10},{3,11},{4,12},{5,13},{6,14},{7,15},{8,0},{9,1},... | collective-permute-start | bytes 786440 | tf_op jit(solution)/shard_map/ppermute | solution.py:313
  80.7 6.6 %collective-permute-done.9.pair_other.rest_1_ = bf16[16,64,128]{2,1,0:T(8,128)(2,1)S(1)} collective-permute-done((bf16[16,64,128]{2,1,0:T(8,128)(2,1)S(1)}, bf16[16,64,128]{2,1,0:T(8,128)(2,1)S(1)}, u32[]{:S(2)}, u32[]{:S(2)}) %collective-permute-start.9) | collective-permute-done | bytes 262176 | tf_op jit(solution)/shard_map/ppermute | solution.py:313
  87.3 10.1 %collective-permute-done.15.far_other.rest_3_ = bf16[16,64,128]{2,1,0:T(8,128)(2,1)S(1)} collective-permute-done((bf16[16,64,128]{2,1,0:T(8,128)(2,1)S(1)}, bf16[16,64,128]{2,1,0:T(8,128)(2,1)S(1)}, u32[]{:S(2)}, u32[]{:S(2)}) %collective-permute-start.15) | collective-permute-done | bytes 262176 | tf_op jit(solution)/shard_map/ppermute | solution.py:313
  97.4 2.6 %merge.1.state = bf16[16,240,128]{2,1,0:T(8,128)(2,1)} custom-call(s32[2]{0:T(128)S(1)} %pad_add_fusion.ids, bf16[16,64,128]{2,1,0:T(8,128)(2,1)S(1)} %get-tuple-element.60.pair_mine, bf16[16,64,128]{2,1,0:T(8,128)(2,1)S(1)} %collective-permute-done.9.pair_other.rest_1_, bf16[16,64,128]{2,1,0:T(8,128)(2,1)S(1)} %get-tuple-element.68.far_mine, ...), custom_call_target="tpu_custom_call" | custom-call | flops 251658240 | bytes 2097152 | tf_op jit(solution)/shard_map/merge/pallas_call | solution.py:455
  100.1 2.5 %couple.1 = bf16[16,240,128]{2,1,0:T(8,128)(2,1)} custom-call(s32[2]{0:T(128)S(1)} %pad_add_fusion.ids, bf16[16,240,128]{2,1,0:T(8,128)(2,1)} %merge.1.state, bf16[16,9,8,128]{3,2,1,0:T(8,128)(2,1)S(1)} %all-to-all-done.received, bf16[16,8,128]{2,1,0:T(8,128)(2,1)S(1)} %get-tuple-element.71.rest_0_, ...), custom_call_target="tpu_custom_call", output_to_operand_aliasing={{}: (1, {})} | custom-call | flops 1024 | bytes 1048576 | tf_op jit(solution)/shard_map/couple/pallas_call | solution.py:464
  (37 shorter events, 6.4 us)
Async XLA Ops:
  0.1 1.2 %copy-start.4 = (bf16[1,16,4,60,128]{4,2,3,1,0:T(4,128)(2,1)S(1)}, bf16[1,16,4,60,128]{4,2,3,1,0:T(4,128)(2,1)}, u32[]{:S(2)}) copy-start(bf16[1,16,4,60,128]{4,2,3,1,0:T(4,128)(2,1)} %param.10) | copy-start | bytes 2949124
  2.3 16.0 %collective-permute-start.5 = (bf16[16,64,128]{2,1,0:T(8,128)(2,1)S(1)}, bf16[16,64,128]{2,1,0:T(8,128)(2,1)S(1)}, u32[]{:S(2)}, u32[]{:S(2)}) collective-permute-start(bf16[16,64,128]{2,1,0:T(8,128)(2,1)S(1)} %get-tuple-element.48), channel_id=1, source_target_pairs={{0,8},{1,9},{2,10},{3,11},{4,12},{5,13},{6,14},{7,15},{8,0},{9,1},... | collective-permute-start | bytes 786440 | tf_op jit(solution)/shard_map/ppermute | solution.py:313
  6.4 16.4 %collective-permute-start.1 = (bf16[16,64,128]{2,1,0:T(8,128)(2,1)S(1)}, bf16[16,64,128]{2,1,0:T(8,128)(2,1)S(1)}, u32[]{:S(2)}, u32[]{:S(2)}) collective-permute-start(bf16[16,64,128]{2,1,0:T(8,128)(2,1)S(1)} %get-tuple-element.43), channel_id=1, source_target_pairs={{0,1},{1,0},{2,3},{3,2},{4,5},{5,4},{6,7},{7,6},{8,9},{9,8},{10,11... | collective-permute-start | bytes 786440 | tf_op jit(solution)/shard_map/ppermute | solution.py:313
  7.9 2.2 %copy-start = (bf16[2,64,128,128]{3,2,1,0:T(8,128)(2,1)S(1)}, bf16[2,64,128,128]{3,2,1,0:T(8,128)(2,1)}, u32[]{:S(2)}) copy-start(bf16[2,64,128,128]{3,2,1,0:T(8,128)(2,1)} %remap.1) | copy-start | bytes 12582916
  10.1 1.6 %copy-start.1 = (bf16[1,64,128,128]{3,2,1,0:T(8,128)(2,1)S(1)}, bf16[1,64,128,128]{3,2,1,0:T(8,128)(2,1)}, u32[]{:S(2)}) copy-start(bf16[1,64,128,128]{3,2,1,0:T(8,128)(2,1)} %param.11) | copy-start | bytes 6291460
  11.7 2.2 %copy-start.8 = (f32[1,60,60]{2,0,1:T(1,128)S(1)}, f32[1,60,60]{2,0,1:T(1,128)}, u32[]{:S(2)}) copy-start(f32[1,60,60]{2,0,1:T(1,128)} %param.12) | copy-start | bytes 43204
  12.5 1.4 %copy-start.2 = (bf16[64,128,128]{2,1,0:T(8,128)(2,1)}, bf16[64,128,128]{2,1,0:T(8,128)(2,1)S(1)}, u32[]{:S(2)}) copy-start(bf16[64,128,128]{2,1,0:T(8,128)(2,1)S(1)} %get-tuple-element.70.weights) | copy-start | bytes 6291460
  18.9 20.5 %collective-permute-start.11 = (bf16[16,64,128]{2,1,0:T(8,128)(2,1)S(1)}, bf16[16,64,128]{2,1,0:T(8,128)(2,1)}, u32[]{:S(2)}, u32[]{:S(2)}) collective-permute-start(bf16[16,64,128]{2,1,0:T(8,128)(2,1)S(1)} %get-tuple-element.65.refs_1_), channel_id=1, source_target_pairs={{0,1},{1,2},{2,3},{3,4},{4,5},{5,6},{6,7},{7,0},{8,9},{9,10},{10,1... | collective-permute-start | bytes 786440 | tf_op jit(solution)/shard_map/ppermute | solution.py:320
  20.5 23.1 %collective-permute-start.12 = (bf16[16,64,128]{2,1,0:T(8,128)(2,1)S(1)}, bf16[16,64,128]{2,1,0:T(8,128)(2,1)}, u32[]{:S(2)}, u32[]{:S(2)}) collective-permute-start(bf16[16,64,128]{2,1,0:T(8,128)(2,1)S(1)} %get-tuple-element.64.refs_0_), channel_id=1, source_target_pairs={{1,0},{2,1},{3,2},{4,3},{5,4},{6,5},{7,6},{0,7},{9,8},{10,9},{11,1... | collective-permute-start | bytes 786440 | tf_op jit(solution)/shard_map/ppermute | solution.py:321
  23.4 0.7 copy-start.6
  24.0 0.7 copy-start.7
  24.7 26.2 %collective-permute-start.2 = (bf16[16,64,128]{2,1,0:T(8,128)(2,1)S(1)}, bf16[16,64,128]{2,1,0:T(8,128)(2,1)S(1)}, u32[]{:S(2)}, u32[]{:S(2)}) collective-permute-start(bf16[16,64,128]{2,1,0:T(8,128)(2,1)S(1)} %get-tuple-element.44.refs_0_), channel_id=1, source_target_pairs={{0,8},{1,9},{2,10},{3,11},{4,12},{5,13},{6,14},{7,15},{8,0},{9,1},... | collective-permute-start | bytes 786440 | tf_op jit(solution)/shard_map/ppermute | solution.py:313
  28.6 10.4 %collective-permute-start.10 = (s32[192]{0:T(256)}, s32[192]{0:T(256)S(1)}, u32[]{:S(2)}, u32[]{:S(2)}) collective-permute-start(s32[192]{0:T(256)} %get-tuple-element.41), channel_id=1, source_target_pairs={{0,8},{1,9},{2,10},{3,11},{4,12},{5,13},{6,14},{7,15},{8,0},{9,1},... | collective-permute-start | bytes 2312 | tf_op jit(solution)/shard_map/ppermute | solution.py:313
  29.3 21.5 %collective-permute-start.3 = (bf16[8,64,128]{2,1,0:T(8,128)(2,1)}, bf16[8,64,128]{2,1,0:T(8,128)(2,1)S(1)}, u32[]{:S(2)}, u32[]{:S(2)}) collective-permute-start(bf16[8,64,128]{2,1,0:T(8,128)(2,1)} %copy-done.7), channel_id=1, source_target_pairs={{0,2},{1,3},{2,4},{3,5},{4,6},{5,7},{6,8},{7,9},{8,10},{9,11},{10,... | collective-permute-start | bytes 393224 | tf_op jit(solution)/shard_map/ppermute | solution.py:320
  39.0 11.8 %collective-permute-start.4 = (bf16[8,64,128]{2,1,0:T(8,128)(2,1)}, bf16[8,64,128]{2,1,0:T(8,128)(2,1)S(1)}, u32[]{:S(2)}, u32[]{:S(2)}) collective-permute-start(bf16[8,64,128]{2,1,0:T(8,128)(2,1)} %copy-done.6), channel_id=1, source_target_pairs={{2,0},{3,1},{4,2},{5,3},{6,4},{7,5},{8,6},{9,7},{10,8},{11,9},{12,... | collective-permute-start | bytes 393224 | tf_op jit(solution)/shard_map/ppermute | solution.py:321
  39.4 7.7 %collective-permute-start = (s32[192]{0:T(256)}, s32[192]{0:T(256)S(1)}, u32[]{:S(2)}, u32[]{:S(2)}) collective-permute-start(s32[192]{0:T(256)} %get-tuple-element.41), channel_id=1, source_target_pairs={{0,1},{1,0},{2,3},{3,2},{4,5},{5,4},{6,7},{7,6},{8,9},{9,8},{10,11... | collective-permute-start | bytes 2312 | tf_op jit(solution)/shard_map/ppermute | solution.py:313
  43.6 0.7 copy-start.5
  46.9 11.1 %collective-permute-start.13 = (bf16[16,64,128]{2,1,0:T(8,128)(2,1)S(1)}, bf16[16,64,128]{2,1,0:T(8,128)(2,1)S(1)}, u32[]{:S(2)}, u32[]{:S(2)}) collective-permute-start(bf16[16,64,128]{2,1,0:T(8,128)(2,1)S(1)} %get-tuple-element.67.refs_1_), channel_id=1, source_target_pairs={{0,1},{1,2},{2,3},{3,4},{4,5},{5,6},{6,7},{7,0},{8,9},{9,10},{10,1... | collective-permute-start | bytes 786440 | tf_op jit(solution)/shard_map/ppermute | solution.py:320
  47.0 11.0 %collective-permute-start.14 = (bf16[16,64,128]{2,1,0:T(8,128)(2,1)S(1)}, bf16[16,64,128]{2,1,0:T(8,128)(2,1)S(1)}, u32[]{:S(2)}, u32[]{:S(2)}) collective-permute-start(bf16[16,64,128]{2,1,0:T(8,128)(2,1)S(1)} %get-tuple-element.66.refs_0_), channel_id=1, source_target_pairs={{1,0},{2,1},{3,2},{4,3},{5,4},{6,5},{7,6},{0,7},{9,8},{10,9},{11,1... | collective-permute-start | bytes 786440 | tf_op jit(solution)/shard_map/ppermute | solution.py:321
  53.2 13.1 %collective-permute-start.6 = (bf16[16,64,128]{2,1,0:T(8,128)(2,1)S(1)}, bf16[16,64,128]{2,1,0:T(8,128)(2,1)S(1)}, u32[]{:S(2)}, u32[]{:S(2)}) collective-permute-start(bf16[16,64,128]{2,1,0:T(8,128)(2,1)S(1)} %get-tuple-element.56.refs_0_), channel_id=1, source_target_pairs={{0,8},{1,9},{2,10},{3,11},{4,12},{5,13},{6,14},{7,15},{8,0},{9,1},... | collective-permute-start | bytes 786440 | tf_op jit(solution)/shard_map/ppermute | solution.py:313
  53.3 8.2 %collective-permute-start.7 = (bf16[8,64,128]{2,1,0:T(8,128)(2,1)S(1)}, bf16[8,64,128]{2,1,0:T(8,128)(2,1)S(1)}, u32[]{:S(2)}, u32[]{:S(2)}) collective-permute-start(bf16[8,64,128]{2,1,0:T(8,128)(2,1)S(1)} %get-tuple-element.58), channel_id=1, source_target_pairs={{0,2},{1,3},{2,4},{3,5},{4,6},{5,7},{6,8},{7,9},{8,10},{9,11},{10,... | collective-permute-start | bytes 393224 | tf_op jit(solution)/shard_map/ppermute | solution.py:320
  53.3 9.9 %collective-permute-start.8 = (bf16[8,64,128]{2,1,0:T(8,128)(2,1)S(1)}, bf16[8,64,128]{2,1,0:T(8,128)(2,1)S(1)}, u32[]{:S(2)}, u32[]{:S(2)}) collective-permute-start(bf16[8,64,128]{2,1,0:T(8,128)(2,1)S(1)} %get-tuple-element.59), channel_id=1, source_target_pairs={{2,0},{3,1},{4,2},{5,3},{6,4},{7,5},{8,6},{9,7},{10,8},{11,9},{12,... | collective-permute-start | bytes 393224 | tf_op jit(solution)/shard_map/ppermute | solution.py:321
  60.3 8.3 %copy-start.3 = (bf16[64,128,128]{2,1,0:T(8,128)(2,1)S(1)}, bf16[64,128,128]{2,1,0:T(8,128)(2,1)}, u32[]{:S(2)}) copy-start(bf16[64,128,128]{2,1,0:T(8,128)(2,1)} %copy-done.2) | copy-start | bytes 6291460
  69.8 1.8 %collective-permute-start.16 = (bf16[16,9,8,128]{3,2,1,0:T(8,128)(2,1)S(1)}, bf16[16,9,8,128]{3,2,1,0:T(8,128)(2,1)}, u32[]{:S(2)}, u32[]{:S(2)}) collective-permute-start(bf16[16,9,8,128]{3,2,1,0:T(8,128)(2,1)S(1)} %partials.1), channel_id=1, source_target_pairs={{0,16},{16,0},{1,17},{17,1},{2,18},{18,2},{3,19},{19,3},{4,20},{20... | collective-permute-start | bytes 884744 | tf_op jit(solution)/shard_map/ppermute | solution.py:313
  71.6 28.5 %all-to-all-start = ((bf16[16,9,8,128]{3,2,1,0:T(8,128)(2,1)}), bf16[16,9,8,128]{3,2,1,0:T(8,128)(2,1)S(1)}, u32[]{:S(2)}, u32[]{:S(2)}) async-start(bf16[16,9,8,128]{3,2,1,0:T(8,128)(2,1)} %collective-permute-done.16), calls=%async_computation | async-start | bytes 589824 | tf_op jit(solution)/shard_map/all_to_all | solution.py:453
  76.4 10.9 %collective-permute-start.9 = (bf16[16,64,128]{2,1,0:T(8,128)(2,1)S(1)}, bf16[16,64,128]{2,1,0:T(8,128)(2,1)S(1)}, u32[]{:S(2)}, u32[]{:S(2)}) collective-permute-start(bf16[16,64,128]{2,1,0:T(8,128)(2,1)S(1)} %get-tuple-element.61), channel_id=1, source_target_pairs={{0,1},{1,0},{2,3},{3,2},{4,5},{5,4},{6,7},{7,6},{8,9},{9,8},{10,11... | collective-permute-start | bytes 786440 | tf_op jit(solution)/shard_map/ppermute | solution.py:313
  78.3 19.1 %collective-permute-start.15 = (bf16[16,64,128]{2,1,0:T(8,128)(2,1)S(1)}, bf16[16,64,128]{2,1,0:T(8,128)(2,1)S(1)}, u32[]{:S(2)}, u32[]{:S(2)}) collective-permute-start(bf16[16,64,128]{2,1,0:T(8,128)(2,1)S(1)} %get-tuple-element.69), channel_id=1, source_target_pairs={{0,8},{1,9},{2,10},{3,11},{4,12},{5,13},{6,14},{7,15},{8,0},{9,1},... | collective-permute-start | bytes 786440 | tf_op jit(solution)/shard_map/ppermute | solution.py:313

commit v5 on v4

--- a/solution.py
+++ b/solution.py
@@ -46,8 +46,8 @@
     return jnp.where(source == other, 1.0, 0.0).astype(BF16)
 
 
-def expand_kernel(group, v, k_hi, k_lo):
-    rows, levels = k_hi.shape[0], v.shape[0]
+def expand_kernel(group, v, k):
+    rows, levels = k.shape[0] // 2, v.shape[0]
     shape = (rows, levels)
     level = lax.broadcasted_iota(I32, shape, 0) // group
     spread = jnp.where(level == lax.broadcasted_iota(I32, shape, 1), 1.0, 0.0).astype(BF16)
@@ -58,21 +58,26 @@
     value = v[...]
     high = value.astype(BF16)
     low = (value - high.astype(F32)).astype(BF16)
-    for part, out in ((high, k_hi), (low, k_lo)):
+    k[...] = jnp.zeros(k.shape, k.dtype)
+    for part, at in ((high, 0), (low, rows)):
         tall = jnp.dot(spread, part, preferred_element_type=F32).astype(BF16)
         full = lax.dot_general(tall, spread, (((1,), (1,)), ((), ())), preferred_element_type=F32)
-        out[...] = jnp.where(same, full, 0.0).astype(BF16)
-
-
-def load_kernel(ids, w, remap, w_out, remap_out, sems):
-    copies = [
-        pltpu.make_async_copy(w, w_out, sems.at[0]),
-        pltpu.make_async_copy(remap.at[1 - ids[1]], remap_out, sems.at[1]),
-    ]
-    for c in copies:
-        c.start()
-    for c in copies:
-        c.wait()
+        full = jnp.where(same, full, 0.0).astype(BF16)
+        k[at : at + rows, :rows] = full
+        if at == 0:
+            k[:rows, rows:] = full
+
+
+def load_kernel(w, w_out, sem):
+    copy = pltpu.make_async_copy(w, w_out, sem)
+    copy.start()
+    copy.wait()
+
+
+def load_half_kernel(ids, remap, out, sem):
+    copy = pltpu.make_async_copy(remap.at[1 - ids[1]], out, sem)
+    copy.start()
+    copy.wait()
 
 
 def table_kernel(*refs):
@@ -153,8 +158,8 @@
 
 
 def step_kernel(pieces, size, ring, own_at, writes, ids, own, mate, *refs):
-    sources, (w, k_hi, k_lo) = refs[:pieces], refs[pieces : pieces + 3]
-    outs, (pool, mid, hi, lo) = refs[pieces + 3 : -4], refs[-4:]
+    sources, (w, k) = refs[:pieces], refs[pieces : pieces + 2]
+    outs, (pool, mid, halves) = refs[pieces + 2 : -3], refs[-3:]
     at = 0
     for src in sources:
         n = src.shape[0]
@@ -162,7 +167,7 @@
         at += n
     count = len(own_at)
     stride = count // 2
-    width = w.shape[1]
+    width, height = w.shape[1], mid.shape[0]
     for b in range(count):
         total = pool[own_at[b]].astype(F32)
         x, table = b // stride, mate if b >= stride else own
@@ -173,21 +178,20 @@
         else:
             where = [pair_index(slot, x, ids[0] % 2, stride) for slot in where]
         what = [table[size + e] for e in entries]
-        for k in range(0, len(what), 2):
-            lhs = jnp.concatenate([pool[where[k]], pool[where[k + 1]]], axis=1)
-            rhs = jnp.concatenate([w[what[k]], w[what[k + 1]]], axis=0)
+        for e in range(0, len(what), 2):
+            lhs = jnp.concatenate([pool[where[e]], pool[where[e + 1]]], axis=1)
+            rhs = jnp.concatenate([w[what[e]], w[what[e + 1]]], axis=0)
             total = total + jnp.dot(lhs, rhs, preferred_element_type=F32)
         lanes = slice(b * width, (b + 1) * width)
         mid[:, lanes] = total
         top = total.astype(BF16)
-        hi[:, lanes] = top
-        lo[:, lanes] = (total - top.astype(F32)).astype(BF16)
-    big, small = k_hi[...], k_lo[...]
+        halves[:height, lanes] = top
+        halves[height:, lanes] = (total - top.astype(F32)).astype(BF16)
+    matrix = k[...]
     for b in range(0, count, 2):
         lanes = slice(b * width, (b + 2) * width)
-        mixed = jnp.dot(big, hi[:, lanes], preferred_element_type=F32)
-        mixed = mixed + jnp.dot(big, lo[:, lanes], preferred_element_type=F32)
-        mixed = mixed + jnp.dot(small, hi[:, lanes], preferred_element_type=F32)
+        mixed = jnp.dot(matrix, halves[:, lanes], preferred_element_type=F32)
+        mixed = mixed[:height] + mixed[height:]
         new = (mid[:, lanes] + jnp.tanh(mixed)).astype(BF16)
         for i in range(2):
             for out, place, rows in writes[b + i]:
@@ -203,17 +207,16 @@
     return pl.pallas_call(
         functools.partial(step_kernel, len(pieces), size, ring, own_at, writes),
         out_shape=[shape_of(o) for o in outs],
-        in_specs=[spec(SMEM)] * 3 + [spec(VMEM)] * len(pieces) + [spec(VMEM)] * 3,
+        in_specs=[spec(SMEM)] * 3 + [spec(VMEM)] * len(pieces) + [spec(VMEM)] * 2,
         out_specs=[spec(VMEM)] * len(outs),
         scratch_shapes=[
             pltpu.VMEM((total, rows, width), BF16),
             pltpu.VMEM((rows, count * width), F32),
-            pltpu.VMEM((rows, count * width), BF16),
-            pltpu.VMEM((rows, count * width), BF16),
+            pltpu.VMEM((2 * rows, count * width), BF16),
         ],
         compiler_params=params(),
         cost_estimate=cost(4 * 2 * count * rows * width * width, 8 * 1024 * 1024),
-    )(*tables, *pieces, w, *k)
+    )(*tables, *pieces, w, k)
 
 
 def partial_kernel(size, entries, ids, own, pair, far, weights, *rest):
@@ -259,7 +262,7 @@
 
 
 def couple_kernel(fields, group, ids, state, received, *rest):
-    pair_mine, pair_other, far_mine, far_other, out, total, top, found, targets, sem = rest
+    pair_mine, pair_other, far_mine, far_other, out, *sums, top, found, targets, sem = rest
     del state
     count, rows, width = top.shape
     peers = received.shape[0]
@@ -269,11 +272,11 @@
     found[...] = jnp.sum(heads, axis=0).astype(I32)
     copy = pltpu.make_async_copy(found, targets, sem)
     copy.start()
-    total[...] = jnp.zeros(total.shape, F32)
+    for total in sums:
+        total[...] = jnp.zeros(total.shape, F32)
     copy.wait()
     for p in range(peers):
-        close = part * (p % 2)
-        side = 2 * part if p < peers // 2 else 3 * part
+        close, side = sums[p % 2], sums[2 if p < peers // 2 else 3]
         for i in range(3 * CAP):
             q = p * 3 * CAP + i
             t = targets[q // width, q % width]
@@ -281,13 +284,13 @@
             if kind == 0:
                 got = received[p, 2 * thin * at : 2 * thin * (at + 1)].astype(F32)
                 got = got.reshape(2 * part, width)
-                total[t, close : close + part] = total[t, close : close + part] + got[:part]
-                total[t, side : side + part] = total[t, side : side + part] + got[part:]
+                close[t] = close[t] + got[:part]
+                side[t] = side[t] + got[part:]
             else:
                 base = CAP * thin * (1 + kind) + at * thin
                 got = received[p, base : base + thin].astype(F32).reshape(part, width)
                 here = close if kind == 1 else side
-                total[t, here : here + part] = total[t, here : here + part] + got
+                here[t] = here[t] + got
     shape = (rows, rows)
     have = lax.broadcasted_iota(I32, shape, 1)
     field = have // part * group + have % part % group
@@ -300,7 +303,8 @@
         for first, mine, other in ((even, pair_mine, pair_other), (is_low, far_mine, far_other)):
             here, there = mine[g].astype(F32), other[g, :part].astype(F32)
             base += [jnp.where(first, here, there), jnp.where(first, there, here)]
-        new = (jnp.concatenate(base, axis=0) + total[g + 1]).astype(BF16)
+        new = [a + total[g + 1] for a, total in zip(base, sums)]
+        new = jnp.concatenate(new, axis=0).astype(BF16)
         top[g] = jnp.dot(pick, new, preferred_element_type=F32).astype(BF16)
     copy = pltpu.make_async_copy(top, out.at[:, pl.ds(0, rows)], sem)
     copy.start()
@@ -380,30 +384,31 @@
             name="pack",
         )(ids, mine, other)
 
-    pair_leads, pair_lasts, up, down = pack(pair_mine, pair_other, 2)
     expand = pl.pallas_call(
         functools.partial(expand_kernel, group),
-        out_shape=[shape_of((rows, rows))] * 2,
+        out_shape=shape_of((2 * rows, 2 * rows)),
         in_specs=[spec(VMEM)],
-        out_specs=[spec(VMEM)] * 2,
+        out_specs=spec(VMEM),
         compiler_params=params(),
         cost_estimate=cost(8 * rows * rows * levels, 1024 * 1024),
         name="expand",
     )
     load = pl.pallas_call(
         load_kernel,
-        out_shape=[shape_of(w.shape), shape_of(remap_weights.shape[1:])],
-        in_specs=[spec(SMEM)] + [spec(HBM)] * 2,
-        out_specs=[spec(VMEM)] * 2,
-        scratch_shapes=[pltpu.SemaphoreType.DMA((2,))],
-        compiler_params=params(),
-        cost_estimate=cost(1024, 8 * 1024 * 1024),
+        out_shape=shape_of(w.shape),
+        in_specs=[spec(HBM)],
+        out_specs=spec(VMEM),
+        scratch_shapes=[pltpu.SemaphoreType.DMA],
+        compiler_params=params(),
+        cost_estimate=cost(1024, 4 * 1024 * 1024),
         name="load",
     )
     k = expand(vertical[0])
-    w, remap = load(ids, w, remap_weights)
-    far_other, k, w, remap = lax.optimization_barrier((far_other, k, w, remap))
+    w = load(w)
+    pair_other, k, w = lax.optimization_barrier((pair_other, k, w))
     tables = (own_table, pair_table, far_table)
+
+    pair_leads, pair_lasts, up, down = pack(pair_mine, pair_other, 2)
     leads, lasts = pack(far_mine, far_other, 0)
 
     tail = 2 * HALO
@@ -429,6 +434,18 @@
                 size, 0, pair_ids, pair_pieces, w, k, places, [body, body, edge, edge], onward
             )
             leads, lasts = run_step(size, ring, far_ids, far_pieces, w, k, places, [body, body], onward)
+    load_half = pl.pallas_call(
+        load_half_kernel,
+        out_shape=shape_of(remap_weights.shape[1:]),
+        in_specs=[spec(SMEM), spec(HBM)],
+        out_specs=spec(VMEM),
+        scratch_shapes=[pltpu.SemaphoreType.DMA],
+        compiler_params=params(),
+        cost_estimate=cost(1024, 4 * 1024 * 1024),
+        name="load",
+    )
+    remap = load_half(ids, remap_weights)
+    tables, remap = lax.optimization_barrier((tables, remap))
     pair_mine, pair_back, pair_top, pair_back_top = run_step(
         size, 0, (ids, tables[0], tables[1]), pair_pieces, w, k, places, ended, finish
     )
@@ -468,7 +485,7 @@
         out_specs=spec(HBM),
         input_output_aliases={1: 0},
         scratch_shapes=[
-            pltpu.VMEM((count + 1, surface, width), F32),
+            *([pltpu.VMEM((count + 1, part, width), F32)] * 4),
             pltpu.VMEM((count, surface, width), BF16),
             pltpu.VMEM((HEAD, width), I32),
             pltpu.SMEM((HEAD, width), I32),

time: 103 us -> 105 us (1.019)
  waiting for transfers between devices: 37.6 us -> 44.4 us
  local copies, waits for them, and re-layouts: 8.29 us -> 5.35 us
    ppermute x9, waiting for transfers between devices: 34.7 us -> 41.1 us  [partner(): return lax.ppermute(value, axis, pairs)]
    unnamed x19 -> x15, local copies, waits for them, and re-layouts: 8.29 us -> 5.35 us
  transfers between devices with their start and end apart: 18 -> 18, of which waited for: 8 -> 8; matrix products, arithmetic and copies ran while one was open for 0% -> 0% of each run, Pallas kernels for 14% -> 13%
where the time goes in v5:
time: 105 us
  waiting for transfers between devices  44.4 us (42%)
  starting transfers between devices  34.7 us (33%)
  Pallas kernels  20.4 us (19%)
  local copies, waits for them, and re-layouts  5.35 us (5%)
    ppermute x9, waiting for transfers between devices, partner(): return lax.ppermute(value, axis, pairs)  41.1 us
    ppermute x9, starting transfers between devices, partner(): return lax.ppermute(value, axis, pairs)  16.6 us
    ppermute x4, starting transfers between devices, shift(): return (before, lax.ppermute(lead, 'tile', down))  11.2 us
    pallas_call x4, Pallas kernels, run_step(): pl.pallas_call(functools.partial(step_kernel, len(pieces), size, ring, ow...  9.3 us
    unnamed x15, local copies, waits for them, and re-layouts  5.35 us
    all_to_all x1, starting transfers between devices, on_device(): lax.all_to_all(payload, 'tile', split_axis=0, concat_axis=0, tiled=True)  4.54 us
    pallas_call x1, Pallas kernels, on_device(): pl.pallas_call(functools.partial(merge_kernel, fields, group, ring), out_...  2.64 us
    ppermute x4, waiting for transfers between devices, shift(): return (before, lax.ppermute(lead, 'tile', down))  2.4 us
  transfers between devices with their start and end apart: 18, of which 8 were waited for; matrix products, arithmetic and copies ran while one was open for 0% of the time, Pallas kernels for 13%

profile of v5, /device:TPU:0, one launch (start us, length us, event | category | flops | bytes accessed | tf_op | source)
XLA Modules:
  0.0 105.1 jit_solution(963679259352170787)
XLA Ops:
  0.1 1.2 %copy-done.2 = bf16[1,16,4,60,128]{4,2,3,1,0:T(4,128)(2,1)S(1)} copy-done((bf16[1,16,4,60,128]{4,2,3,1,0:T(4,128)(2,1)S(1)}, bf16[1,16,4,60,128]{4,2,3,1,0:T(4,128)(2,1)}, u32[]{:S(2)}) %copy-start.2) | copy-done | bytes 983064
  1.3 1.0 split.1
  2.3 4.1 %collective-permute-start.10 = (bf16[16,64,128]{2,1,0:T(8,128)(2,1)S(1)}, bf16[16,64,128]{2,1,0:T(8,128)(2,1)S(1)}, u32[]{:S(2)}, u32[]{:S(2)}) collective-permute-start(bf16[16,64,128]{2,1,0:T(8,128)(2,1)S(1)} %get-tuple-element.59), channel_id=1, source_target_pairs={{0,8},{1,9},{2,10},{3,11},{4,12},{5,13},{6,14},{7,15},{8,0},{9,1},... | collective-permute-start | bytes 786440 | tf_op jit(solution)/shard_map/ppermute | solution.py:317
  6.4 1.5 %collective-permute-start.2 = (bf16[16,64,128]{2,1,0:T(8,128)(2,1)S(1)}, bf16[16,64,128]{2,1,0:T(8,128)(2,1)S(1)}, u32[]{:S(2)}, u32[]{:S(2)}) collective-permute-start(bf16[16,64,128]{2,1,0:T(8,128)(2,1)S(1)} %get-tuple-element.43), channel_id=1, source_target_pairs={{0,1},{1,0},{2,3},{3,2},{4,5},{5,4},{6,7},{7,6},{8,9},{9,8},{10,11... | collective-permute-start | bytes 786440 | tf_op jit(solution)/shard_map/ppermute | solution.py:317
  7.9 10.4 %collective-permute-done.10.other = bf16[16,64,128]{2,1,0:T(8,128)(2,1)S(1)} collective-permute-done((bf16[16,64,128]{2,1,0:T(8,128)(2,1)S(1)}, bf16[16,64,128]{2,1,0:T(8,128)(2,1)S(1)}, u32[]{:S(2)}, u32[]{:S(2)}) %collective-permute-start.10) | collective-permute-done | bytes 262176 | tf_op jit(solution)/shard_map/ppermute | solution.py:317
  18.9 1.6 %collective-permute-start.11 = (bf16[16,64,128]{2,1,0:T(8,128)(2,1)S(1)}, bf16[16,64,128]{2,1,0:T(8,128)(2,1)}, u32[]{:S(2)}, u32[]{:S(2)}) collective-permute-start(bf16[16,64,128]{2,1,0:T(8,128)(2,1)S(1)} %get-tuple-element.61.refs_1_), channel_id=1, source_target_pairs={{0,1},{1,2},{2,3},{3,4},{4,5},{5,6},{6,7},{7,0},{8,9},{9,10},{10,1... | collective-permute-start | bytes 786440 | tf_op jit(solution)/shard_map/ppermute | solution.py:324
  20.5 2.3 %collective-permute-start.12 = (bf16[16,64,128]{2,1,0:T(8,128)(2,1)S(1)}, bf16[16,64,128]{2,1,0:T(8,128)(2,1)}, u32[]{:S(2)}, u32[]{:S(2)}) collective-permute-start(bf16[16,64,128]{2,1,0:T(8,128)(2,1)S(1)} %get-tuple-element.60.refs_0_), channel_id=1, source_target_pairs={{1,0},{2,1},{3,2},{4,3},{5,4},{6,5},{7,6},{0,7},{9,8},{10,9},{11,1... | collective-permute-start | bytes 786440 | tf_op jit(solution)/shard_map/ppermute | solution.py:325
  22.8 1.6 %copy-done.1 = bf16[1,64,128,128]{3,2,1,0:T(8,128)(2,1)S(1)} copy-done((bf16[1,64,128,128]{3,2,1,0:T(8,128)(2,1)S(1)}, bf16[1,64,128,128]{3,2,1,0:T(8,128)(2,1)}, u32[]{:S(2)}) %copy-start.1) | copy-done | bytes 2097176
  27.3 2.2 %collective-permute-start.3 = (bf16[16,64,128]{2,1,0:T(8,128)(2,1)S(1)}, bf16[16,64,128]{2,1,0:T(8,128)(2,1)S(1)}, u32[]{:S(2)}, u32[]{:S(2)}) collective-permute-start(bf16[16,64,128]{2,1,0:T(8,128)(2,1)S(1)} %get-tuple-element.45.refs_0_), channel_id=1, source_target_pairs={{0,8},{1,9},{2,10},{3,11},{4,12},{5,13},{6,14},{7,15},{8,0},{9,1},... | collective-permute-start | bytes 786440 | tf_op jit(solution)/shard_map/ppermute | solution.py:317
  29.6 1.7 %table.1 = (s32[192]{0:T(256)}, s32[192]{0:T(256)}) custom-call(s32[4,16]{1,0:T(4,128)} %bitcast.26, s32[4,16]{1,0:T(4,128)} %bitcast.27, s32[1,16]{1,0:T(1,128)} %refs_2_.1, s32[1,16]{1,0:T(1,128)} %refs_3_.1, s32[1,16]{1,0:T(1,128)} %bitcast.28, s32[1,16]{1,0:T(1,128)} %refs_5_.1), custom_call_target="tpu_custom_call" | custom-call | tf_op jit(solution)/shard_map/table/pallas_call | solution.py:365
  31.2 0.8 collective-permute-start.1
  32.7 8.9 %collective-permute-done.1.mate.far = s32[192]{0:T(256)S(1)} collective-permute-done((s32[192]{0:T(256)}, s32[192]{0:T(256)S(1)}, u32[]{:S(2)}, u32[]{:S(2)}) %collective-permute-start.1) | collective-permute-done | bytes 800 | tf_op jit(solution)/shard_map/ppermute | solution.py:317
  42.0 3.6 %collective-permute-start = (s32[192]{0:T(256)}, s32[192]{0:T(256)S(1)}, u32[]{:S(2)}, u32[]{:S(2)}) collective-permute-start(s32[192]{0:T(256)} %get-tuple-element.39), channel_id=1, source_target_pairs={{0,1},{1,0},{2,3},{3,2},{4,5},{5,4},{6,7},{7,6},{8,9},{9,8},{10,11... | collective-permute-start | bytes 2312 | tf_op jit(solution)/shard_map/ppermute | solution.py:317
  46.3 2.8 %shard_map.102 = (bf16[16,64,128]{2,1,0:T(8,128)(2,1)S(1)}, bf16[16,64,128]{2,1,0:T(8,128)(2,1)S(1)}) custom-call(s32[2]{0:T(128)S(1)} %pad_add_fusion.ids, s32[192]{0:T(256)S(1)} %copy-done.3, s32[192]{0:T(256)S(1)} %collective-permute-done.1.mate.far, bf16[16,64,128]{2,1,0:T(8,128)(2,1)S(1)} %get-tuple-element.60.refs_0_, ...), custom_call_target="tpu_custom_call" | custom-call | flops 268435456 | bytes 8388608 | tf_op jit(solution)/shard_map/pallas_call | solution.py:207
  49.1 3.8 %collective-permute-start.14 = (bf16[16,64,128]{2,1,0:T(8,128)(2,1)S(1)}, bf16[16,64,128]{2,1,0:T(8,128)(2,1)S(1)}, u32[]{:S(2)}, u32[]{:S(2)}) collective-permute-start(bf16[16,64,128]{2,1,0:T(8,128)(2,1)S(1)} %get-tuple-element.62.refs_0_), channel_id=1, source_target_pairs={{1,0},{2,1},{3,2},{4,3},{5,4},{6,5},{7,6},{0,7},{9,8},{10,9},{11,1... | collective-permute-start | bytes 786440 | tf_op jit(solution)/shard_map/ppermute | solution.py:325
  52.9 2.2 %shard_map.100 = (bf16[16,64,128]{2,1,0:T(8,128)(2,1)S(1)}, bf16[16,64,128]{2,1,0:T(8,128)(2,1)S(1)}, bf16[8,64,128]{2,1,0:T(8,128)(2,1)S(1)}, bf16[8,64,128]{2,1,0:T(8,128)(2,1)S(1)}) custom-call(s32[2]{0:T(128)S(1)} %pad_add_fusion.ids, s32[192]{0:T(256)S(1)} %copy-done.3, s32[192]{0:T(256)S(1)} %collective-permute-done.mate.pair, ...), custom_call_target="tpu_custom_call" | custom-call | flops 268435456 | bytes 8388608 | tf_op jit(solution)/shard_map/pallas_call | solution.py:207
  55.3 4.7 %collective-permute-start.8 = (bf16[8,64,128]{2,1,0:T(8,128)(2,1)S(1)}, bf16[8,64,128]{2,1,0:T(8,128)(2,1)S(1)}, u32[]{:S(2)}, u32[]{:S(2)}) collective-permute-start(bf16[8,64,128]{2,1,0:T(8,128)(2,1)S(1)} %get-tuple-element.54), channel_id=1, source_target_pairs={{2,0},{3,1},{4,2},{5,3},{6,4},{7,5},{8,6},{9,7},{10,8},{11,9},{12,... | collective-permute-start | bytes 393224 | tf_op jit(solution)/shard_map/ppermute | solution.py:325
  60.0 0.7 load.2.weights
  60.8 2.1 %shard_map.103 = (bf16[16,64,128]{2,1,0:T(8,128)(2,1)S(1)}, bf16[16,64,128]{2,1,0:T(8,128)(2,1)S(1)}, bf16[16,8,128]{2,1,0:T(8,128)(2,1)S(1)}, bf16[16,8,128]{2,1,0:T(8,128)(2,1)S(1)}) custom-call(s32[2]{0:T(128)S(1)} %pad_add_fusion.ids, s32[192]{0:T(256)S(1)} %copy-done.3, s32[192]{0:T(256)S(1)} %collective-permute-done.1.mate.far, ...), custom_call_target="tpu_custom_call" | custom-call | flops 268435456 | bytes 8388608 | tf_op jit(solution)/shard_map/pallas_call | solution.py:207
  62.9 0.9 collective-permute-done.7.refs_3_
  63.8 2.4 %collective-permute-done.8.refs_4_ = bf16[8,64,128]{2,1,0:T(8,128)(2,1)S(1)} collective-permute-done((bf16[8,64,128]{2,1,0:T(8,128)(2,1)S(1)}, bf16[8,64,128]{2,1,0:T(8,128)(2,1)S(1)}, u32[]{:S(2)}, u32[]{:S(2)}) %collective-permute-start.8) | collective-permute-done | bytes 131104 | tf_op jit(solution)/shard_map/ppermute | solution.py:325
  66.2 3.3 %collective-permute-done.6.refs_2_ = bf16[16,64,128]{2,1,0:T(8,128)(2,1)S(1)} collective-permute-done((bf16[16,64,128]{2,1,0:T(8,128)(2,1)S(1)}, bf16[16,64,128]{2,1,0:T(8,128)(2,1)S(1)}, u32[]{:S(2)}, u32[]{:S(2)}) %collective-permute-start.6) | collective-permute-done | bytes 262176 | tf_op jit(solution)/shard_map/ppermute | solution.py:317
  69.5 2.2 %shard_map.101 = (bf16[16,64,128]{2,1,0:T(8,128)(2,1)S(1)}, bf16[16,64,128]{2,1,0:T(8,128)(2,1)S(1)}, bf16[16,8,128]{2,1,0:T(8,128)(2,1)S(1)}, bf16[16,8,128]{2,1,0:T(8,128)(2,1)S(1)}) custom-call(s32[2]{0:T(128)S(1)} %pad_add_fusion.ids, s32[192]{0:T(256)S(1)} %copy-done.3, s32[192]{0:T(256)S(1)} %collective-permute-done.mate.pair, ...), custom_call_target="tpu_custom_call" | custom-call | flops 268435456 | bytes 8388608 | tf_op jit(solution)/shard_map/pallas_call | solution.py:207
  71.7 1.2 %partials.1 = bf16[16,9,8,128]{3,2,1,0:T(8,128)(2,1)S(1)} custom-call(s32[2]{0:T(128)S(1)} %pad_add_fusion.ids, s32[192]{0:T(256)S(1)} %copy-done.3, s32[192]{0:T(256)S(1)} %collective-permute-done.mate.pair, s32[192]{0:T(256)S(1)} %collective-permute-done.1.mate.far, bf16[64,128,128]{2,1,0:T(8,128)(2,1)S(1)} %load.2.weights, ...), custom_call_target="tpu_custom_call" | custom-call | flops 16777216 | bytes 2097152 | tf_op jit(solution)/shard_map/partials/pallas_call | solution.py:468
  73.0 1.7 %collective-permute-done.16 = bf16[16,9,8,128]{3,2,1,0:T(8,128)(2,1)} collective-permute-done((bf16[16,9,8,128]{3,2,1,0:T(8,128)(2,1)S(1)}, bf16[16,9,8,128]{3,2,1,0:T(8,128)(2,1)}, u32[]{:S(2)}, u32[]{:S(2)}) %collective-permute-start.16) | collective-permute-done | bytes 294944 | tf_op jit(solution)/shard_map/ppermute | solution.py:317
  74.7 4.5 %all-to-all-start = ((bf16[16,9,8,128]{3,2,1,0:T(8,128)(2,1)}), bf16[16,9,8,128]{3,2,1,0:T(8,128)(2,1)S(1)}, u32[]{:S(2)}, u32[]{:S(2)}) async-start(bf16[16,9,8,128]{3,2,1,0:T(8,128)(2,1)} %collective-permute-done.16), calls=%async_computation | async-start | bytes 589824 | tf_op jit(solution)/shard_map/all_to_all | solution.py:470
  79.2 1.9 %collective-permute-start.9 = (bf16[16,64,128]{2,1,0:T(8,128)(2,1)S(1)}, bf16[16,64,128]{2,1,0:T(8,128)(2,1)S(1)}, u32[]{:S(2)}, u32[]{:S(2)}) collective-permute-start(bf16[16,64,128]{2,1,0:T(8,128)(2,1)S(1)} %get-tuple-element.56), channel_id=1, source_target_pairs={{0,1},{1,0},{2,3},{3,2},{4,5},{5,4},{6,7},{7,6},{8,9},{9,8},{10,11... | collective-permute-start | bytes 786440 | tf_op jit(solution)/shard_map/ppermute | solution.py:317
  81.2 2.4 %collective-permute-start.15 = (bf16[16,64,128]{2,1,0:T(8,128)(2,1)S(1)}, bf16[16,64,128]{2,1,0:T(8,128)(2,1)S(1)}, u32[]{:S(2)}, u32[]{:S(2)}) collective-permute-start(bf16[16,64,128]{2,1,0:T(8,128)(2,1)S(1)} %get-tuple-element.65), channel_id=1, source_target_pairs={{0,8},{1,9},{2,10},{3,11},{4,12},{5,13},{6,14},{7,15},{8,0},{9,1},... | collective-permute-start | bytes 786440 | tf_op jit(solution)/shard_map/ppermute | solution.py:317
  83.5 6.6 %collective-permute-done.9.pair_other.rest_1_ = bf16[16,64,128]{2,1,0:T(8,128)(2,1)S(1)} collective-permute-done((bf16[16,64,128]{2,1,0:T(8,128)(2,1)S(1)}, bf16[16,64,128]{2,1,0:T(8,128)(2,1)S(1)}, u32[]{:S(2)}, u32[]{:S(2)}) %collective-permute-start.9) | collective-permute-done | bytes 262176 | tf_op jit(solution)/shard_map/ppermute | solution.py:317
  90.2 10.1 %collective-permute-done.15.far_other.rest_3_ = bf16[16,64,128]{2,1,0:T(8,128)(2,1)S(1)} collective-permute-done((bf16[16,64,128]{2,1,0:T(8,128)(2,1)S(1)}, bf16[16,64,128]{2,1,0:T(8,128)(2,1)S(1)}, u32[]{:S(2)}, u32[]{:S(2)}) %collective-permute-start.15) | collective-permute-done | bytes 262176 | tf_op jit(solution)/shard_map/ppermute | solution.py:317
  100.2 2.6 %merge.1.state = bf16[16,240,128]{2,1,0:T(8,128)(2,1)} custom-call(s32[2]{0:T(128)S(1)} %pad_add_fusion.ids, bf16[16,64,128]{2,1,0:T(8,128)(2,1)S(1)} %get-tuple-element.55.pair_mine, bf16[16,64,128]{2,1,0:T(8,128)(2,1)S(1)} %collective-permute-done.9.pair_other.rest_1_, bf16[16,64,128]{2,1,0:T(8,128)(2,1)S(1)} %get-tuple-element.64.far_mine, ...), custom_call_target="tpu_custom_call" | custom-call | flops 251658240 | bytes 2097152 | tf_op jit(solution)/shard_map/merge/pallas_call | solution.py:472
  102.9 2.2 %couple.1 = bf16[16,240,128]{2,1,0:T(8,128)(2,1)} custom-call(s32[2]{0:T(128)S(1)} %pad_add_fusion.ids, bf16[16,240,128]{2,1,0:T(8,128)(2,1)} %merge.1.state, bf16[16,9,8,128]{3,2,1,0:T(8,128)(2,1)S(1)} %all-to-all-done.received, bf16[16,8,128]{2,1,0:T(8,128)(2,1)S(1)} %get-tuple-element.67.rest_0_, ...), custom_call_target="tpu_custom_call", output_to_operand_aliasing={{}: (1, {})} | custom-call | flops 1024 | bytes 1048576 | tf_op jit(solution)/shard_map/couple/pallas_call | solution.py:481
  (34 shorter events, 5.7 us)
Async XLA Ops:
  0.1 1.2 %copy-start.2 = (bf16[1,16,4,60,128]{4,2,3,1,0:T(4,128)(2,1)S(1)}, bf16[1,16,4,60,128]{4,2,3,1,0:T(4,128)(2,1)}, u32[]{:S(2)}) copy-start(bf16[1,16,4,60,128]{4,2,3,1,0:T(4,128)(2,1)} %param.10) | copy-start | bytes 2949124
  2.3 16.0 %collective-permute-start.10 = (bf16[16,64,128]{2,1,0:T(8,128)(2,1)S(1)}, bf16[16,64,128]{2,1,0:T(8,128)(2,1)S(1)}, u32[]{:S(2)}, u32[]{:S(2)}) collective-permute-start(bf16[16,64,128]{2,1,0:T(8,128)(2,1)S(1)} %get-tuple-element.59), channel_id=1, source_target_pairs={{0,8},{1,9},{2,10},{3,11},{4,12},{5,13},{6,14},{7,15},{8,0},{9,1},... | collective-permute-start | bytes 786440 | tf_op jit(solution)/shard_map/ppermute | solution.py:317
  6.4 19.0 %collective-permute-start.2 = (bf16[16,64,128]{2,1,0:T(8,128)(2,1)S(1)}, bf16[16,64,128]{2,1,0:T(8,128)(2,1)S(1)}, u32[]{:S(2)}, u32[]{:S(2)}) collective-permute-start(bf16[16,64,128]{2,1,0:T(8,128)(2,1)S(1)} %get-tuple-element.43), channel_id=1, source_target_pairs={{0,1},{1,0},{2,3},{3,2},{4,5},{5,4},{6,7},{7,6},{8,9},{9,8},{10,11... | collective-permute-start | bytes 786440 | tf_op jit(solution)/shard_map/ppermute | solution.py:317
  18.9 23.1 %collective-permute-start.11 = (bf16[16,64,128]{2,1,0:T(8,128)(2,1)S(1)}, bf16[16,64,128]{2,1,0:T(8,128)(2,1)}, u32[]{:S(2)}, u32[]{:S(2)}) collective-permute-start(bf16[16,64,128]{2,1,0:T(8,128)(2,1)S(1)} %get-tuple-element.61.refs_1_), channel_id=1, source_target_pairs={{0,1},{1,2},{2,3},{3,4},{4,5},{5,6},{6,7},{7,0},{8,9},{9,10},{10,1... | collective-permute-start | bytes 786440 | tf_op jit(solution)/shard_map/ppermute | solution.py:324
  20.5 25.1 %collective-permute-start.12 = (bf16[16,64,128]{2,1,0:T(8,128)(2,1)S(1)}, bf16[16,64,128]{2,1,0:T(8,128)(2,1)}, u32[]{:S(2)}, u32[]{:S(2)}) collective-permute-start(bf16[16,64,128]{2,1,0:T(8,128)(2,1)S(1)} %get-tuple-element.60.refs_0_), channel_id=1, source_target_pairs={{1,0},{2,1},{3,2},{4,3},{5,4},{6,5},{7,6},{0,7},{9,8},{10,9},{11,1... | collective-permute-start | bytes 786440 | tf_op jit(solution)/shard_map/ppermute | solution.py:325
  22.8 1.6 %copy-start.1 = (bf16[1,64,128,128]{3,2,1,0:T(8,128)(2,1)S(1)}, bf16[1,64,128,128]{3,2,1,0:T(8,128)(2,1)}, u32[]{:S(2)}) copy-start(bf16[1,64,128,128]{3,2,1,0:T(8,128)(2,1)} %param.11) | copy-start | bytes 6291460
  24.4 0.8 copy-start.6
  26.0 0.6 copy-start.4
  26.7 0.7 copy-start.5
  27.3 25.6 %collective-permute-start.3 = (bf16[16,64,128]{2,1,0:T(8,128)(2,1)S(1)}, bf16[16,64,128]{2,1,0:T(8,128)(2,1)S(1)}, u32[]{:S(2)}, u32[]{:S(2)}) collective-permute-start(bf16[16,64,128]{2,1,0:T(8,128)(2,1)S(1)} %get-tuple-element.45.refs_0_), channel_id=1, source_target_pairs={{0,8},{1,9},{2,10},{3,11},{4,12},{5,13},{6,14},{7,15},{8,0},{9,1},... | collective-permute-start | bytes 786440 | tf_op jit(solution)/shard_map/ppermute | solution.py:317
  31.2 10.4 %collective-permute-start.1 = (s32[192]{0:T(256)}, s32[192]{0:T(256)S(1)}, u32[]{:S(2)}, u32[]{:S(2)}) collective-permute-start(s32[192]{0:T(256)} %get-tuple-element.39), channel_id=1, source_target_pairs={{0,8},{1,9},{2,10},{3,11},{4,12},{5,13},{6,14},{7,15},{8,0},{9,1},... | collective-permute-start | bytes 2312 | tf_op jit(solution)/shard_map/ppermute | solution.py:317
  32.0 20.9 %collective-permute-start.4 = (bf16[8,64,128]{2,1,0:T(8,128)(2,1)}, bf16[8,64,128]{2,1,0:T(8,128)(2,1)S(1)}, u32[]{:S(2)}, u32[]{:S(2)}) collective-permute-start(bf16[8,64,128]{2,1,0:T(8,128)(2,1)} %copy-done.5), channel_id=1, source_target_pairs={{0,2},{1,3},{2,4},{3,5},{4,6},{5,7},{6,8},{7,9},{8,10},{9,11},{10,... | collective-permute-start | bytes 393224 | tf_op jit(solution)/shard_map/ppermute | solution.py:324
  41.6 11.3 %collective-permute-start.5 = (bf16[8,64,128]{2,1,0:T(8,128)(2,1)}, bf16[8,64,128]{2,1,0:T(8,128)(2,1)S(1)}, u32[]{:S(2)}, u32[]{:S(2)}) collective-permute-start(bf16[8,64,128]{2,1,0:T(8,128)(2,1)} %copy-done.4), channel_id=1, source_target_pairs={{2,0},{3,1},{4,2},{5,3},{6,4},{7,5},{8,6},{9,7},{10,8},{11,9},{12,... | collective-permute-start | bytes 393224 | tf_op jit(solution)/shard_map/ppermute | solution.py:325
  42.0 7.1 %collective-permute-start = (s32[192]{0:T(256)}, s32[192]{0:T(256)S(1)}, u32[]{:S(2)}, u32[]{:S(2)}) collective-permute-start(s32[192]{0:T(256)} %get-tuple-element.39), channel_id=1, source_target_pairs={{0,1},{1,0},{2,3},{3,2},{4,5},{5,4},{6,7},{7,6},{8,9},{9,8},{10,11... | collective-permute-start | bytes 2312 | tf_op jit(solution)/shard_map/ppermute | solution.py:317
  45.6 0.7 copy-start.3
  46.3 13.7 %copy-start = (bf16[2,64,128,128]{3,2,1,0:T(8,128)(2,1)S(1)}, bf16[2,64,128,128]{3,2,1,0:T(8,128)(2,1)}, u32[]{:S(2)}) copy-start(bf16[2,64,128,128]{3,2,1,0:T(8,128)(2,1)} %remap.1) | copy-start | bytes 12582916
  49.0 11.7 %collective-permute-start.13 = (bf16[16,64,128]{2,1,0:T(8,128)(2,1)S(1)}, bf16[16,64,128]{2,1,0:T(8,128)(2,1)S(1)}, u32[]{:S(2)}, u32[]{:S(2)}) collective-permute-start(bf16[16,64,128]{2,1,0:T(8,128)(2,1)S(1)} %get-tuple-element.63.refs_1_), channel_id=1, source_target_pairs={{0,1},{1,2},{2,3},{3,4},{4,5},{5,6},{6,7},{7,0},{8,9},{9,10},{10,1... | collective-permute-start | bytes 786440 | tf_op jit(solution)/shard_map/ppermute | solution.py:324
  49.1 11.7 %collective-permute-start.14 = (bf16[16,64,128]{2,1,0:T(8,128)(2,1)S(1)}, bf16[16,64,128]{2,1,0:T(8,128)(2,1)S(1)}, u32[]{:S(2)}, u32[]{:S(2)}) collective-permute-start(bf16[16,64,128]{2,1,0:T(8,128)(2,1)S(1)} %get-tuple-element.62.refs_0_), channel_id=1, source_target_pairs={{1,0},{2,1},{3,2},{4,3},{5,4},{6,5},{7,6},{0,7},{9,8},{10,9},{11,1... | collective-permute-start | bytes 786440 | tf_op jit(solution)/shard_map/ppermute | solution.py:325
  55.1 14.4 %collective-permute-start.6 = (bf16[16,64,128]{2,1,0:T(8,128)(2,1)S(1)}, bf16[16,64,128]{2,1,0:T(8,128)(2,1)S(1)}, u32[]{:S(2)}, u32[]{:S(2)}) collective-permute-start(bf16[16,64,128]{2,1,0:T(8,128)(2,1)S(1)} %get-tuple-element.51.refs_0_), channel_id=1, source_target_pairs={{0,8},{1,9},{2,10},{3,11},{4,12},{5,13},{6,14},{7,15},{8,0},{9,1},... | collective-permute-start | bytes 786440 | tf_op jit(solution)/shard_map/ppermute | solution.py:317
  55.2 8.6 %collective-permute-start.7 = (bf16[8,64,128]{2,1,0:T(8,128)(2,1)S(1)}, bf16[8,64,128]{2,1,0:T(8,128)(2,1)S(1)}, u32[]{:S(2)}, u32[]{:S(2)}) collective-permute-start(bf16[8,64,128]{2,1,0:T(8,128)(2,1)S(1)} %get-tuple-element.53), channel_id=1, source_target_pairs={{0,2},{1,3},{2,4},{3,5},{4,6},{5,7},{6,8},{7,9},{8,10},{9,11},{10,... | collective-permute-start | bytes 393224 | tf_op jit(solution)/shard_map/ppermute | solution.py:324
  55.3 10.9 %collective-permute-start.8 = (bf16[8,64,128]{2,1,0:T(8,128)(2,1)S(1)}, bf16[8,64,128]{2,1,0:T(8,128)(2,1)S(1)}, u32[]{:S(2)}, u32[]{:S(2)}) collective-permute-start(bf16[8,64,128]{2,1,0:T(8,128)(2,1)S(1)} %get-tuple-element.54), channel_id=1, source_target_pairs={{2,0},{3,1},{4,2},{5,3},{6,4},{7,5},{8,6},{9,7},{10,8},{11,9},{12,... | collective-permute-start | bytes 393224 | tf_op jit(solution)/shard_map/ppermute | solution.py:325
  72.9 1.8 %collective-permute-start.16 = (bf16[16,9,8,128]{3,2,1,0:T(8,128)(2,1)S(1)}, bf16[16,9,8,128]{3,2,1,0:T(8,128)(2,1)}, u32[]{:S(2)}, u32[]{:S(2)}) collective-permute-start(bf16[16,9,8,128]{3,2,1,0:T(8,128)(2,1)S(1)} %partials.1), channel_id=1, source_target_pairs={{0,16},{16,0},{1,17},{17,1},{2,18},{18,2},{3,19},{19,3},{4,20},{20... | collective-permute-start | bytes 884744 | tf_op jit(solution)/shard_map/ppermute | solution.py:317
  74.7 28.2 %all-to-all-start = ((bf16[16,9,8,128]{3,2,1,0:T(8,128)(2,1)}), bf16[16,9,8,128]{3,2,1,0:T(8,128)(2,1)S(1)}, u32[]{:S(2)}, u32[]{:S(2)}) async-start(bf16[16,9,8,128]{3,2,1,0:T(8,128)(2,1)} %collective-permute-done.16), calls=%async_computation | async-start | bytes 589824 | tf_op jit(solution)/shard_map/all_to_all | solution.py:470
  79.2 10.9 %collective-permute-start.9 = (bf16[16,64,128]{2,1,0:T(8,128)(2,1)S(1)}, bf16[16,64,128]{2,1,0:T(8,128)(2,1)S(1)}, u32[]{:S(2)}, u32[]{:S(2)}) collective-permute-start(bf16[16,64,128]{2,1,0:T(8,128)(2,1)S(1)} %get-tuple-element.56), channel_id=1, source_target_pairs={{0,1},{1,0},{2,3},{3,2},{4,5},{5,4},{6,7},{7,6},{8,9},{9,8},{10,11... | collective-permute-start | bytes 786440 | tf_op jit(solution)/shard_map/ppermute | solution.py:317
  81.2 19.1 %collective-permute-start.15 = (bf16[16,64,128]{2,1,0:T(8,128)(2,1)S(1)}, bf16[16,64,128]{2,1,0:T(8,128)(2,1)S(1)}, u32[]{:S(2)}, u32[]{:S(2)}) collective-permute-start(bf16[16,64,128]{2,1,0:T(8,128)(2,1)S(1)} %get-tuple-element.65), channel_id=1, source_target_pairs={{0,8},{1,9},{2,10},{3,11},{4,12},{5,13},{6,14},{7,15},{8,0},{9,1},... | collective-permute-start | bytes 786440 | tf_op jit(solution)/shard_map/ppermute | solution.py:317
